TPU v7x, 32 devices: a whole 2x2x4 slice. The times are simulated.
32 devices in a mesh: radar: 4 (over x, core), tile: 8 (over z, y).
Axes of the slice: x: 2, y: 2, z: 4, core: 2. Of those that a mesh axis runs over, the one named last changes fastest.
Arguments:
- background: float32 [3, 128, 32, 1024], P(None, 'tile', None, 'radar'), may hold values from -6 to 6
- interp: bfloat16 [2048, 128, 128], P(('radar', 'tile')), may hold values from -0.5 to 0.5
- beam: bfloat16 [2048, 3, 128], P(('radar', 'tile')), may hold values from -1 to 1
- observed: bfloat16 [2048, 128], P(('radar', 'tile')), may hold values from -6 to 6
- cell_block: int32 [2048], P(('radar', 'tile')), may hold values from 0 to 1023
- sweep_count: int32 [32, 32], P(('radar', 'tile')), may hold values from 0 to 2, as said below
Outputs:
- wind_field: float32 [3, 128, 32, 1024], P(None, 'tile', None, 'radar')
- strain: float32 [6, 128, 32, 1024], P(None, 'tile', None, 'radar')
- cost_trace: float32 [2], replicated
Inputs may be any that keep to these rules, and one draw needn't show every extreme that they name: `cell_block`: the cell block, within the owner's 16 x 32 x 256 cells of one component, read by a slot. `sweep_count`: every source device has an owning device to which all 2 of its slots are live.
All inputs are finite; a program needn't handle non-finite values.
Results may differ from a plain program's by a relative error of at most 0.0014.
Values may be sent and summed in bfloat16 or wider, within the bound.
No kernel may reach another device: no remote copies, remote signals or barrier semaphores. Data moves between devices by JAX's collectives and lax.ppermute only.
A program may use at most 64 MiB of HBM per device.

v0:
```python
import jax
import jax.numpy as jnp
from jax import lax
from jax.sharding import PartitionSpec as P

ITERS = 2


BACKGROUND_WEIGHT = 0.5
DIVERGENCE_WEIGHT = 1.0
STEP_LENGTH = 0.3
EPSILON = 1e-06


def with_halo(x, sides, width):
    for axis, dim in sides:
        size, length = (lax.axis_size(axis), x.shape[dim])
        up = [(i, (i + 1) % size) for i in range(size - 1)]
        down = [(j, i) for i, j in up]
        last = lax.slice_in_dim(x, length - width, length, axis=dim)
        first = lax.slice_in_dim(x, 0, width, axis=dim)
        before = lax.ppermute(last, axis, up)
        after = lax.ppermute(first, axis, down)
        x = jnp.concatenate([before, x, after], axis=dim)
    return x


def vertical_diff(values):
    padded = jnp.pad(values, ((0, 0), (1, 1), (0, 0)))
    return 0.5 * (padded[:, 2:, :] - padded[:, :-2, :])


def along_x(values):
    return 0.5 * (values[2:, :, 1:-1] - values[:-2, :, 1:-1])


def along_y(values):
    return 0.5 * (values[1:-1, :, 2:] - values[1:-1, :, :-2])


def along_z(values):
    return vertical_diff(values[1:-1, :, 1:-1])


def observe(cell_rows, weights, beam_rows, looked, alive_mask):
    projected = jnp.einsum("knc,ngc->nkg", cell_rows, weights, preferred_element_type=jnp.float32)
    beam_values = beam_rows.astype(jnp.float32)
    radial = jnp.sum(beam_values * projected, axis=1)
    misfit = alive_mask[:, None] * (radial - looked.astype(jnp.float32))
    adjoint = (beam_values * misfit[:, None, :]).astype(jnp.bfloat16)
    returned = jnp.einsum("nkg,ngc->knc", adjoint, weights, preferred_element_type=jnp.float32)
    return (0.5 * jnp.sum(misfit * misfit), returned)


def spread_cycle(wind_field, tile_count, radar_count):
    width_x = wind_field.shape[1]
    width_y = wind_field.shape[3]
    rim = with_halo(wind_field, (("radar", 3), ("tile", 1)), 2)
    cycle = along_x(rim[0]) + along_y(rim[1]) + along_z(rim[2])
    row_place = lax.axis_index("tile") * width_x - 1 + jnp.arange(width_x + 2, dtype=jnp.int32)
    col_place = lax.axis_index("radar") * width_y - 1 + jnp.arange(width_y + 2, dtype=jnp.int32)
    row_inside = (row_place >= 0) & (row_place < width_x * tile_count)
    col_inside = (col_place >= 0) & (col_place < width_y * radar_count)
    inside = row_inside[:, None, None] & col_inside[None, None, :]
    cycle = jnp.where(inside, cycle, 0.0)
    spread = cycle[1:-1, :, 1:-1]
    push = jnp.stack([-along_x(cycle), -along_y(cycle), -vertical_diff(spread)])
    return (spread, push)


def shards(background, interp, beam, observed, cell_block, sweep_count):
    radar_count = lax.axis_size("radar")
    tile_count = lax.axis_size("tile")
    devices = radar_count * tile_count
    width_x = background.shape[1]
    levels = background.shape[2]
    width_y = background.shape[3]
    slots = interp.shape[0] // devices
    gate_size = interp.shape[1]
    block_total = width_x * levels * width_y // gate_size
    total_cells = 3 * width_x * levels * width_y * devices
    total_gates = interp.shape[0] * devices * gate_size
    own_index = cell_block.reshape(devices, slots)
    own_alive = (
        jnp.arange(slots, dtype=jnp.int32)[None, :] < sweep_count.reshape(devices)[:, None]
    ).astype(jnp.int32)
    packed = jnp.stack([own_index, own_alive], 1)
    asked = lax.all_to_all(packed, ("radar", "tile"), split_axis=0, concat_axis=0, tiled=True)
    asked_index = asked[:, 0, :].reshape(-1)
    asked_alive = asked[:, 1, :].reshape(-1).astype(jnp.float32)
    got_weights, got_beam, got_looked = (
        lax.all_to_all(
            interp.reshape(devices, slots, gate_size, gate_size),
            ("radar", "tile"),
            split_axis=0,
            concat_axis=0,
            tiled=True,
        ),
        lax.all_to_all(
            beam.reshape(devices, slots, 3, gate_size),
            ("radar", "tile"),
            split_axis=0,
            concat_axis=0,
            tiled=True,
        ),
        lax.all_to_all(
            observed.reshape(devices, slots, gate_size),
            ("radar", "tile"),
            split_axis=0,
            concat_axis=0,
            tiled=True,
        ),
    )
    got_weights = got_weights.reshape(devices * slots, gate_size, gate_size)
    got_beam = got_beam.reshape(devices * slots, 3, gate_size)
    got_looked = got_looked.reshape(devices * slots, gate_size)
    wind_field = background
    trace = []
    for step_index in range(ITERS):
        flat = wind_field.reshape(3, block_total, gate_size)
        empty = jnp.zeros((3, block_total, gate_size), jnp.float32)
        chosen = flat[:, asked_index, :].astype(jnp.bfloat16)
        obs_cost, returned = observe(chosen, got_weights, got_beam, got_looked, asked_alive)
        obs_cost, obs_flat = (obs_cost, empty.at[:, asked_index, :].add(returned))
        obs_grad = obs_flat.reshape(wind_field.shape)
        spread, push = spread_cycle(wind_field, tile_count, radar_count)
        offset = wind_field - background
        gradient = obs_grad + BACKGROUND_WEIGHT * offset + DIVERGENCE_WEIGHT * push
        local_cost = (
            obs_cost
            + 0.5 * BACKGROUND_WEIGHT * jnp.sum(offset * offset)
            + 0.5 * DIVERGENCE_WEIGHT * jnp.sum(spread * spread)
        )
        cost_sum, square_sum = lax.psum(
            (local_cost, jnp.sum(gradient * gradient)), ("radar", "tile")
        )
        scale = jnp.sqrt(square_sum / total_cells + EPSILON)
        wind_field = wind_field - STEP_LENGTH * gradient / scale
        trace.append(cost_sum / total_gates)
    faces = with_halo(wind_field, (("radar", 3), ("tile", 1)), 1)
    east_wind, north_wind, upward_wind = (faces[0], faces[1], faces[2])
    strain = jnp.stack(
        [
            along_x(east_wind),
            along_y(north_wind),
            along_z(upward_wind),
            0.5 * (along_y(east_wind) + along_x(north_wind)),
            0.5 * (along_z(east_wind) + along_x(upward_wind)),
            0.5 * (along_z(north_wind) + along_y(upward_wind)),
        ]
    )
    return (wind_field, strain, jnp.stack(trace))


def solution(mesh):
    placed = (
        P(None, "tile", None, "radar"),
        P(("radar", "tile"), None, None),
        P(("radar", "tile"), None, None),
        P(("radar", "tile"), None),
        P(("radar", "tile")),
        P(("radar", "tile"), None),
    )
    return jax.shard_map(
        shards,
        mesh=mesh,
        in_specs=placed,
        out_specs=(P(None, "tile", None, "radar"), P(None, "tile", None, "radar"), P()),
        check_vma=False,
    )
```

profile of v0, /device:TPU:1, one launch (start us, length us, event | category | flops | bytes accessed | tf_op | source)
XLA Modules:
  0.0 292.6 jit_solution(12038039125268304084)
XLA Ops:
  2.8 7.1 %all-to-all-start = ((s32[32,2,2]{2,1,0:T(2,128)}), s32[32,2,2]{2,1,0:T(2,128)S(1)}, u32[]{:S(2)}, u32[]{:S(2)}) async-start(s32[32,2,2]{2,1,0:T(2,128)} %copy.109), calls=%async_computation | async-start | bytes 65536 | tf_op jit(solution)/shard_map/all_to_all | solution.py:88
  10.7 6.2 %all-to-all-done = s32[32,2,2]{2,1,0:T(2,128)S(1)} async-done(((s32[32,2,2]{2,1,0:T(2,128)}), s32[32,2,2]{2,1,0:T(2,128)S(1)}, u32[]{:S(2)}, u32[]{:S(2)}) %all-to-all-start) | async-done | bytes 544 | tf_op jit(solution)/shard_map/all_to_all | solution.py:88
  16.9 8.9 %all_to_all.20 = bf16[32,2,3,128]{3,1,2,0:T(2,128)(2,1)S(1)} all-to-all(bf16[32,2,3,128]{3,1,2,0:T(2,128)(2,1)S(1)} %copy.110), channel_id=1, replica_groups=mesh['radar'=4,'tile'=8] {'radar','tile'}, dimensions={0} | all-to-all | bytes 98304 | tf_op jit(solution)/shard_map/all_to_all | solution.py:99
  25.8 3.5 %all-to-all-start.2 = ((bf16[32,2,128,128]{3,2,1,0:T(8,128)(2,1)}), bf16[32,2,128,128]{3,2,1,0:T(8,128)(2,1)}, u32[]{:S(2)}, u32[]{:S(2)}) async-start(bf16[32,2,128,128]{3,2,1,0:T(8,128)(2,1)} %bitcast.87), calls=%async_computation.2 | async-start | bytes 4194304 | tf_op jit(solution)/shard_map/all_to_all | solution.py:92
  30.7 3.5 %collective-permute-start = (f32[3,16,32,2]{2,1,3,0:T(8,128)}, f32[3,16,32,2]{2,1,3,0:T(8,128)}, u32[]{:S(2)}, u32[]{:S(2)}) collective-permute-start(f32[3,16,32,2]{2,1,3,0:T(8,128)} %copy.136), channel_id=1, source_target_pairs={{0,8},{8,16},{16,24},{1,9},{9,17},{17,25},{2,10},{10,18},{18,26},{... | collective-permute-start | bytes 36872 | tf_op jit(solution)/shard_map/ppermute | solution.py:22
  35.2 1.9 collective-permute-start.1
  44.6 3.4 %collective-permute-start.2 = (f32[3,2,32,260]{3,2,1,0:T(8,128)S(1)}, f32[3,2,32,260]{3,2,1,0:T(8,128)S(1)}, u32[]{:S(2)}, u32[]{:S(2)}) collective-permute-start(f32[3,2,32,260]{3,2,1,0:T(8,128)S(1)} %get-tuple-element.19), channel_id=1, source_target_pairs={{0,1},{1,2},{2,3},{3,4},{4,5},{5,6},{6,7},{8,9},{9,10},{10,11},{11... | collective-permute-start | bytes 599048 | tf_op jit(solution)/shard_map/ppermute | solution.py:22
  49.4 10.3 %collective-permute-done.2 = f32[3,2,32,260]{3,2,1,0:T(8,128)S(1)} collective-permute-done((f32[3,2,32,260]{3,2,1,0:T(8,128)S(1)}, f32[3,2,32,260]{3,2,1,0:T(8,128)S(1)}, u32[]{:S(2)}, u32[]{:S(2)}) %collective-permute-start.2) | collective-permute-done | bytes 199712 | tf_op jit(solution)/shard_map/ppermute | solution.py:22
  59.8 1.5 collective-permute-done.3
  63.4 2.2 multiply_reduce_fusion.5
  66.5 12.5 %all-to-all-done.2 = bf16[32,2,128,128]{3,2,1,0:T(8,128)(2,1)} async-done(((bf16[32,2,128,128]{3,2,1,0:T(8,128)(2,1)}), bf16[32,2,128,128]{3,2,1,0:T(8,128)(2,1)}, u32[]{:S(2)}, u32[]{:S(2)}) %all-to-all-start.2) | async-done | bytes 2097184 | tf_op jit(solution)/shard_map/all_to_all | solution.py:92
  79.0 13.4 %all-to-all-start.3 = ((bf16[32,2,128]{2,1,0:T(2,128)(2,1)}), bf16[32,2,128]{2,1,0:T(2,128)(2,1)S(1)}, u32[]{:S(2)}, u32[]{:S(2)}) async-start(bf16[32,2,128]{2,1,0:T(2,128)(2,1)} %bitcast.7), calls=%async_computation.3 | async-start | bytes 32768 | tf_op jit(solution)/shard_map/all_to_all | solution.py:106
  92.4 2.8 fusion
  95.2 3.9 %all-to-all-done.3 = bf16[32,2,128]{2,1,0:T(2,128)(2,1)S(1)} async-done(((bf16[32,2,128]{2,1,0:T(2,128)(2,1)}), bf16[32,2,128]{2,1,0:T(2,128)(2,1)S(1)}, u32[]{:S(2)}, u32[]{:S(2)}) %all-to-all-start.3) | async-done | bytes 16416 | tf_op jit(solution)/shard_map/all_to_all | solution.py:106
  99.2 2.2 fusion.60
  101.4 1.6 broadcast.143.clone
  103.0 7.1 %scatter_fusion = f32[3,1024,128]{2,0,1:T(4,128)} fusion(f32[3,1024,128]{2,0,1:T(4,128)} %broadcast.143.clone, s32[64]{0:T(128)S(1)} %copy-done.6, f32[64,3,128]{2,1,0:T(4,128)S(1)} %fusion.60), kind=kCustom, calls=%fused_computation.2 | custom fusion | flops 24576 | bytes 295168 | tf_op jit(solution)/shard_map/scatter-add | solution.py:124
  110.1 2.8 copy.116
  113.0 1.7 reshape.212
  114.7 2.9 %multiply_reduce_fusion.3 = f32[]{:T(128)} fusion(f32[1,16,32,256]{3,2,1,0:T(8,128)} %fusion.15, f32[1,16,32,256]{3,2,1,0:T(8,128)} %get-tuple-element.39, f32[1,16,32,256]{3,2,1,0:T(8,128)} %get-tuple-element.38, f32[3,16,32,256]{3,2,1,0:T(8,128)S(1)} %reshape.212, f32[3,16,32,256]{3,2,1,0:T(8,128)S(1)} %copy-done), kind=kLoop, calls=%fused_computation.14 | loop fusion | flops 3145727 | bytes 4718596 | tf_op jit(solution)/shard_map/reduce_sum | solution.py:135
  118.3 38.0 %psum.28 = f32[]{:T(128)} all-reduce(f32[]{:T(128)} %multiply_reduce_fusion.3), channel_id=1, replica_groups=mesh['radar'=4,'tile'=8] {'radar','tile'}, use_global_device_ids=true, to_apply=%region_3.4 | all-reduce | flops 1 | bytes 8 | tf_op jit(solution)/shard_map/psum | solution.py:134
  157.0 3.2 %multiply_reduce_fusion.1 = (f32[]{:T(128)}, f32[]{:T(128)}, f32[3,16,32,256]{3,2,1,0:T(8,128)S(1)}) fusion(f32[3,16,32,256]{3,2,1,0:T(8,128)S(1)} %copy-done, f32[]{:T(128)S(6)} %sqrt.6, f32[1,16,32,256]{3,2,1,0:T(8,128)} %fusion.15, f32[1,16,32,256]{3,2,1,0:T(8,128)} %get-tuple-element.39, f32[1,16,32,256]{3,2,1,0:T(8,128)} %get-tuple-element.38, ...), kind=kLoop, calls=%fused_computation.10 | loop fusion | flops 5505022 | bytes 6291468 | tf_op jit(solution)/shard_map/reduce_sum | solution.py:131
  162.7 1.6 copy.121
  164.3 1.9 gather_fusion.1
  166.2 2.8 fusion.1
  170.5 5.1 %collective-permute-start.4 = (f32[3,16,32,2]{2,1,3,0:T(8,128)S(1)}, f32[3,16,32,2]{2,1,3,0:T(8,128)S(1)}, u32[]{:S(2)}, u32[]{:S(2)}) collective-permute-start(f32[3,16,32,2]{2,1,3,0:T(8,128)S(1)} %copy.125), channel_id=1, source_target_pairs={{0,8},{8,16},{16,24},{1,9},{9,17},{17,25},{2,10},{10,18},{18,26},{... | collective-permute-start | bytes 36872 | tf_op jit(solution)/shard_map/ppermute | solution.py:22
  175.6 2.1 copy.126
  177.7 1.9 collective-permute-start.5
  184.2 2.1 copy.128
  186.3 2.1 pad_maximum_fusion.5
  188.4 3.2 %collective-permute-start.6 = (f32[3,2,32,260]{3,2,1,0:T(8,128)}, f32[3,2,32,260]{3,2,1,0:T(8,128)}, u32[]{:S(2)}, u32[]{:S(2)}) collective-permute-start(f32[3,2,32,260]{3,2,1,0:T(8,128)} %get-tuple-element.17), channel_id=1, source_target_pairs={{0,1},{1,2},{2,3},{3,4},{4,5},{5,6},{6,7},{8,9},{9,10},{10,11},{11... | collective-permute-start | bytes 599048 | tf_op jit(solution)/shard_map/ppermute | solution.py:22
  193.0 2.2 fusion.58
  195.3 1.6 broadcast.143
  196.9 7.1 %scatter_fusion.1 = f32[3,1024,128]{2,0,1:T(4,128)} fusion(f32[3,1024,128]{2,0,1:T(4,128)} %broadcast.143, s32[64]{0:T(128)S(1)} %copy-done.7, f32[64,3,128]{2,1,0:T(4,128)S(1)} %fusion.58), kind=kCustom, calls=%fused_computation.3 | custom fusion | flops 24576 | bytes 295168 | tf_op jit(solution)/shard_map/scatter-add | solution.py:124
  204.0 2.8 copy.124
  206.8 2.7 reshape.214
  209.5 2.4 pad_maximum_fusion.1
  213.2 2.3 multiply_reduce_fusion.4
  216.2 2.1 fusion.19
  218.3 4.2 %multiply_reduce_fusion.2 = (f32[]{:T(128)}, f32[3,16,32,256]{3,2,1,0:T(8,128)}) fusion(f32[1,16,32,256]{3,2,1,0:T(8,128)} %fusion.19, f32[1,16,32,256]{3,2,1,0:T(8,128)} %get-tuple-element.43, f32[1,16,32,256]{3,2,1,0:T(8,128)} %get-tuple-element.42, f32[3,16,32,256]{3,2,1,0:T(8,128)} %reshape.214, f32[3,16,32,256]{3,2,1,0:T(8,128)S(1)} %get-tuple-element.10, ...), kind=kLoop, calls=%fused_computation.12 | loop fusion | flops 3145727 | bytes 7864324 | tf_op jit(solution)/shard_map/reduce_sum | solution.py:135
  222.5 40.7 %all-reduce.7 = (f32[]{:T(128)}, f32[]{:T(128)}, f32[]{:T(128)}) all-reduce(f32[]{:T(128)} %get-tuple-element.11, f32[]{:T(128)S(6)} %add.135, f32[]{:T(128)S(6)} %add.133), channel_id=1, replica_groups=mesh['radar'=4,'tile'=8] {'radar','tile'}, use_global_device_ids=true, to_apply=%region_7.8 | all-reduce | flops 3 | bytes 24 | tf_op jit(solution)/shard_map/psum | solution.py:134
  263.9 1.7 divide_subtract_fusion
  266.3 4.9 %collective-permute-start.8 = (f32[3,16,32,1]{2,1,3,0:T(8,128)S(1)}, f32[3,16,32,1]{2,1,3,0:T(8,128)S(1)}, u32[]{:S(2)}, u32[]{:S(2)}) collective-permute-start(f32[3,16,32,1]{2,1,3,0:T(8,128)S(1)} %copy.129), channel_id=1, source_target_pairs={{0,8},{8,16},{16,24},{1,9},{9,17},{17,25},{2,10},{10,18},{18,26},{... | collective-permute-start | bytes 18440 | tf_op jit(solution)/shard_map/ppermute | solution.py:22
  271.6 1.9 collective-permute-start.9
  275.2 1.5 collective-permute-done.9
  277.2 4.1 %collective-permute-start.10 = (f32[3,1,32,258]{3,2,1,0:T(8,128)S(1)}, f32[3,1,32,258]{3,2,1,0:T(8,128)S(1)}, u32[]{:S(2)}, u32[]{:S(2)}) collective-permute-start(f32[3,1,32,258]{3,2,1,0:T(8,128)S(1)} %get-tuple-element.15), channel_id=1, source_target_pairs={{0,1},{1,2},{2,3},{3,4},{4,5},{5,6},{6,7},{8,9},{9,10},{10,11},{11... | collective-permute-start | bytes 297224 | tf_op jit(solution)/shard_map/ppermute | solution.py:22
  283.3 4.3 %collective-permute-done.11 = f32[3,1,32,258]{3,2,1,0:T(8,128)S(1)} collective-permute-done((f32[3,1,32,258]{3,2,1,0:T(8,128)S(1)}, f32[3,1,32,258]{3,2,1,0:T(8,128)S(1)}, u32[]{:S(2)}, u32[]{:S(2)}) %collective-permute-start.11) | collective-permute-done | bytes 99104 | tf_op jit(solution)/shard_map/ppermute | solution.py:23
  290.9 1.7 copy-done.4
  (90 shorter events, 33.0 us)
Async XLA Ops:
  2.8 14.1 %all-to-all-start = ((s32[32,2,2]{2,1,0:T(2,128)}), s32[32,2,2]{2,1,0:T(2,128)S(1)}, u32[]{:S(2)}, u32[]{:S(2)}) async-start(s32[32,2,2]{2,1,0:T(2,128)} %copy.109), calls=%async_computation | async-start | bytes 65536 | tf_op jit(solution)/shard_map/all_to_all | solution.py:88
  25.8 3.5 %copy-start = (f32[3,16,32,256]{3,2,1,0:T(8,128)S(1)}, f32[3,16,32,256]{3,2,1,0:T(8,128)}, u32[]{:S(2)}) copy-start(f32[3,16,32,256]{3,2,1,0:T(8,128)} %param.6) | copy-start | bytes 4718596
  25.8 53.2 %all-to-all-start.2 = ((bf16[32,2,128,128]{3,2,1,0:T(8,128)(2,1)}), bf16[32,2,128,128]{3,2,1,0:T(8,128)(2,1)}, u32[]{:S(2)}, u32[]{:S(2)}) async-start(bf16[32,2,128,128]{3,2,1,0:T(8,128)(2,1)} %bitcast.87), calls=%async_computation.2 | async-start | bytes 4194304 | tf_op jit(solution)/shard_map/all_to_all | solution.py:92
  30.7 10.5 %collective-permute-start = (f32[3,16,32,2]{2,1,3,0:T(8,128)}, f32[3,16,32,2]{2,1,3,0:T(8,128)}, u32[]{:S(2)}, u32[]{:S(2)}) collective-permute-start(f32[3,16,32,2]{2,1,3,0:T(8,128)} %copy.136), channel_id=1, source_target_pairs={{0,8},{8,16},{16,24},{1,9},{9,17},{17,25},{2,10},{10,18},{18,26},{... | collective-permute-start | bytes 36872 | tf_op jit(solution)/shard_map/ppermute | solution.py:22
  35.2 8.0 %collective-permute-start.1 = (f32[3,16,32,2]{2,1,3,0:T(8,128)}, f32[3,16,32,2]{2,1,3,0:T(8,128)}, u32[]{:S(2)}, u32[]{:S(2)}) collective-permute-start(f32[3,16,32,2]{2,1,3,0:T(8,128)} %copy.137), channel_id=1, source_target_pairs={{8,0},{16,8},{24,16},{9,1},{17,9},{25,17},{10,2},{18,10},{26,18},{... | collective-permute-start | bytes 36872 | tf_op jit(solution)/shard_map/ppermute | solution.py:23
  38.4 0.6 copy-start.5
  44.6 15.1 %collective-permute-start.2 = (f32[3,2,32,260]{3,2,1,0:T(8,128)S(1)}, f32[3,2,32,260]{3,2,1,0:T(8,128)S(1)}, u32[]{:S(2)}, u32[]{:S(2)}) collective-permute-start(f32[3,2,32,260]{3,2,1,0:T(8,128)S(1)} %get-tuple-element.19), channel_id=1, source_target_pairs={{0,1},{1,2},{2,3},{3,4},{4,5},{5,6},{6,7},{8,9},{9,10},{10,11},{11... | collective-permute-start | bytes 599048 | tf_op jit(solution)/shard_map/ppermute | solution.py:22
  48.0 13.2 %collective-permute-start.3 = (f32[3,2,32,260]{3,2,1,0:T(8,128)S(1)}, f32[3,2,32,260]{3,2,1,0:T(8,128)S(1)}, u32[]{:S(2)}, u32[]{:S(2)}) collective-permute-start(f32[3,2,32,260]{3,2,1,0:T(8,128)S(1)} %get-tuple-element.20), channel_id=1, source_target_pairs={{1,0},{2,1},{3,2},{4,3},{5,4},{6,5},{7,6},{9,8},{10,9},{11,10},{12... | collective-permute-start | bytes 599048 | tf_op jit(solution)/shard_map/ppermute | solution.py:23
  65.6 33.5 %copy-start.8 = (f32[64]{0:T(128)S(1)}, f32[64]{0:T(128)}, u32[]{:S(2)}) copy-start(f32[64]{0:T(128)} %convert_element_type.74) | copy-start | bytes 772
  79.0 20.1 %all-to-all-start.3 = ((bf16[32,2,128]{2,1,0:T(2,128)(2,1)}), bf16[32,2,128]{2,1,0:T(2,128)(2,1)S(1)}, u32[]{:S(2)}, u32[]{:S(2)}) async-start(bf16[32,2,128]{2,1,0:T(2,128)(2,1)} %bitcast.7), calls=%async_computation.3 | async-start | bytes 32768 | tf_op jit(solution)/shard_map/all_to_all | solution.py:106
  99.2 3.8 %copy-start.6 = (s32[64]{0:T(128)S(1)}, s32[64]{0:T(128)}, u32[]{:S(2)}) copy-start(s32[64]{0:T(128)} %copy-done.5) | copy-start | bytes 772
  114.7 3.0 %copy-start.2 = (f32[3,16,32,256]{3,2,1,0:T(8,128)}, f32[3,16,32,256]{3,2,1,0:T(8,128)S(1)}, u32[]{:S(2)}) copy-start(f32[3,16,32,256]{3,2,1,0:T(8,128)S(1)} %reshape.212) | copy-start | bytes 4718596
  161.3 1.4 copy-start.3
  166.2 13.4 %copy-start.9 = (f32[64]{0:T(128)S(1)}, f32[64]{0:T(128)}, u32[]{:S(2)}) copy-start(f32[64]{0:T(128)} %convert_element_type.74) | copy-start | bytes 772
  170.5 12.5 %collective-permute-start.4 = (f32[3,16,32,2]{2,1,3,0:T(8,128)S(1)}, f32[3,16,32,2]{2,1,3,0:T(8,128)S(1)}, u32[]{:S(2)}, u32[]{:S(2)}) collective-permute-start(f32[3,16,32,2]{2,1,3,0:T(8,128)S(1)} %copy.125), channel_id=1, source_target_pairs={{0,8},{8,16},{16,24},{1,9},{9,17},{17,25},{2,10},{10,18},{18,26},{... | collective-permute-start | bytes 36872 | tf_op jit(solution)/shard_map/ppermute | solution.py:22
  177.7 6.5 %collective-permute-start.5 = (f32[3,16,32,2]{2,1,3,0:T(8,128)}, f32[3,16,32,2]{2,1,3,0:T(8,128)}, u32[]{:S(2)}, u32[]{:S(2)}) collective-permute-start(f32[3,16,32,2]{2,1,3,0:T(8,128)} %copy.126), channel_id=1, source_target_pairs={{8,0},{16,8},{24,16},{9,1},{17,9},{25,17},{10,2},{18,10},{26,18},{... | collective-permute-start | bytes 36872 | tf_op jit(solution)/shard_map/ppermute | solution.py:23
  188.4 21.1 %collective-permute-start.6 = (f32[3,2,32,260]{3,2,1,0:T(8,128)}, f32[3,2,32,260]{3,2,1,0:T(8,128)}, u32[]{:S(2)}, u32[]{:S(2)}) collective-permute-start(f32[3,2,32,260]{3,2,1,0:T(8,128)} %get-tuple-element.17), channel_id=1, source_target_pairs={{0,1},{1,2},{2,3},{3,4},{4,5},{5,6},{6,7},{8,9},{9,10},{10,11},{11... | collective-permute-start | bytes 599048 | tf_op jit(solution)/shard_map/ppermute | solution.py:22
  191.6 5.3 %copy-start.7 = (s32[64]{0:T(128)S(1)}, s32[64]{0:T(128)}, u32[]{:S(2)}) copy-start(s32[64]{0:T(128)} %copy-done.5) | copy-start | bytes 772
  191.6 17.9 %collective-permute-start.7 = (f32[3,2,32,260]{3,2,1,0:T(8,128)}, f32[3,2,32,260]{3,2,1,0:T(8,128)}, u32[]{:S(2)}, u32[]{:S(2)}) collective-permute-start(f32[3,2,32,260]{3,2,1,0:T(8,128)} %get-tuple-element.18), channel_id=1, source_target_pairs={{1,0},{2,1},{3,2},{4,3},{5,4},{6,5},{7,6},{9,8},{10,9},{11,10},{12... | collective-permute-start | bytes 599048 | tf_op jit(solution)/shard_map/ppermute | solution.py:23
  265.6 21.9 %copy-start.1 = (f32[3,16,32,256]{3,2,1,0:T(8,128)}, f32[3,16,32,256]{3,2,1,0:T(8,128)S(1)}, u32[]{:S(2)}) copy-start(f32[3,16,32,256]{3,2,1,0:T(8,128)S(1)} %divide_subtract_fusion) | copy-start | bytes 4718596
  266.3 8.5 %collective-permute-start.8 = (f32[3,16,32,1]{2,1,3,0:T(8,128)S(1)}, f32[3,16,32,1]{2,1,3,0:T(8,128)S(1)}, u32[]{:S(2)}, u32[]{:S(2)}) collective-permute-start(f32[3,16,32,1]{2,1,3,0:T(8,128)S(1)} %copy.129), channel_id=1, source_target_pairs={{0,8},{8,16},{16,24},{1,9},{9,17},{17,25},{2,10},{10,18},{18,26},{... | collective-permute-start | bytes 18440 | tf_op jit(solution)/shard_map/ppermute | solution.py:22
  271.6 5.1 %collective-permute-start.9 = (f32[3,16,32,1]{2,1,3,0:T(8,128)S(1)}, f32[3,16,32,1]{2,1,3,0:T(8,128)S(1)}, u32[]{:S(2)}, u32[]{:S(2)}) collective-permute-start(f32[3,16,32,1]{2,1,3,0:T(8,128)S(1)} %copy.130), channel_id=1, source_target_pairs={{8,0},{16,8},{24,16},{9,1},{17,9},{25,17},{10,2},{18,10},{26,18},{... | collective-permute-start | bytes 18440 | tf_op jit(solution)/shard_map/ppermute | solution.py:23
  277.2 6.0 %collective-permute-start.10 = (f32[3,1,32,258]{3,2,1,0:T(8,128)S(1)}, f32[3,1,32,258]{3,2,1,0:T(8,128)S(1)}, u32[]{:S(2)}, u32[]{:S(2)}) collective-permute-start(f32[3,1,32,258]{3,2,1,0:T(8,128)S(1)} %get-tuple-element.15), channel_id=1, source_target_pairs={{0,1},{1,2},{2,3},{3,4},{4,5},{5,6},{6,7},{8,9},{9,10},{10,11},{11... | collective-permute-start | bytes 297224 | tf_op jit(solution)/shard_map/ppermute | solution.py:22
  281.4 6.2 %collective-permute-start.11 = (f32[3,1,32,258]{3,2,1,0:T(8,128)S(1)}, f32[3,1,32,258]{3,2,1,0:T(8,128)S(1)}, u32[]{:S(2)}, u32[]{:S(2)}) collective-permute-start(f32[3,1,32,258]{3,2,1,0:T(8,128)S(1)} %get-tuple-element.16), channel_id=1, source_target_pairs={{1,0},{2,1},{3,2},{4,3},{5,4},{6,5},{7,6},{9,8},{10,9},{11,10},{12... | collective-permute-start | bytes 297224 | tf_op jit(solution)/shard_map/ppermute | solution.py:23
  290.9 1.7 copy-start.4
where the time goes:
time: 294 us; the launch traced here: 293 us
  blocking collectives  87.6 us (30%)
  starting transfers between devices  58 us (20%)
  other arithmetic  46.2 us (16%)
  waiting for transfers between devices  42 us (14%)
  local copies, waits for them, and re-layouts  41 us (14%)
  matrix products  10 us (3%)
  between operations  7.66 us (3%)
    psum x2, blocking collectives, shards(): lax.psum((local_cost, jnp.sum(gradient * gradient)), ('radar', 'tile'))  78.7 us
    ppermute x6, starting transfers between devices, with_halo(): before = lax.ppermute(last, axis, up)  24.3 us
    scatter-add x2, other arithmetic, shards(): obs_cost, obs_flat = (obs_cost, empty.at[:, asked_index, :].add(returned))  14.2 us
    all_to_all x1, starting transfers between devices, shards(): lax.all_to_all(observed.reshape(devices, slots, gate_size), ('radar', 'ti...  13.4 us
    all_to_all x1, waiting for transfers between devices, shards(): lax.all_to_all(interp.reshape(devices, slots, gate_size, gate_size), ('ra...  12.5 us
    ppermute x6, waiting for transfers between devices, with_halo(): before = lax.ppermute(last, axis, up)  11.3 us
    ppermute x6, starting transfers between devices, with_halo(): after = lax.ppermute(first, axis, down)  9.74 us
    all_to_all x1, blocking collectives, shards(): lax.all_to_all(beam.reshape(devices, slots, 3, gate_size), ('radar', 'til...  8.91 us
  transfers between devices with their start and end apart: 15, of which 9 were waited for; matrix products, arithmetic and copies ran while one was open for 13% of the time, Pallas kernels for 0%

commit v1 on v0

--- a/solution.py
+++ b/solution.py
@@ -50,6 +50,14 @@
     adjoint = (beam_values * misfit[:, None, :]).astype(jnp.bfloat16)
     returned = jnp.einsum("nkg,ngc->knc", adjoint, weights, preferred_element_type=jnp.float32)
     return (0.5 * jnp.sum(misfit * misfit), returned)
+
+
+def total_of(first, second, devices):
+    lane = lax.broadcasted_iota(jnp.int32, (devices, 128), 1)
+    row = jnp.where(lane == 0, first, jnp.where(lane == 1, second, 0.0))
+    rows = lax.all_to_all(row, ("radar", "tile"), split_axis=0, concat_axis=0, tiled=True)
+    sums = jnp.sum(rows, axis=0)
+    return sums[0], sums[1]
 
 
 def spread_cycle(wind_field, tile_count, radar_count):
@@ -131,9 +139,7 @@
             + 0.5 * BACKGROUND_WEIGHT * jnp.sum(offset * offset)
             + 0.5 * DIVERGENCE_WEIGHT * jnp.sum(spread * spread)
         )
-        cost_sum, square_sum = lax.psum(
-            (local_cost, jnp.sum(gradient * gradient)), ("radar", "tile")
-        )
+        cost_sum, square_sum = total_of(local_cost, jnp.sum(gradient * gradient), devices)
         scale = jnp.sqrt(square_sum / total_cells + EPSILON)
         wind_field = wind_field - STEP_LENGTH * gradient / scale
         trace.append(cost_sum / total_gates)

time: 294 us -> 230 us (0.78)
  blocking collectives: 87.6 us -> 28.8 us
  starting transfers between devices: 58 us -> 52.4 us
    psum x2 -> x0, blocking collectives: 78.7 us -> none  [shards(): lax.psum((local_cost, jnp.sum(gradient * gradient)), ('radar', 'tile'))]
    all_to_all x0 -> x2, blocking collectives: none -> 19.9 us  [total_of(): lax.all_to_all(row, ('radar', 'tile'), split_axis=0, concat_axis=0, tiled...]
    ppermute x6, starting transfers between devices: 24.3 us -> 17.7 us  [with_halo(): before = lax.ppermute(last, axis, up)]
    reduce_sum x2 -> x1, other arithmetic: 7.11 us -> 4.03 us  [shards(): jnp.sum(gradient * gradient)]
  transfers between devices with their start and end apart: 15 -> 15, of which waited for: 9 -> 10; matrix products, arithmetic and copies ran while one was open for 13% -> 17% of each run, Pallas kernels for 0% -> 0%
where the time goes in v1:
time: 230 us; the launch traced here: 229 us
  starting transfers between devices  52.4 us (23%)
  other arithmetic  47.4 us (21%)
  local copies, waits for them, and re-layouts  41.6 us (18%)
  waiting for transfers between devices  40.9 us (18%)
  blocking collectives  28.8 us (13%)
  matrix products  10 us (4%)
  between operations  7.74 us (3%)
    all_to_all x2, blocking collectives, total_of(): lax.all_to_all(row, ('radar', 'tile'), split_axis=0, concat_axis=0, tiled...  19.9 us
    ppermute x6, starting transfers between devices, with_halo(): before = lax.ppermute(last, axis, up)  17.7 us
    scatter-add x2, other arithmetic, shards(): obs_cost, obs_flat = (obs_cost, empty.at[:, asked_index, :].add(returned))  14.2 us
    all_to_all x1, starting transfers between devices, shards(): lax.all_to_all(observed.reshape(devices, slots, gate_size), ('radar', 'ti...  14.1 us
    all_to_all x1, waiting for transfers between devices, shards(): lax.all_to_all(interp.reshape(devices, slots, gate_size, gate_size), ('ra...  11.8 us
    ppermute x6, waiting for transfers between devices, with_halo(): before = lax.ppermute(last, axis, up)  10.8 us
    ppermute x6, starting transfers between devices, with_halo(): after = lax.ppermute(first, axis, down)  9.97 us
    all_to_all x1, blocking collectives, shards(): lax.all_to_all(beam.reshape(devices, slots, 3, gate_size), ('radar', 'til...  8.91 us
  transfers between devices with their start and end apart: 15, of which 10 were waited for; matrix products, arithmetic and copies ran while one was open for 17% of the time, Pallas kernels for 0%

profile of v1, /device:TPU:1, one launch (start us, length us, event | category | flops | bytes accessed | tf_op | source)
XLA Modules:
  0.0 228.7 jit_solution(14976996943867748629)
XLA Ops:
  2.8 7.1 %all-to-all-start = ((s32[32,2,2]{2,1,0:T(2,128)}), s32[32,2,2]{2,1,0:T(2,128)S(1)}, u32[]{:S(2)}, u32[]{:S(2)}) async-start(s32[32,2,2]{2,1,0:T(2,128)} %copy.134), calls=%async_computation | async-start | bytes 65536 | tf_op jit(solution)/shard_map/all_to_all | solution.py:96
  10.7 6.2 %all-to-all-done = s32[32,2,2]{2,1,0:T(2,128)S(1)} async-done(((s32[32,2,2]{2,1,0:T(2,128)}), s32[32,2,2]{2,1,0:T(2,128)S(1)}, u32[]{:S(2)}, u32[]{:S(2)}) %all-to-all-start) | async-done | bytes 544 | tf_op jit(solution)/shard_map/all_to_all | solution.py:96
  16.9 8.9 %all_to_all.32 = bf16[32,2,3,128]{3,1,2,0:T(2,128)(2,1)S(1)} all-to-all(bf16[32,2,3,128]{3,1,2,0:T(2,128)(2,1)S(1)} %copy.135), channel_id=1, replica_groups=mesh['radar'=4,'tile'=8] {'radar','tile'}, dimensions={0} | all-to-all | bytes 98304 | tf_op jit(solution)/shard_map/all_to_all | solution.py:107
  25.8 3.5 %all-to-all-start.2 = ((bf16[32,2,128,128]{3,2,1,0:T(8,128)(2,1)}), bf16[32,2,128,128]{3,2,1,0:T(8,128)(2,1)}, u32[]{:S(2)}, u32[]{:S(2)}) async-start(bf16[32,2,128,128]{3,2,1,0:T(8,128)(2,1)} %bitcast.89), calls=%async_computation.2 | async-start | bytes 4194304 | tf_op jit(solution)/shard_map/all_to_all | solution.py:100
  30.7 3.5 %collective-permute-start = (f32[3,16,32,2]{2,1,3,0:T(8,128)}, f32[3,16,32,2]{2,1,3,0:T(8,128)}, u32[]{:S(2)}, u32[]{:S(2)}) collective-permute-start(f32[3,16,32,2]{2,1,3,0:T(8,128)} %copy.163), channel_id=1, source_target_pairs={{0,8},{8,16},{16,24},{1,9},{9,17},{17,25},{2,10},{10,18},{18,26},{... | collective-permute-start | bytes 36872 | tf_op jit(solution)/shard_map/ppermute | solution.py:22
  35.2 1.9 collective-permute-start.1
  44.6 3.4 %collective-permute-start.2 = (f32[3,2,32,260]{3,2,1,0:T(8,128)S(1)}, f32[3,2,32,260]{3,2,1,0:T(8,128)S(1)}, u32[]{:S(2)}, u32[]{:S(2)}) collective-permute-start(f32[3,2,32,260]{3,2,1,0:T(8,128)S(1)} %get-tuple-element.15), channel_id=1, source_target_pairs={{0,1},{1,2},{2,3},{3,4},{4,5},{5,6},{6,7},{8,9},{9,10},{10,11},{11... | collective-permute-start | bytes 599048 | tf_op jit(solution)/shard_map/ppermute | solution.py:22
  49.4 10.3 %collective-permute-done.2 = f32[3,2,32,260]{3,2,1,0:T(8,128)S(1)} collective-permute-done((f32[3,2,32,260]{3,2,1,0:T(8,128)S(1)}, f32[3,2,32,260]{3,2,1,0:T(8,128)S(1)}, u32[]{:S(2)}, u32[]{:S(2)}) %collective-permute-start.2) | collective-permute-done | bytes 199712 | tf_op jit(solution)/shard_map/ppermute | solution.py:22
  59.8 1.5 collective-permute-done.3
  63.4 2.2 multiply_reduce_fusion.5
  67.2 11.8 %all-to-all-done.2 = bf16[32,2,128,128]{3,2,1,0:T(8,128)(2,1)} async-done(((bf16[32,2,128,128]{3,2,1,0:T(8,128)(2,1)}), bf16[32,2,128,128]{3,2,1,0:T(8,128)(2,1)}, u32[]{:S(2)}, u32[]{:S(2)}) %all-to-all-start.2) | async-done | bytes 2097184 | tf_op jit(solution)/shard_map/all_to_all | solution.py:100
  79.0 14.1 %all-to-all-start.3 = ((bf16[32,2,128]{2,1,0:T(2,128)(2,1)}), bf16[32,2,128]{2,1,0:T(2,128)(2,1)S(1)}, u32[]{:S(2)}, u32[]{:S(2)}) async-start(bf16[32,2,128]{2,1,0:T(2,128)(2,1)} %bitcast.7), calls=%async_computation.3 | async-start | bytes 32768 | tf_op jit(solution)/shard_map/all_to_all | solution.py:114
  93.1 2.8 %fusion = f32[64,128]{1,0:T(8,128)S(1)} fusion(bf16[64,128,128]{2,1,0:T(8,128)(2,1)} %bitcast.6, f32[64,3,128]{2,0,1:T(8,128)S(1)} %bitcast.85, bf16[64,3,128]{2,1,0:T(4,128)(2,1)S(1)} %gather_fusion), kind=kOutput, calls=%fused_computation.21 | convolution fusion | flops 6332416 | bytes 2277376 | tf_op jit(solution)/shard_map/knc,ngc->nkg/dot_general | solution.py:46
  95.9 3.9 %all-to-all-done.3 = bf16[32,2,128]{2,1,0:T(2,128)(2,1)S(1)} async-done(((bf16[32,2,128]{2,1,0:T(2,128)(2,1)}), bf16[32,2,128]{2,1,0:T(2,128)(2,1)S(1)}, u32[]{:S(2)}, u32[]{:S(2)}) %all-to-all-start.3) | async-done | bytes 16416 | tf_op jit(solution)/shard_map/all_to_all | solution.py:114
  99.9 2.2 fusion.60
  102.1 1.6 broadcast.233.clone
  103.7 7.1 %scatter_fusion = f32[3,1024,128]{2,0,1:T(4,128)} fusion(f32[3,1024,128]{2,0,1:T(4,128)} %broadcast.233.clone, s32[64]{0:T(128)S(1)} %copy-done.6, f32[64,3,128]{2,1,0:T(4,128)S(1)} %fusion.60), kind=kCustom, calls=%fused_computation.2 | custom fusion | flops 24576 | bytes 295168 | tf_op jit(solution)/shard_map/scatter-add | solution.py:132
  110.8 2.8 %copy.141 = f32[3,1024,128]{2,1,0:T(8,128)} copy(f32[3,1024,128]{2,0,1:T(4,128)} %scatter_fusion) | data formatting | bytes 3145728 | tf_op jit(solution)/shard_map/scatter-add | solution.py:132
  113.7 1.7 reshape.302
  116.9 2.5 %multiply_reduce_fusion.3 = (f32[]{:T(128)}, f32[]{:T(128)}) fusion(f32[3,16,32,256]{3,2,1,0:T(8,128)S(1)} %copy-done, f32[1,16,32,256]{3,2,1,0:T(8,128)} %fusion.15, f32[1,16,32,256]{3,2,1,0:T(8,128)} %get-tuple-element.39, f32[1,16,32,256]{3,2,1,0:T(8,128)} %get-tuple-element.38, f32[3,16,32,256]{3,2,1,0:T(8,128)S(1)} %reshape.302), kind=kLoop, calls=%fused_computation.14 | loop fusion | flops 3932158 | bytes 4718600 | tf_op jit(solution)/shard_map/reduce_sum | solution.py:139
  120.8 8.8 %all_to_all.33 = f32[32,1,128]{2,1,0:T(1,128)S(1)} all-to-all(f32[32,1,128]{2,1,0:T(1,128)S(1)} %broadcast_select_fusion.1), channel_id=1, replica_groups=mesh['radar'=4,'tile'=8] {'radar','tile'}, dimensions={0} | all-to-all | bytes 32768 | tf_op jit(solution)/shard_map/all_to_all | solution.py:58
  130.9 3.1 %multiply_reduce_fusion.1 = (f32[]{:T(128)}, f32[3,16,32,256]{3,2,1,0:T(8,128)S(1)}) fusion(f32[3,16,32,256]{3,2,1,0:T(8,128)S(1)} %copy-done, f32[]{:T(128)} %bitcast.18, f32[1,16,32,256]{3,2,1,0:T(8,128)} %fusion.15, f32[1,16,32,256]{3,2,1,0:T(8,128)} %get-tuple-element.39, f32[1,16,32,256]{3,2,1,0:T(8,128)} %get-tuple-element.38, ...), kind=kLoop, calls=%fused_computation.11 | loop fusion | flops 4718591 | bytes 6291464 | tf_op jit(solution)/shard_map/reduce_sum | solution.py:139
  136.5 1.6 copy.149
  138.2 1.9 gather_fusion.1
  140.0 2.8 %fusion.1 = f32[64,128]{1,0:T(8,128)S(1)} fusion(bf16[64,128,128]{2,1,0:T(8,128)(2,1)} %bitcast.6, f32[64,3,128]{2,0,1:T(8,128)S(1)} %bitcast.87, bf16[64,3,128]{2,1,0:T(4,128)(2,1)S(1)} %gather_fusion.1), kind=kOutput, calls=%fused_computation.22 | convolution fusion | flops 6332416 | bytes 2277376 | tf_op jit(solution)/shard_map/knc,ngc->nkg/dot_general | solution.py:46
  142.8 1.5 copy.153
  144.3 2.8 %collective-permute-start.4 = (f32[3,16,32,2]{2,1,3,0:T(8,128)S(1)}, f32[3,16,32,2]{2,1,3,0:T(8,128)S(1)}, u32[]{:S(2)}, u32[]{:S(2)}) collective-permute-start(f32[3,16,32,2]{2,1,3,0:T(8,128)S(1)} %copy.153), channel_id=1, source_target_pairs={{0,8},{8,16},{16,24},{1,9},{9,17},{17,25},{2,10},{10,18},{18,26},{... | collective-permute-start | bytes 36872 | tf_op jit(solution)/shard_map/ppermute | solution.py:22
  148.6 1.9 collective-permute-start.5
  154.1 2.1 copy.156
  156.2 2.1 pad_maximum_fusion.5
  158.3 2.9 %collective-permute-start.6 = (f32[3,2,32,260]{3,2,1,0:T(8,128)}, f32[3,2,32,260]{3,2,1,0:T(8,128)}, u32[]{:S(2)}, u32[]{:S(2)}) collective-permute-start(f32[3,2,32,260]{3,2,1,0:T(8,128)} %get-tuple-element.13), channel_id=1, source_target_pairs={{0,1},{1,2},{2,3},{3,4},{4,5},{5,6},{6,7},{8,9},{9,10},{10,11},{11... | collective-permute-start | bytes 599048 | tf_op jit(solution)/shard_map/ppermute | solution.py:22
  162.7 2.2 fusion.58
  164.9 1.6 broadcast.233
  166.5 7.1 %scatter_fusion.1 = f32[3,1024,128]{2,0,1:T(4,128)} fusion(f32[3,1024,128]{2,0,1:T(4,128)} %broadcast.233, s32[64]{0:T(128)S(1)} %copy-done.7, f32[64,3,128]{2,1,0:T(4,128)S(1)} %fusion.58), kind=kCustom, calls=%fused_computation.3 | custom fusion | flops 24576 | bytes 295168 | tf_op jit(solution)/shard_map/scatter-add | solution.py:132
  173.6 2.8 %copy.152 = f32[3,1024,128]{2,1,0:T(8,128)} copy(f32[3,1024,128]{2,0,1:T(4,128)} %scatter_fusion.1) | data formatting | bytes 3145728 | tf_op jit(solution)/shard_map/scatter-add | solution.py:132
  176.5 2.7 %reshape.304 = f32[3,16,32,256]{3,2,1,0:T(8,128)} reshape(f32[3,1024,128]{2,1,0:T(8,128)} %copy.152) | data formatting | bytes 3145728 | tf_op jit(solution)/shard_map/reshape | solution.py:133
  179.2 2.4 %pad_maximum_fusion.1 = f32[3,20,32,260]{3,2,1,0:T(8,128)S(1)} fusion(f32[3,2,32,260]{3,2,1,0:T(8,128)} %collective-permute-done.7, f32[3,16,32,2]{3,2,1,0:T(8,128)} %copy.156, f32[3,16,32,256]{3,2,1,0:T(8,128)S(1)} %get-tuple-element.6, f32[3,16,32,2]{3,2,1,0:T(8,128)} %copy.155, f32[3,2,32,260]{3,2,1,0:T(8,128)} %collective-permute-done.6), kind=kLoop, calls=%fused_computation.5 | loop fusion | flops 1996800 | bytes 3993600 | tf_op jit(solution)/shard_map/concatenate | solution.py:24
  182.8 2.3 %multiply_reduce_fusion.4 = (f32[]{:T(128)}, f32[16,32,256]{2,1,0:T(8,128)}, f32[1,16,32,256]{3,2,1,0:T(8,128)}, f32[1,16,32,256]{3,2,1,0:T(8,128)}) fusion(f32[18,32,258]{2,1,0:T(8,128)S(1)} %fusion.9), kind=kLoop, calls=%fused_computation.110 | loop fusion | flops 1048575 | bytes 4194308 | tf_op jit(solution)/shard_map/reduce_sum | solution.py:140
  187.1 4.0 %multiply_reduce_fusion = (f32[]{:T(128)}, f32[3,16,32,256]{3,2,1,0:T(8,128)}) fusion(f32[1,16,32,256]{3,2,1,0:T(8,128)S(1)} %fusion.19, f32[1,16,32,256]{3,2,1,0:T(8,128)} %get-tuple-element.35, f32[1,16,32,256]{3,2,1,0:T(8,128)} %get-tuple-element.34, f32[3,16,32,256]{3,2,1,0:T(8,128)} %reshape.304, f32[3,16,32,256]{3,2,1,0:T(8,128)S(1)} %get-tuple-element.6, ...), kind=kLoop, calls=%fused_computation.10 | loop fusion | flops 3145727 | bytes 7864324 | tf_op jit(solution)/shard_map/reduce_sum | solution.py:142
  191.7 11.0 %all_to_all.34 = f32[32,1,128]{2,1,0:T(1,128)S(1)} all-to-all(f32[32,1,128]{2,1,0:T(1,128)S(1)} %broadcast_select_fusion), channel_id=1, replica_groups=mesh['radar'=4,'tile'=8] {'radar','tile'}, dimensions={0} | all-to-all | bytes 32768 | tf_op jit(solution)/shard_map/all_to_all | solution.py:58
  204.0 1.7 divide_subtract_fusion
  206.4 2.8 %collective-permute-start.8 = (f32[3,16,32,1]{2,1,3,0:T(8,128)S(1)}, f32[3,16,32,1]{2,1,3,0:T(8,128)S(1)}, u32[]{:S(2)}, u32[]{:S(2)}) collective-permute-start(f32[3,16,32,1]{2,1,3,0:T(8,128)S(1)} %copy.158), channel_id=1, source_target_pairs={{0,8},{8,16},{16,24},{1,9},{9,17},{17,25},{2,10},{10,18},{18,26},{... | collective-permute-start | bytes 18440 | tf_op jit(solution)/shard_map/ppermute | solution.py:22
  209.6 1.9 collective-permute-start.9
  213.2 1.5 collective-permute-done.9
  215.2 2.2 collective-permute-start.10
  217.5 1.5 collective-permute-start.11
  219.6 4.0 %collective-permute-done.11 = f32[3,1,32,258]{3,2,1,0:T(8,128)S(1)} collective-permute-done((f32[3,1,32,258]{3,2,1,0:T(8,128)S(1)}, f32[3,1,32,258]{3,2,1,0:T(8,128)S(1)}, u32[]{:S(2)}, u32[]{:S(2)}) %collective-permute-start.11) | collective-permute-done | bytes 99104 | tf_op jit(solution)/shard_map/ppermute | solution.py:23
  227.1 1.7 copy-done.4
  (104 shorter events, 36.5 us)
Async XLA Ops:
  2.8 14.1 %all-to-all-start = ((s32[32,2,2]{2,1,0:T(2,128)}), s32[32,2,2]{2,1,0:T(2,128)S(1)}, u32[]{:S(2)}, u32[]{:S(2)}) async-start(s32[32,2,2]{2,1,0:T(2,128)} %copy.134), calls=%async_computation | async-start | bytes 65536 | tf_op jit(solution)/shard_map/all_to_all | solution.py:96
  25.8 3.5 %copy-start = (f32[3,16,32,256]{3,2,1,0:T(8,128)S(1)}, f32[3,16,32,256]{3,2,1,0:T(8,128)}, u32[]{:S(2)}) copy-start(f32[3,16,32,256]{3,2,1,0:T(8,128)} %param.6) | copy-start | bytes 4718596
  25.8 53.2 %all-to-all-start.2 = ((bf16[32,2,128,128]{3,2,1,0:T(8,128)(2,1)}), bf16[32,2,128,128]{3,2,1,0:T(8,128)(2,1)}, u32[]{:S(2)}, u32[]{:S(2)}) async-start(bf16[32,2,128,128]{3,2,1,0:T(8,128)(2,1)} %bitcast.89), calls=%async_computation.2 | async-start | bytes 4194304 | tf_op jit(solution)/shard_map/all_to_all | solution.py:100
  30.7 10.5 %collective-permute-start = (f32[3,16,32,2]{2,1,3,0:T(8,128)}, f32[3,16,32,2]{2,1,3,0:T(8,128)}, u32[]{:S(2)}, u32[]{:S(2)}) collective-permute-start(f32[3,16,32,2]{2,1,3,0:T(8,128)} %copy.163), channel_id=1, source_target_pairs={{0,8},{8,16},{16,24},{1,9},{9,17},{17,25},{2,10},{10,18},{18,26},{... | collective-permute-start | bytes 36872 | tf_op jit(solution)/shard_map/ppermute | solution.py:22
  35.2 8.0 %collective-permute-start.1 = (f32[3,16,32,2]{2,1,3,0:T(8,128)}, f32[3,16,32,2]{2,1,3,0:T(8,128)}, u32[]{:S(2)}, u32[]{:S(2)}) collective-permute-start(f32[3,16,32,2]{2,1,3,0:T(8,128)} %copy.164), channel_id=1, source_target_pairs={{8,0},{16,8},{24,16},{9,1},{17,9},{25,17},{10,2},{18,10},{26,18},{... | collective-permute-start | bytes 36872 | tf_op jit(solution)/shard_map/ppermute | solution.py:23
  38.9 0.5 copy-start.5
  44.6 15.1 %collective-permute-start.2 = (f32[3,2,32,260]{3,2,1,0:T(8,128)S(1)}, f32[3,2,32,260]{3,2,1,0:T(8,128)S(1)}, u32[]{:S(2)}, u32[]{:S(2)}) collective-permute-start(f32[3,2,32,260]{3,2,1,0:T(8,128)S(1)} %get-tuple-element.15), channel_id=1, source_target_pairs={{0,1},{1,2},{2,3},{3,4},{4,5},{5,6},{6,7},{8,9},{9,10},{10,11},{11... | collective-permute-start | bytes 599048 | tf_op jit(solution)/shard_map/ppermute | solution.py:22
  48.0 13.2 %collective-permute-start.3 = (f32[3,2,32,260]{3,2,1,0:T(8,128)S(1)}, f32[3,2,32,260]{3,2,1,0:T(8,128)S(1)}, u32[]{:S(2)}, u32[]{:S(2)}) collective-permute-start(f32[3,2,32,260]{3,2,1,0:T(8,128)S(1)} %get-tuple-element.16), channel_id=1, source_target_pairs={{1,0},{2,1},{3,2},{4,3},{5,4},{6,5},{7,6},{9,8},{10,9},{11,10},{12... | collective-permute-start | bytes 599048 | tf_op jit(solution)/shard_map/ppermute | solution.py:23
  65.6 34.1 %copy-start.8 = (f32[64]{0:T(128)S(1)}, f32[64]{0:T(128)}, u32[]{:S(2)}) copy-start(f32[64]{0:T(128)} %convert_element_type.74) | copy-start | bytes 772
  79.0 20.7 %all-to-all-start.3 = ((bf16[32,2,128]{2,1,0:T(2,128)(2,1)}), bf16[32,2,128]{2,1,0:T(2,128)(2,1)S(1)}, u32[]{:S(2)}, u32[]{:S(2)}) async-start(bf16[32,2,128]{2,1,0:T(2,128)(2,1)} %bitcast.7), calls=%async_computation.3 | async-start | bytes 32768 | tf_op jit(solution)/shard_map/all_to_all | solution.py:114
  99.9 3.8 %copy-start.6 = (s32[64]{0:T(128)S(1)}, s32[64]{0:T(128)}, u32[]{:S(2)}) copy-start(s32[64]{0:T(128)} %copy-done.5) | copy-start | bytes 772
  115.4 4.0 %copy-start.2 = (f32[3,16,32,256]{3,2,1,0:T(8,128)}, f32[3,16,32,256]{3,2,1,0:T(8,128)S(1)}, u32[]{:S(2)}) copy-start(f32[3,16,32,256]{3,2,1,0:T(8,128)S(1)} %reshape.302) | copy-start | bytes 4718596
  116.9 3.8 %copy-start.10 = (pred[128]{0:T(512)(128)(4,1)S(1)}, pred[128]{0:T(512)(128)(4,1)}, u32[]{:S(2)}) copy-start(pred[128]{0:T(512)(128)(4,1)} %iota_compare_fusion.1) | copy-start | bytes 388
  135.1 1.4 copy-start.3
  138.2 12.4 %copy-start.9 = (f32[64]{0:T(128)S(1)}, f32[64]{0:T(128)}, u32[]{:S(2)}) copy-start(f32[64]{0:T(128)} %convert_element_type.74) | copy-start | bytes 772
  144.3 8.3 %collective-permute-start.4 = (f32[3,16,32,2]{2,1,3,0:T(8,128)S(1)}, f32[3,16,32,2]{2,1,3,0:T(8,128)S(1)}, u32[]{:S(2)}, u32[]{:S(2)}) collective-permute-start(f32[3,16,32,2]{2,1,3,0:T(8,128)S(1)} %copy.153), channel_id=1, source_target_pairs={{0,8},{8,16},{16,24},{1,9},{9,17},{17,25},{2,10},{10,18},{18,26},{... | collective-permute-start | bytes 36872 | tf_op jit(solution)/shard_map/ppermute | solution.py:22
  148.6 5.5 %collective-permute-start.5 = (f32[3,16,32,2]{2,1,3,0:T(8,128)S(1)}, f32[3,16,32,2]{2,1,3,0:T(8,128)}, u32[]{:S(2)}, u32[]{:S(2)}) collective-permute-start(f32[3,16,32,2]{2,1,3,0:T(8,128)S(1)} %copy.154), channel_id=1, source_target_pairs={{8,0},{16,8},{24,16},{9,1},{17,9},{25,17},{10,2},{18,10},{26,18},{... | collective-permute-start | bytes 36872 | tf_op jit(solution)/shard_map/ppermute | solution.py:23
  158.3 20.8 %collective-permute-start.6 = (f32[3,2,32,260]{3,2,1,0:T(8,128)}, f32[3,2,32,260]{3,2,1,0:T(8,128)}, u32[]{:S(2)}, u32[]{:S(2)}) collective-permute-start(f32[3,2,32,260]{3,2,1,0:T(8,128)} %get-tuple-element.13), channel_id=1, source_target_pairs={{0,1},{1,2},{2,3},{3,4},{4,5},{5,6},{6,7},{8,9},{9,10},{10,11},{11... | collective-permute-start | bytes 599048 | tf_op jit(solution)/shard_map/ppermute | solution.py:22
  161.3 5.3 %copy-start.7 = (s32[64]{0:T(128)S(1)}, s32[64]{0:T(128)}, u32[]{:S(2)}) copy-start(s32[64]{0:T(128)} %copy-done.5) | copy-start | bytes 772
  161.3 17.9 %collective-permute-start.7 = (f32[3,2,32,260]{3,2,1,0:T(8,128)}, f32[3,2,32,260]{3,2,1,0:T(8,128)}, u32[]{:S(2)}, u32[]{:S(2)}) collective-permute-start(f32[3,2,32,260]{3,2,1,0:T(8,128)} %get-tuple-element.14), channel_id=1, source_target_pairs={{1,0},{2,1},{3,2},{4,3},{5,4},{6,5},{7,6},{9,8},{10,9},{11,10},{12... | collective-permute-start | bytes 599048 | tf_op jit(solution)/shard_map/ppermute | solution.py:23
  187.1 4.6 %copy-start.11 = (pred[128]{0:T(512)(128)(4,1)S(1)}, pred[128]{0:T(512)(128)(4,1)}, u32[]{:S(2)}) copy-start(pred[128]{0:T(512)(128)(4,1)} %iota_compare_fusion.1) | copy-start | bytes 388
  205.8 17.9 %copy-start.1 = (f32[3,16,32,256]{3,2,1,0:T(8,128)}, f32[3,16,32,256]{3,2,1,0:T(8,128)S(1)}, u32[]{:S(2)}) copy-start(f32[3,16,32,256]{3,2,1,0:T(8,128)S(1)} %divide_subtract_fusion) | copy-start | bytes 4718596
  206.4 6.4 %collective-permute-start.8 = (f32[3,16,32,1]{2,1,3,0:T(8,128)S(1)}, f32[3,16,32,1]{2,1,3,0:T(8,128)S(1)}, u32[]{:S(2)}, u32[]{:S(2)}) collective-permute-start(f32[3,16,32,1]{2,1,3,0:T(8,128)S(1)} %copy.158), channel_id=1, source_target_pairs={{0,8},{8,16},{16,24},{1,9},{9,17},{17,25},{2,10},{10,18},{18,26},{... | collective-permute-start | bytes 18440 | tf_op jit(solution)/shard_map/ppermute | solution.py:22
  209.6 5.1 %collective-permute-start.9 = (f32[3,16,32,1]{2,1,3,0:T(8,128)S(1)}, f32[3,16,32,1]{2,1,3,0:T(8,128)S(1)}, u32[]{:S(2)}, u32[]{:S(2)}) collective-permute-start(f32[3,16,32,1]{2,1,3,0:T(8,128)S(1)} %copy.159), channel_id=1, source_target_pairs={{8,0},{16,8},{24,16},{9,1},{17,9},{25,17},{10,2},{18,10},{26,18},{... | collective-permute-start | bytes 18440 | tf_op jit(solution)/shard_map/ppermute | solution.py:23
  215.2 4.4 %collective-permute-start.10 = (f32[3,1,32,258]{3,2,1,0:T(8,128)S(1)}, f32[3,1,32,258]{3,2,1,0:T(8,128)S(1)}, u32[]{:S(2)}, u32[]{:S(2)}) collective-permute-start(f32[3,1,32,258]{3,2,1,0:T(8,128)S(1)} %get-tuple-element.11), channel_id=1, source_target_pairs={{0,1},{1,2},{2,3},{3,4},{4,5},{5,6},{6,7},{8,9},{9,10},{10,11},{11... | collective-permute-start | bytes 297224 | tf_op jit(solution)/shard_map/ppermute | solution.py:22
  217.5 6.2 %collective-permute-start.11 = (f32[3,1,32,258]{3,2,1,0:T(8,128)S(1)}, f32[3,1,32,258]{3,2,1,0:T(8,128)S(1)}, u32[]{:S(2)}, u32[]{:S(2)}) collective-permute-start(f32[3,1,32,258]{3,2,1,0:T(8,128)S(1)} %get-tuple-element.12), channel_id=1, source_target_pairs={{1,0},{2,1},{3,2},{4,3},{5,4},{6,5},{7,6},{9,8},{10,9},{11,10},{12... | collective-permute-start | bytes 297224 | tf_op jit(solution)/shard_map/ppermute | solution.py:23
  227.0 1.7 copy-start.4

commit v2 on v0

v2 whole, which is shorter than its diff:
```python
import functools

import jax
import jax.numpy as jnp
from jax import lax
from jax.experimental import pallas as pl
from jax.experimental.pallas import tpu as pltpu
from jax.sharding import PartitionSpec as P

BACKGROUND_WEIGHT = 0.5
DIVERGENCE_WEIGHT = 1.0
STEP_LENGTH = 0.3
EPSILON = 1e-06

AXES = ("radar", "tile")
LANES = 128
F32 = jnp.float32
BF16 = jnp.bfloat16

COL_WY, COL_WX, COL_PART = 0, 1, 2
ROW_WX, ROW_PART, ROW_CORNER = 0, 1, 2


def exchange(x):
    return lax.all_to_all(x, AXES, split_axis=0, concat_axis=0, tiled=True)


def shifted(x, axis, step):
    size = lax.axis_size(axis)
    pairs = [(i, i + step) for i in range(size) if 0 <= i + step < size]
    return lax.ppermute(x, axis, pairs)


def iota(shape, dim):
    return lax.broadcasted_iota(jnp.int32, shape, dim)


def diff_levels(a, period):
    rows = a.shape[0]
    level = lax.rem(iota(a.shape, 0), jnp.int32(period))
    above = jnp.where(level == period - 1, 0.0, pltpu.roll(a, rows - 1, 0))
    below = jnp.where(level == 0, 0.0, pltpu.roll(a, 1, 0))
    return above - below


def diff_columns(a, left, right):
    width = a.shape[1]
    lane = iota(a.shape, 1)
    after = jnp.where(lane == width - 1, right, pltpu.roll(a, width - 1, 1))
    before = jnp.where(lane == 0, left, pltpu.roll(a, 1, 1))
    return after - before


def to_rows(columns):
    fill = jnp.zeros((LANES - columns.shape[0], columns.shape[1]), F32)
    return jnp.concatenate([columns, fill], axis=0).T


def from_fields(fields, rows):
    lane = iota((rows, LANES), 1)
    out = jnp.zeros((rows, LANES), F32)
    for f, field in enumerate(fields):
        out = jnp.where(lane == f, field, out)
    return out


def sum_rows(a):
    total = a[:, :LANES]
    for start in range(LANES, a.shape[1], LANES):
        total = total + a[:, start : start + LANES]
    return jnp.sum(total, axis=0, keepdims=True)


def own_place():
    return lax.axis_index("radar") * lax.axis_size("tile") + lax.axis_index("tile")


def block_at(index, runs):
    return lax.div(index, jnp.int32(runs)), lax.rem(index, jnp.int32(runs))


def read_block(ref, k, row, run):
    line = ref[k, pl.ds(row, 1), :]
    out = line[:, :LANES]
    for h in range(1, ref.shape[2] // LANES):
        out = jnp.where(run == h, line[:, h * LANES : (h + 1) * LANES], out)
    return out


def edge_columns(w_ref, left_out, right_out, scratch, levels):
    rows, width = w_ref.shape[1], w_ref.shape[2]
    cells = rows // levels
    for out, start, side in ((left_out, 0, 0), (right_out, width - LANES, 1)):
        lanes = slice(start, start + LANES)
        for x in range(cells):
            here = slice(x * levels, (x + 1) * levels)
            wx, wy, wz = (w_ref[k, here, lanes] for k in range(3))
            part = diff_levels(wz, levels)
            if x + 1 < cells:
                part = part + w_ref[0, (x + 1) * levels : (x + 2) * levels, lanes]
            if x > 0:
                part = part - w_ref[0, (x - 1) * levels : x * levels, lanes]
            if side == 0:
                part = 0.5 * (part[:, 0:1] + wy[:, 1:2])
                fields = (wy[:, 0:1], wx[:, 0:1], part)
            else:
                part = 0.5 * (part[:, LANES - 1 :] - wy[:, LANES - 2 : LANES - 1])
                fields = (wy[:, LANES - 1 :], wx[:, LANES - 1 :], part)
            scratch[here, :] = from_fields(fields, levels)
        out[...] = scratch[...].T[:8]


def edge_columns_kernel(levels, w_ref, left_out, right_out, scratch):
    edge_columns(w_ref, left_out, right_out, scratch, levels)


def edge_rows_kernel(levels, w_ref, left_ref, right_ref, up_out, down_out):
    rows, width = w_ref.shape[1], w_ref.shape[2]
    lane = iota((levels, width), 1)
    for out, first, tail in ((up_out, 0, False), (down_out, rows - levels, True)):
        here = slice(first, first + levels)
        base = first // LANES * LANES
        take = slice(first - base, first - base + levels)
        left = to_rows(left_ref[:, base : base + LANES])[take]
        right = to_rows(right_ref[:, base : base + LANES])[take]
        part = diff_levels(w_ref[2, here, :], levels)
        part = part + diff_columns(
            w_ref[1, here, :], left[:, COL_WY : COL_WY + 1], right[:, COL_WY : COL_WY + 1]
        )
        if tail:
            part = part - w_ref[0, first - levels : first, :]
        else:
            part = part + w_ref[0, levels : 2 * levels, :]
        out[ROW_WX] = w_ref[0, here, :]
        out[ROW_PART] = 0.5 * part
        out[ROW_CORNER] = jnp.where(
            lane == 0,
            left[:, COL_WX : COL_WX + 1],
            jnp.where(lane == width - 1, right[:, COL_WX : COL_WX + 1], 0.0),
        )


def cycle_kernel(levels, w_ref, left_ref, right_ref, above_ref, below_ref, push_out, spread_out, total_out, ring, left_rows, right_rows):
    rows, width = w_ref.shape[1], w_ref.shape[2]
    cells = rows // levels
    left_rows[...] = to_rows(left_ref[...])
    right_rows[...] = to_rows(right_ref[...])
    has_left = jnp.where(lax.axis_index("radar") > 0, 1.0, 0.0)
    has_right = jnp.where(lax.axis_index("radar") < lax.axis_size("radar") - 1, 1.0, 0.0)
    has_above = jnp.where(lax.axis_index("tile") > 0, 1.0, 0.0)
    has_below = jnp.where(lax.axis_index("tile") < lax.axis_size("tile") - 1, 1.0, 0.0)
    first, last = slice(0, levels), slice(rows - levels, rows)
    ring[0:levels, :] = has_above * (above_ref[ROW_PART] + 0.5 * w_ref[0, first, :])
    ring[rows + levels : rows + 2 * levels, :] = has_below * (below_ref[ROW_PART] - 0.5 * w_ref[0, last, :])
    total = jnp.zeros((levels, width), F32)
    for x in range(cells):
        here = slice(x * levels, (x + 1) * levels)
        after = w_ref[0, (x + 1) * levels : (x + 2) * levels, :] if x + 1 < cells else below_ref[ROW_WX]
        before = w_ref[0, (x - 1) * levels : x * levels, :] if x > 0 else above_ref[ROW_WX]
        spread = 0.5 * (
            (after - before)
            + diff_columns(
                w_ref[1, here, :],
                left_rows[here, COL_WY : COL_WY + 1],
                right_rows[here, COL_WY : COL_WY + 1],
            )
            + diff_levels(w_ref[2, here, :], levels)
        )
        ring[(x + 1) * levels : (x + 2) * levels, :] = spread
        spread_out[here, :] = spread
        total = total + spread * spread
    total_out[...] = jnp.broadcast_to(0.5 * DIVERGENCE_WEIGHT * sum_rows(total), total_out.shape)
    for x in range(cells):
        here = slice(x * levels, (x + 1) * levels)
        left = left_rows[here, COL_PART : COL_PART + 1] + 0.5 * w_ref[1, here, 0:1]
        right = right_rows[here, COL_PART : COL_PART + 1] - 0.5 * w_ref[1, here, width - 1 : width]
        if x == 0:
            left = left - 0.5 * above_ref[ROW_CORNER, :, 0:1]
            right = right - 0.5 * above_ref[ROW_CORNER, :, width - 1 : width]
        if x == cells - 1:
            left = left + 0.5 * below_ref[ROW_CORNER, :, 0:1]
            right = right + 0.5 * below_ref[ROW_CORNER, :, width - 1 : width]
        spread = ring[(x + 1) * levels : (x + 2) * levels, :]
        after = ring[(x + 2) * levels : (x + 3) * levels, :]
        before = ring[x * levels : (x + 1) * levels, :]
        push_out[0, here, :] = (-0.5 * DIVERGENCE_WEIGHT) * (after - before)
        push_out[1, here, :] = (-0.5 * DIVERGENCE_WEIGHT) * diff_columns(spread, has_left * left, has_right * right)
        push_out[2, here, :] = (-0.5 * DIVERGENCE_WEIGHT) * diff_levels(spread, levels)


def for_slots(count, body, step=4):
    def run(i, carry):
        for j in range(step):
            body(i * step + j)
        return carry

    lax.fori_loop(0, count // step, run, 0)


def pick_kernel(slots, asked_ref, w_ref, out_ref, rows_ref):
    me = own_place()
    runs = w_ref.shape[2] // LANES
    rows_ref[...] = jnp.zeros_like(rows_ref)

    def one(s):
        for p in range(slots):
            row, run = block_at(asked_ref[s, me * slots + p], runs)
            for k in range(3):
                rows_ref[s, 3 * p + k : 3 * p + k + 1, :] = read_block(w_ref, k, row, run)

    for_slots(out_ref.shape[0], one)
    out_ref[...] = rows_ref[...].astype(out_ref.dtype)


def project(cells_of, weights_ref, proj_ref, sources, slots, height):
    def one(s):
        weights = weights_ref[pl.ds(s * slots, slots)].reshape(slots * LANES, LANES)
        seen = lax.dot_general(cells_of(s), weights, (((1,), (1,)), ((), ())), preferred_element_type=F32)
        here = pl.ds(pl.multiple_of(s * height, height), height)
        for p in range(slots):
            proj_ref[p, here, :] = seen[:, p * LANES : (p + 1) * LANES]

    for_slots(sources, one)


def radial(proj_ref, sight_ref, p, sources, height):
    total = jnp.zeros((sources, LANES), F32)
    for k in range(3):
        total = total + sight_ref[3 * p + k] * proj_ref[p, pl.ds(3 * p + k, sources, stride=height), :]
    return total


def give_back(misfits, weights_ref, sight_ref, adj_ref, out_ref, sources, slots, height):
    adj_ref[...] = jnp.zeros_like(adj_ref)
    for p in range(slots):
        for k in range(3):
            adj_ref[p, pl.ds(3 * p + k, sources, stride=height), :] = sight_ref[3 * p + k] * misfits[p]

    def one(s):
        weights = weights_ref[pl.ds(s * slots, slots)].reshape(slots * LANES, LANES)
        here = pl.ds(pl.multiple_of(s * height, height), height)
        adjoint = jnp.concatenate([adj_ref[p, here, :] for p in range(slots)], axis=1).astype(BF16)
        out_ref[s] = lax.dot_general(adjoint, weights, (((1,), (0,)), ((), ())), preferred_element_type=F32)

    for_slots(sources, one)


def first_source_kernel(slots, cells_ref, weights_ref, sight_ref, returned_out, misfit_out, cost_out, proj_ref, adj_ref):
    sources, height = cells_ref.shape[0], cells_ref.shape[1]
    project(lambda s: cells_ref[s].astype(BF16), weights_ref, proj_ref, sources, slots, height)
    misfits = []
    cost = jnp.zeros((1, LANES), F32)
    for p in range(slots):
        misfit = radial(proj_ref, sight_ref, p, sources, height) - sight_ref[3 * slots + p]
        misfit_out[p] = misfit
        cost = cost + 0.5 * jnp.sum(misfit * misfit, axis=0, keepdims=True)
        misfits.append(misfit)
    cost_out[...] = jnp.broadcast_to(cost, cost_out.shape)
    give_back(misfits, weights_ref, sight_ref, adj_ref, returned_out, sources, slots, height)


def second_source_kernel(slots, total_cells, total_gates, got_ref, weights_ref, sight_ref, misfit_ref, returned_out, step_out, cost_out, done_out, proj_ref, adj_ref):
    sources, height = got_ref.shape[0], got_ref.shape[1]
    project(lambda s: got_ref[s].astype(BF16), weights_ref, proj_ref, sources, slots, height)
    squares = jnp.sum(got_ref[:, 3 * slots, :], axis=0, keepdims=True)
    squares = jnp.sum(squares, axis=1, keepdims=True)
    costs = jnp.sum(got_ref[:, 3 * slots + 1, :], axis=0, keepdims=True)
    costs = jnp.sum(costs, axis=1, keepdims=True)
    step = STEP_LENGTH / jnp.sqrt(squares / total_cells + EPSILON)
    step_out[...] = jnp.broadcast_to(step, step_out.shape)
    done_out[...] = jnp.broadcast_to(costs / total_gates, done_out.shape)
    misfits = []
    cost = jnp.zeros((1, LANES), F32)
    for p in range(slots):
        misfit = misfit_ref[p] - step * radial(proj_ref, sight_ref, p, sources, height)
        cost = cost + 0.5 * jnp.sum(misfit * misfit, axis=0, keepdims=True)
        misfits.append(misfit)
    cost_out[...] = jnp.broadcast_to(cost, cost_out.shape)
    give_back(misfits, weights_ref, sight_ref, adj_ref, returned_out, sources, slots, height)


def scatter_rows(slots, asked_ref, returned_ref, out_ref):
    me = own_place()
    runs = out_ref.shape[2] // LANES
    place = iota((8, LANES), 0)

    def one(s):
        for p in range(slots):
            row, run = block_at(asked_ref[s, me * slots + p], runs)
            within = lax.rem(row, jnp.int32(8))
            base = pl.multiple_of(row - within, 8)
            lanes = pl.ds(pl.multiple_of(run * LANES, LANES), LANES)
            for k in range(3):
                line = returned_ref[s, 3 * p + k : 3 * p + k + 1, :]
                out_ref[k, pl.ds(base, 8), lanes] += jnp.where(place == within, line, 0.0)

    for_slots(returned_ref.shape[0], one)


def square_sum(values_ref, levels):
    rows, width = values_ref.shape[1], values_ref.shape[2]
    total = jnp.zeros((levels, width), F32)
    for k in range(3):
        for x in range(rows // levels):
            piece = values_ref[k, x * levels : (x + 1) * levels, :]
            total = total + piece * piece
    return sum_rows(total)


def first_owner_kernel(slots, levels, asked_ref, returned_ref, push_ref, seen_cost_ref, spread_cost_ref, gradient_out, give_out, left_out, right_out, scratch):
    gradient_out[...] = push_ref[...]
    scatter_rows(slots, asked_ref, returned_ref, gradient_out)
    give_out[...] = jnp.zeros_like(give_out)
    me = own_place()
    runs = gradient_out.shape[2] // LANES

    def one(s):
        for p in range(slots):
            row, run = block_at(asked_ref[s, me * slots + p], runs)
            for k in range(3):
                give_out[s, 3 * p + k : 3 * p + k + 1, :] = read_block(gradient_out, k, row, run)

    for_slots(give_out.shape[0], one)
    sources = give_out.shape[0]
    give_out[:, 3 * slots, :] = jnp.broadcast_to(square_sum(gradient_out, levels), (sources, LANES))
    cost = seen_cost_ref[0:1, :] + spread_cost_ref[0:1, :]
    give_out[:, 3 * slots + 1, :] = jnp.broadcast_to(cost, (sources, LANES))
    edge_columns(gradient_out, left_out, right_out, scratch, levels)


def rest_kernel(levels, background_ref, gradient_ref, push_ref, bent_ref, spread_ref, bent_spread_ref, step_ref, rest_out, wind_out, cost_out):
    rows, width = gradient_ref.shape[1], gradient_ref.shape[2]
    step = step_ref[0:1, 0:1]
    offset_cost = jnp.zeros((levels, width), F32)
    spread_cost = jnp.zeros((levels, width), F32)
    for x in range(rows // levels):
        here = slice(x * levels, (x + 1) * levels)
        spread = spread_ref[here, :] - step * bent_spread_ref[here, :]
        spread_cost = spread_cost + spread * spread
        for k in range(3):
            offset = step * gradient_ref[k, here, :]
            offset_cost = offset_cost + offset * offset
            wind_out[k, here, :] = background_ref[k, here, :] - offset
            rest_out[k, here, :] = push_ref[k, here, :] - (BACKGROUND_WEIGHT * offset + step * bent_ref[k, here, :])
    cost = (0.5 * BACKGROUND_WEIGHT) * offset_cost + (0.5 * DIVERGENCE_WEIGHT) * spread_cost
    cost_out[...] = jnp.broadcast_to(sum_rows(cost), cost_out.shape)


def second_owner_kernel(slots, levels, asked_ref, returned_ref, rest_ref, wind_ref, seen_cost_ref, rest_cost_ref, gradient_out, give_out, up_out, down_out, left_out, right_out, scratch):
    gradient_out[...] = rest_ref[...]
    scatter_rows(slots, asked_ref, returned_ref, gradient_out)
    rows, width = gradient_out.shape[1], gradient_out.shape[2]
    half = LANES // 2
    squares = square_sum(gradient_out, levels)
    cost = seen_cost_ref[0:1, :] + rest_cost_ref[0:1, :]
    lane = iota((1, LANES), 1)
    squares = squares + pltpu.roll(squares, half, 1)
    cost = cost + pltpu.roll(cost, half, 1)
    give_out[...] = jnp.broadcast_to(jnp.where(lane < half, squares, cost), give_out.shape)
    for k in range(3):
        up_out[k] = wind_ref[k, 0:levels, :]
        up_out[3 + k] = gradient_out[k, 0:levels, :]
        down_out[k] = wind_ref[k, rows - levels : rows, :]
        down_out[3 + k] = gradient_out[k, rows - levels : rows, :]
    for out, column in ((left_out, 0), (right_out, width - 1)):
        for x in range(rows // levels):
            here = slice(x * levels, (x + 1) * levels)
            fields = [wind_ref[k, here, column : column + 1] for k in range(3)]
            fields += [gradient_out[k, here, column : column + 1] for k in range(3)]
            scratch[here, :] = from_fields(fields, levels)
        out[...] = scratch[...].T[:8]


def final_kernel(levels, total_cells, total_gates, sums_ref, first_cost_ref, wind_ref, gradient_ref, left_ref, right_ref, above_ref, below_ref, wind_out, strain_out, cost_out, left_rows, right_rows):
    rows, width = wind_ref.shape[1], wind_ref.shape[2]
    cells = rows // levels
    half = LANES // 2
    sums = jnp.sum(sums_ref[...], axis=0, keepdims=True)
    lane = iota((1, LANES), 1)
    squares = jnp.sum(jnp.where(lane < half, sums, 0.0), axis=1, keepdims=True)
    cost = jnp.sum(jnp.where(lane < half, 0.0, sums), axis=1, keepdims=True) / total_gates
    step = STEP_LENGTH / jnp.sqrt(squares / total_cells + EPSILON)
    out_lane = iota(cost_out.shape, 1)
    cost_out[...] = jnp.where(out_lane == 0, first_cost_ref[...], cost)
    left_rows[...] = to_rows(left_ref[...])
    right_rows[...] = to_rows(right_ref[...])
    for x in range(cells):
        here = slice(x * levels, (x + 1) * levels)
        for k in range(3):
            wind_out[k, here, :] = wind_ref[k, here, :] - step * gradient_ref[k, here, :]
    for x in range(cells):
        here = slice(x * levels, (x + 1) * levels)
        along = []
        for k in range(3):
            value = wind_out[k, here, :]
            if x + 1 < cells:
                after = wind_out[k, (x + 1) * levels : (x + 2) * levels, :]
            else:
                after = below_ref[k] - step * below_ref[3 + k]
            if x > 0:
                before = wind_out[k, (x - 1) * levels : x * levels, :]
            else:
                before = above_ref[k] - step * above_ref[3 + k]
            left = left_rows[here, k : k + 1] - step * left_rows[here, 3 + k : 4 + k]
            right = right_rows[here, k : k + 1] - step * right_rows[here, 3 + k : 4 + k]
            along.append((after - before, diff_columns(value, left, right), diff_levels(value, levels)))
        (xx, xy, xz), (yx, yy, yz), (zx, zy, zz) = along
        strain_out[0, here, :] = 0.5 * xx
        strain_out[1, here, :] = 0.5 * yy
        strain_out[2, here, :] = 0.5 * zz
        strain_out[3, here, :] = 0.25 * (xy + yx)
        strain_out[4, here, :] = 0.25 * (xz + zx)
        strain_out[5, here, :] = 0.25 * (yz + zy)


def shape(*dims, dtype=F32):
    return jax.ShapeDtypeStruct(dims, dtype)


VMEM = pl.BlockSpec(memory_space=pltpu.VMEM)
SMEM = pl.BlockSpec(memory_space=pltpu.SMEM)


def call(kernel, name, out_shape, args, scratch=(), scalars=0, flops=100000):
    return pl.pallas_call(
        kernel,
        name=name,
        out_shape=out_shape,
        in_specs=[SMEM] * scalars + [VMEM] * (len(args) - scalars),
        out_specs=jax.tree.map(lambda _: VMEM, out_shape),
        scratch_shapes=list(scratch),
        compiler_params=pltpu.CompilerParams(vmem_limit_bytes=32 * 1024 * 1024),
        cost_estimate=pl.CostEstimate(flops=flops, bytes_accessed=1 << 20, transcendentals=0),
    )(*args)


def shards(background, interp, beam, observed, cell_block, sweep_count):
    radar_count = lax.axis_size("radar")
    tile_count = lax.axis_size("tile")
    devices = radar_count * tile_count
    width_x, levels, width_y = background.shape[1:]
    slots = interp.shape[0] // devices
    gate_size = interp.shape[1]
    rows = width_x * levels
    height = -(-(3 * slots + 2) // 8) * 8
    total_cells = float(3 * rows * width_y * devices)
    total_gates = float(interp.shape[0] * devices * gate_size)
    field = background.reshape(3, rows, width_y)
    lanes = -(-devices * slots // LANES) * LANES
    line = jnp.pad(cell_block, (0, lanes - devices * slots))
    asked = exchange(jnp.broadcast_to(line[None, :], (devices, lanes)))

    live = (jnp.arange(slots, dtype=jnp.int32)[:, None, None] < sweep_count.reshape(1, devices, 1)).astype(F32)
    sight = beam.reshape(devices, slots, 3, gate_size).transpose(1, 2, 0, 3).astype(F32) * live[:, None]
    seen = observed.reshape(devices, slots, gate_size).transpose(1, 0, 2).astype(F32) * live
    sight = jnp.concatenate([sight.reshape(3 * slots, devices, gate_size), seen], axis=0)

    edges = (shape(8, rows), shape(8, rows))
    row_edges = (shape(3, levels, width_y), shape(3, levels, width_y))
    grid = shape(3, rows, width_y)
    line_out = shape(8, LANES)
    side = pltpu.VMEM((rows, LANES), F32)

    def cycle(values, sides):
        left = shifted(sides[1], "radar", 1)
        right = shifted(sides[0], "radar", -1)
        up, down = call(functools.partial(edge_rows_kernel, levels), "edge_rows", row_edges, (values, left, right))
        above = shifted(down, "tile", 1)
        below = shifted(up, "tile", -1)
        return call(
            functools.partial(cycle_kernel, levels),
            "cycle",
            (grid, shape(rows, width_y), line_out),
            (values, left, right, above, below),
            (pltpu.VMEM((rows + 2 * levels, width_y), F32), side, side),
        )

    sides = call(functools.partial(edge_columns_kernel, levels), "edge_columns", edges, (field,), (side,))
    push, spread, spread_cost = cycle(field, sides)

    cells = call(
        functools.partial(pick_kernel, slots),
        "pick",
        shape(devices, height, LANES, dtype=BF16),
        (asked, field),
        (pltpu.VMEM((devices, height, LANES), F32),),
        scalars=1,
    )
    cells = exchange(cells)
    products = (
        pltpu.VMEM((slots, devices * height, LANES), F32),
        pltpu.VMEM((slots, devices * height, LANES), F32),
    )
    returned, misfit, seen_cost = call(
        functools.partial(first_source_kernel, slots),
        "first_source",
        (shape(devices, height, LANES), shape(slots, devices, LANES), line_out),
        (cells, interp, sight),
        products,
    )
    returned = exchange(returned)
    gradient, give, left, right = call(
        functools.partial(first_owner_kernel, slots, levels),
        "first_owner",
        (grid, shape(devices, height, LANES)) + edges,
        (asked, returned, push, seen_cost, spread_cost),
        (side,),
        scalars=1,
    )
    got = exchange(give)
    bent, bent_spread, _ = cycle(gradient, (left, right))
    returned, step, seen_cost, first_cost = call(
        functools.partial(second_source_kernel, slots, total_cells, total_gates),
        "second_source",
        (shape(devices, height, LANES), line_out, line_out, line_out),
        (got, interp, sight, misfit),
        products,
    )
    returned = exchange(returned)
    rest, wind, rest_cost = call(
        functools.partial(rest_kernel, levels),
        "rest",
        (grid, grid, line_out),
        (field, gradient, push, bent, spread, bent_spread, step),
    )
    six_rows = (shape(6, levels, width_y), shape(6, levels, width_y))
    gradient, give, up, down, left, right = call(
        functools.partial(second_owner_kernel, slots, levels),
        "second_owner",
        (grid, shape(devices, LANES)) + six_rows + edges,
        (asked, returned, rest, wind, seen_cost, rest_cost),
        (side,),
        scalars=1,
    )
    sums = exchange(give)
    from_left = shifted(right, "radar", 1)
    from_right = shifted(left, "radar", -1)
    above = shifted(down, "tile", 1)
    below = shifted(up, "tile", -1)
    wind, strain, costs = call(
        functools.partial(final_kernel, levels, total_cells, total_gates),
        "final",
        (grid, shape(6, rows, width_y), line_out),
        (sums, first_cost, wind, gradient, from_left, from_right, above, below),
        (side, side),
    )
    return (
        wind.reshape(background.shape),
        strain.reshape(6, width_x, levels, width_y),
        costs[0, :2],
    )


def solution(mesh):
    placed = (
        P(None, "tile", None, "radar"),
        P(("radar", "tile"), None, None),
        P(("radar", "tile"), None, None),
        P(("radar", "tile"), None),
        P(("radar", "tile")),
        P(("radar", "tile"), None),
    )
    return jax.shard_map(
        shards,
        mesh=mesh,
        in_specs=placed,
        out_specs=(P(None, "tile", None, "radar"), P(None, "tile", None, "radar"), P()),
        check_vma=False,
    )
```

time: 294 us -> 145 us (0.49)
  blocking collectives: 87.6 us -> 13.2 us
  other arithmetic: 46.2 us -> 2.39 us
  Pallas kernels: 0 us -> 28.7 us
  local copies, waits for them, and re-layouts: 41 us -> 18.2 us
  waiting for transfers between devices: 42 us -> 28.6 us
  matrix products: 10 us -> 0 us
  between operations: 7.66 us -> 0.95 us
  starting transfers between devices: 58 us -> 52.1 us
    psum x2 -> x0, blocking collectives: 78.7 us -> none  [shards(): lax.psum((local_cost, jnp.sum(gradient * gradient)), ('radar', 'tile'))]
    pallas_call x0 -> x12, Pallas kernels: none -> 28.7 us  [call(): pl.pallas_call(kernel, name=name, out_shape=out_shape, in_specs=[SMEM] *...]
    reduce_sum x6 -> x0, other arithmetic: 15.5 us -> none  [the longest x2 7.11 us: shards(): jnp.sum(gradient * gradient)]
    scatter-add x2 -> x0, other arithmetic: 14.2 us -> none  [shards(): obs_cost, obs_flat = (obs_cost, empty.at[:, asked_index, :].add(returned))]
    unnamed x22 -> x46, local copies, waits for them, and re-layouts: 4.2 us -> 16.4 us
    all_to_all x3 -> x5, waiting for transfers between devices: 22.6 us -> 11.5 us  [exchange(): return lax.all_to_all(x, AXES, split_axis=0, concat_axis=0, tiled=True)]
    dot_general x4 -> x0, matrix products: 10 us -> none  [the longest x2 5.57 us: observe(): jnp.einsum('knc,ngc->nkg', cell_rows, weights, preferred_element_type=jnp...]
    reshape x7 -> x0, local copies, waits for them, and re-layouts: 8.86 us -> none  [the longest x2 4.4 us: shards(): obs_grad = obs_flat.reshape(wind_field.shape)]
  transfers between devices with their start and end apart: 15 -> 17, of which waited for: 9 -> 9; matrix products, arithmetic and copies ran while one was open for 13% -> 2% of each run, Pallas kernels for 0% -> 5%
where the time goes in v2:
time: 145 us; the launch traced here: 144 us
  starting transfers between devices  52.1 us (36%)
  Pallas kernels  28.7 us (20%)
  waiting for transfers between devices  28.6 us (20%)
  local copies, waits for them, and re-layouts  18.2 us (13%)
  blocking collectives  13.2 us (9%)
  other arithmetic  2.39 us (2%)
    ppermute x12, starting transfers between devices, shifted(): return lax.ppermute(x, axis, pairs)  30.7 us
    pallas_call x12, Pallas kernels, call(): pl.pallas_call(kernel, name=name, out_shape=out_shape, in_specs=[SMEM] *...  28.7 us
    all_to_all x5, starting transfers between devices, exchange(): return lax.all_to_all(x, AXES, split_axis=0, concat_axis=0, tiled=True)  21.5 us
    ppermute x12, waiting for transfers between devices, shifted(): return lax.ppermute(x, axis, pairs)  17.1 us
    unnamed x46, local copies, waits for them, and re-layouts  16.4 us
    all_to_all x1, blocking collectives, exchange(): return lax.all_to_all(x, AXES, split_axis=0, concat_axis=0, tiled=True)  13.2 us
    all_to_all x5, waiting for transfers between devices, exchange(): return lax.all_to_all(x, AXES, split_axis=0, concat_axis=0, tiled=True)  11.5 us
  transfers between devices with their start and end apart: 17, of which 9 were waited for; matrix products, arithmetic and copies ran while one was open for 2% of the time, Pallas kernels for 5%

profile of v2, /device:TPU:1, one launch (start us, length us, event | category | flops | bytes accessed | tf_op | source)
XLA Modules:
  0.0 144.2 jit_solution(10272917971632731305)
XLA Ops:
  1.9 7.1 %all-to-all-start = ((s32[32,1,128]{2,1,0:T(1,128)}), s32[32,1,128]{2,1,0:T(1,128)S(1)}, u32[]{:S(2)}, u32[]{:S(2)}) async-start(s32[32,1,128]{2,1,0:T(1,128)} %broadcast_in_dim.2), calls=%async_computation | async-start | bytes 32768 | tf_op jit(solution)/shard_map/all_to_all | solution.py:25
  9.7 0.8 convert.9
  10.6 0.7 convert.8
  11.3 4.3 %all-to-all-done = s32[32,1,128]{2,1,0:T(1,128)S(1)} async-done(((s32[32,1,128]{2,1,0:T(1,128)}), s32[32,1,128]{2,1,0:T(1,128)S(1)}, u32[]{:S(2)}, u32[]{:S(2)}) %all-to-all-start) | async-done | bytes 16416 | tf_op jit(solution)/shard_map/all_to_all | solution.py:25
  15.7 1.4 copy-done
  17.1 1.9 %pick.1 = bf16[32,8,128]{2,1,0:T(8,128)(2,1)} custom-call(s32[32,128]{1,0:T(8,128)S(1)} %bitcast.29, f32[3,512,256]{2,1,0:T(8,128)S(1)} %bitcast.24), custom_call_target="tpu_custom_call" | custom-call | flops 100000 | bytes 1048576 | tf_op jit(solution)/shard_map/pick/pallas_call | solution.py:425
  19.0 3.0 %all-to-all-start.1 = ((bf16[32,8,128]{2,1,0:T(8,128)(2,1)}), bf16[32,8,128]{2,1,0:T(8,128)(2,1)S(1)}, u32[]{:S(2)}, u32[]{:S(2)}) async-start(bf16[32,8,128]{2,1,0:T(8,128)(2,1)} %pick.1), calls=%async_computation.1 | async-start | bytes 131072 | tf_op jit(solution)/shard_map/all_to_all | solution.py:25
  22.0 7.2 %all-to-all-done.1.cells_ref = bf16[32,8,128]{2,1,0:T(8,128)(2,1)S(1)} async-done(((bf16[32,8,128]{2,1,0:T(8,128)(2,1)}), bf16[32,8,128]{2,1,0:T(8,128)(2,1)S(1)}, u32[]{:S(2)}, u32[]{:S(2)}) %all-to-all-start.1) | async-done | bytes 65568 | tf_op jit(solution)/shard_map/all_to_all | solution.py:25
  29.2 1.6 %copy-done.2 = bf16[64,128,128]{2,1,0:T(8,128)(2,1)S(1)} copy-done((bf16[64,128,128]{2,1,0:T(8,128)(2,1)S(1)}, bf16[64,128,128]{2,1,0:T(8,128)(2,1)}, u32[]{:S(2)}) %copy-start.2) | copy-done | bytes 2097176
  30.8 3.4 %first_source.1 = (f32[32,8,128]{2,1,0:T(8,128)}, f32[2,32,128]{2,1,0:T(8,128)S(1)}, f32[8,128]{1,0:T(8,128)S(1)}) custom-call(bf16[32,8,128]{2,1,0:T(8,128)(2,1)S(1)} %all-to-all-done.1.cells_ref, bf16[64,128,128]{2,1,0:T(8,128)(2,1)S(1)} %copy-done.2, f32[8,32,128]{2,1,0:T(8,128)S(1)} %pad_maximum_fusion.sight_ref), custom_call_target="tpu_custom_call" | custom-call | flops 100000 | bytes 1048576 | tf_op jit(solution)/shard_map/first_source/pallas_call | solution.py:425
  34.2 2.6 %all-to-all-start.2 = ((f32[32,8,128]{2,1,0:T(8,128)}), f32[32,8,128]{2,1,0:T(8,128)S(1)}, u32[]{:S(2)}, u32[]{:S(2)}) async-start(f32[32,8,128]{2,1,0:T(8,128)} %get-tuple-element.37), calls=%async_computation.2 | async-start | bytes 262144 | tf_op jit(solution)/shard_map/all_to_all | solution.py:25
  36.8 2.4 %edge_columns.1 = (f32[8,512]{1,0:T(8,128)S(1)}, f32[8,512]{1,0:T(8,128)S(1)}) custom-call(f32[3,512,256]{2,1,0:T(8,128)S(1)} %bitcast.25), custom_call_target="tpu_custom_call" | custom-call | flops 100000 | bytes 1048576 | tf_op jit(solution)/shard_map/edge_columns/pallas_call | solution.py:425
  39.1 3.5 %collective-permute-start = (f32[8,512]{1,0:T(8,128)S(1)}, f32[8,512]{1,0:T(8,128)S(1)}, u32[]{:S(2)}, u32[]{:S(2)}) collective-permute-start(f32[8,512]{1,0:T(8,128)S(1)} %get-tuple-element.38), channel_id=1, source_target_pairs={{0,8},{8,16},{16,24},{1,9},{9,17},{17,25},{2,10},{10,18},{18,26},{... | collective-permute-start | bytes 49160 | tf_op jit(solution)/shard_map/ppermute | solution.py:31
  42.7 1.9 %collective-permute-start.1 = (f32[8,512]{1,0:T(8,128)S(1)}, f32[8,512]{1,0:T(8,128)S(1)}, u32[]{:S(2)}, u32[]{:S(2)}) collective-permute-start(f32[8,512]{1,0:T(8,128)S(1)} %get-tuple-element.39), channel_id=1, source_target_pairs={{8,0},{16,8},{24,16},{9,1},{17,9},{25,17},{10,2},{18,10},{26,18},{... | collective-permute-start | bytes 49160 | tf_op jit(solution)/shard_map/ppermute | solution.py:31
  44.6 3.1 %collective-permute-done.1.right_ref = f32[8,512]{1,0:T(8,128)S(1)} collective-permute-done((f32[8,512]{1,0:T(8,128)S(1)}, f32[8,512]{1,0:T(8,128)S(1)}, u32[]{:S(2)}, u32[]{:S(2)}) %collective-permute-start.1) | collective-permute-done | bytes 16416 | tf_op jit(solution)/shard_map/ppermute | solution.py:31
  48.0 3.1 %collective-permute-start.2 = (f32[3,32,256]{2,1,0:T(8,128)S(1)}, f32[3,32,256]{2,1,0:T(8,128)S(1)}, u32[]{:S(2)}, u32[]{:S(2)}) collective-permute-start(f32[3,32,256]{2,1,0:T(8,128)S(1)} %get-tuple-element.40), channel_id=1, source_target_pairs={{0,1},{1,2},{2,3},{3,4},{4,5},{5,6},{6,7},{8,9},{9,10},{10,11},{11... | collective-permute-start | bytes 294920 | tf_op jit(solution)/shard_map/ppermute | solution.py:31
  51.1 1.3 collective-permute-start.3
  52.7 3.7 %collective-permute-done.3.below_ref = f32[3,32,256]{2,1,0:T(8,128)S(1)} collective-permute-done((f32[3,32,256]{2,1,0:T(8,128)S(1)}, f32[3,32,256]{2,1,0:T(8,128)S(1)}, u32[]{:S(2)}, u32[]{:S(2)}) %collective-permute-start.3) | collective-permute-done | bytes 98336 | tf_op jit(solution)/shard_map/ppermute | solution.py:31
  56.5 2.2 %cycle.2 = (f32[3,512,256]{2,1,0:T(8,128)S(1)}, f32[512,256]{1,0:T(8,128)S(1)}, f32[8,128]{1,0:T(8,128)S(1)}) custom-call(f32[3,512,256]{2,1,0:T(8,128)S(1)} %bitcast.27, f32[8,512]{1,0:T(8,128)S(1)} %collective-permute-done.left_ref, f32[8,512]{1,0:T(8,128)S(1)} %collective-permute-done.1.right_ref, f32[3,32,256]{2,1,0:T(8,128)S(1)} %collective-permute-done.2.above_ref, ...), custom_call_target="tpu_custom_call" | custom-call | flops 100000 | bytes 1048576 | tf_op jit(solution)/shard_map/cycle/pallas_call | solution.py:425
  58.7 1.1 copy-done.7
  59.8 0.8 copy-done.12
  60.6 1.4 copy-done.8
  62.0 4.2 %first_owner.1 = (f32[3,512,256]{2,1,0:T(8,128)S(1)}, f32[32,8,128]{2,1,0:T(8,128)S(1)}, f32[8,512]{1,0:T(8,128)S(1)}, f32[8,512]{1,0:T(8,128)S(1)}) custom-call(s32[32,128]{1,0:T(8,128)S(1)} %bitcast.30, f32[32,8,128]{2,1,0:T(8,128)S(1)} %all-to-all-done.2.returned_ref, f32[3,512,256]{2,1,0:T(8,128)S(1)} %copy-done.8, ...), custom_call_target="tpu_custom_call" | custom-call | flops 100000 | bytes 1048576 | tf_op jit(solution)/shard_map/first_owner/pallas_call | solution.py:425
  66.2 13.2 %all_to_all.39.got_ref = f32[32,8,128]{2,1,0:T(8,128)S(1)} all-to-all(f32[32,8,128]{2,1,0:T(8,128)S(1)} %get-tuple-element.45), channel_id=1, replica_groups=mesh['radar'=4,'tile'=8] {'radar','tile'}, dimensions={0} | all-to-all | bytes 262144 | tf_op jit(solution)/shard_map/all_to_all | solution.py:25
  79.4 1.6 %copy-done.3 = bf16[64,128,128]{2,1,0:T(8,128)(2,1)S(1)} copy-done((bf16[64,128,128]{2,1,0:T(8,128)(2,1)S(1)}, bf16[64,128,128]{2,1,0:T(8,128)(2,1)}, u32[]{:S(2)}) %copy-start.3) | copy-done | bytes 2097176
  81.0 3.5 %second_source.1 = (f32[32,8,128]{2,1,0:T(8,128)}, f32[8,128]{1,0:T(8,128)S(1)}, f32[8,128]{1,0:T(8,128)S(1)}, f32[8,128]{1,0:T(8,128)S(1)}) custom-call(f32[32,8,128]{2,1,0:T(8,128)S(1)} %all_to_all.39.got_ref, bf16[64,128,128]{2,1,0:T(8,128)(2,1)S(1)} %copy-done.3, f32[8,32,128]{2,1,0:T(8,128)S(1)} %pad_maximum_fusion.sight_ref, ...), custom_call_target="tpu_custom_call" | custom-call | flops 100000 | bytes 1048576 | tf_op jit(solution)/shard_map/second_source/pallas_call | solution.py:425
  84.5 2.6 %all-to-all-start.4 = ((f32[32,8,128]{2,1,0:T(8,128)}), f32[32,8,128]{2,1,0:T(8,128)S(1)}, u32[]{:S(2)}, u32[]{:S(2)}) async-start(f32[32,8,128]{2,1,0:T(8,128)} %get-tuple-element.47), calls=%async_computation.4 | async-start | bytes 262144 | tf_op jit(solution)/shard_map/all_to_all | solution.py:25
  87.0 3.5 %collective-permute-start.4 = (f32[8,512]{1,0:T(8,128)S(1)}, f32[8,512]{1,0:T(8,128)S(1)}, u32[]{:S(2)}, u32[]{:S(2)}) collective-permute-start(f32[8,512]{1,0:T(8,128)S(1)} %get-tuple-element.49), channel_id=1, source_target_pairs={{0,8},{8,16},{16,24},{1,9},{9,17},{17,25},{2,10},{10,18},{18,26},{... | collective-permute-start | bytes 49160 | tf_op jit(solution)/shard_map/ppermute | solution.py:31
  90.6 1.9 %collective-permute-start.5 = (f32[8,512]{1,0:T(8,128)S(1)}, f32[8,512]{1,0:T(8,128)S(1)}, u32[]{:S(2)}, u32[]{:S(2)}) collective-permute-start(f32[8,512]{1,0:T(8,128)S(1)} %get-tuple-element.50), channel_id=1, source_target_pairs={{8,0},{16,8},{24,16},{9,1},{17,9},{25,17},{10,2},{18,10},{26,18},{... | collective-permute-start | bytes 49160 | tf_op jit(solution)/shard_map/ppermute | solution.py:31
  92.5 3.1 %collective-permute-done.5.right_ref = f32[8,512]{1,0:T(8,128)S(1)} collective-permute-done((f32[8,512]{1,0:T(8,128)S(1)}, f32[8,512]{1,0:T(8,128)S(1)}, u32[]{:S(2)}, u32[]{:S(2)}) %collective-permute-start.5) | collective-permute-done | bytes 16416 | tf_op jit(solution)/shard_map/ppermute | solution.py:31
  95.9 3.3 %collective-permute-start.6 = (f32[3,32,256]{2,1,0:T(8,128)S(1)}, f32[3,32,256]{2,1,0:T(8,128)S(1)}, u32[]{:S(2)}, u32[]{:S(2)}) collective-permute-start(f32[3,32,256]{2,1,0:T(8,128)S(1)} %get-tuple-element.51), channel_id=1, source_target_pairs={{0,1},{1,2},{2,3},{3,4},{4,5},{5,6},{6,7},{8,9},{9,10},{10,11},{11... | collective-permute-start | bytes 294920 | tf_op jit(solution)/shard_map/ppermute | solution.py:31
  99.2 1.3 collective-permute-start.7
  100.8 3.7 %collective-permute-done.7.below_ref = f32[3,32,256]{2,1,0:T(8,128)S(1)} collective-permute-done((f32[3,32,256]{2,1,0:T(8,128)S(1)}, f32[3,32,256]{2,1,0:T(8,128)S(1)}, u32[]{:S(2)}, u32[]{:S(2)}) %collective-permute-start.7) | collective-permute-done | bytes 98336 | tf_op jit(solution)/shard_map/ppermute | solution.py:31
  104.5 2.1 %cycle.3 = (f32[3,512,256]{2,1,0:T(8,128)S(1)}, f32[512,256]{1,0:T(8,128)S(1)}, f32[8,128]{1,0:T(8,128)}) custom-call(f32[3,512,256]{2,1,0:T(8,128)S(1)} %get-tuple-element.48.w_ref.gradient_ref, f32[8,512]{1,0:T(8,128)S(1)} %collective-permute-done.4.left_ref, f32[8,512]{1,0:T(8,128)S(1)} %collective-permute-done.5.right_ref, ...), custom_call_target="tpu_custom_call" | custom-call | flops 100000 | bytes 1048576 | tf_op jit(solution)/shard_map/cycle/pallas_call | solution.py:425
  107.3 1.1 copy-done.4
  108.4 1.1 copy-done.10
  109.5 1.4 copy-done.5
  110.9 1.4 copy-done.11
  112.4 3.2 %second_owner.1 = (f32[3,512,256]{2,1,0:T(8,128)S(1)}, f32[32,128]{1,0:T(8,128)S(1)}, f32[6,32,256]{2,1,0:T(8,128)}, f32[6,32,256]{2,1,0:T(8,128)}, f32[8,512]{1,0:T(8,128)S(1)}, /*index=5*/f32[8,512]{1,0:T(8,128)S(1)}) custom-call(s32[32,128]{1,0:T(8,128)S(1)} %bitcast.31, f32[32,8,128]{2,1,0:T(8,128)S(1)} %all-to-all-done.4.returned_ref, ...), custom_call_target="tpu_custom_call" | custom-call | flops 100000 | bytes 1048576 | tf_op jit(solution)/shard_map/second_owner/pallas_call | solution.py:425
  115.6 4.0 %collective-permute-start.10 = (f32[6,32,256]{2,1,0:T(8,128)}, f32[6,32,256]{2,1,0:T(8,128)S(1)}, u32[]{:S(2)}, u32[]{:S(2)}) collective-permute-start(f32[6,32,256]{2,1,0:T(8,128)} %get-tuple-element.66), channel_id=1, source_target_pairs={{0,1},{1,2},{2,3},{3,4},{4,5},{5,6},{6,7},{8,9},{9,10},{10,11},{11... | collective-permute-start | bytes 589832 | tf_op jit(solution)/shard_map/ppermute | solution.py:31
  119.6 1.3 collective-permute-start.11
  120.9 6.3 %all-to-all-start.5 = ((f32[32,1,128]{2,1,0:T(1,128)}), f32[32,1,128]{2,1,0:T(1,128)S(1)}, u32[]{:S(2)}, u32[]{:S(2)}) async-start(f32[32,1,128]{2,1,0:T(1,128)} %bitcast.33), calls=%async_computation.5 | async-start | bytes 32768 | tf_op jit(solution)/shard_map/all_to_all | solution.py:25
  127.2 3.5 %collective-permute-start.8 = (f32[8,512]{1,0:T(8,128)}, f32[8,512]{1,0:T(8,128)S(1)}, u32[]{:S(2)}, u32[]{:S(2)}) collective-permute-start(f32[8,512]{1,0:T(8,128)} %copy-done.22), channel_id=1, source_target_pairs={{0,8},{8,16},{16,24},{1,9},{9,17},{17,25},{2,10},{10,18},{18,26},{... | collective-permute-start | bytes 49160 | tf_op jit(solution)/shard_map/ppermute | solution.py:31
  130.7 1.9 %collective-permute-start.9 = (f32[8,512]{1,0:T(8,128)}, f32[8,512]{1,0:T(8,128)S(1)}, u32[]{:S(2)}, u32[]{:S(2)}) collective-permute-start(f32[8,512]{1,0:T(8,128)} %copy-done.21), channel_id=1, source_target_pairs={{8,0},{16,8},{24,16},{9,1},{17,9},{25,17},{10,2},{18,10},{26,18},{... | collective-permute-start | bytes 49160 | tf_op jit(solution)/shard_map/ppermute | solution.py:31
  133.3 2.7 %collective-permute-done.9.right_ref = f32[8,512]{1,0:T(8,128)S(1)} collective-permute-done((f32[8,512]{1,0:T(8,128)}, f32[8,512]{1,0:T(8,128)S(1)}, u32[]{:S(2)}, u32[]{:S(2)}) %collective-permute-start.9) | collective-permute-done | bytes 16416 | tf_op jit(solution)/shard_map/ppermute | solution.py:31
  136.7 0.7 copy-done.15
  137.4 0.7 copy-done.17
  138.8 4.9 %final.1 = (f32[3,512,256]{2,1,0:T(8,128)}, f32[6,512,256]{2,1,0:T(8,128)}, f32[8,128]{1,0:T(8,128)S(1)}) custom-call(f32[32,128]{1,0:T(8,128)S(1)} %bitcast.32, f32[8,128]{1,0:T(8,128)S(1)} %copy-done.20, f32[3,512,256]{2,1,0:T(8,128)S(1)} %copy-done.6, f32[3,512,256]{2,1,0:T(8,128)S(1)} %get-tuple-element.63.gradient_ref, f32[8,512]{1,0:T(8,128)S(1)} %copy-done.15, ...), custom_call_target="tpu_custom_call" | custom-call | flops 100000 | bytes 1048576 | tf_op jit(solution)/shard_map/final/pallas_call | solution.py:425
  (54 shorter events, 6.2 us)
Async XLA Ops:
  1.9 13.7 %all-to-all-start = ((s32[32,1,128]{2,1,0:T(1,128)}), s32[32,1,128]{2,1,0:T(1,128)S(1)}, u32[]{:S(2)}, u32[]{:S(2)}) async-start(s32[32,1,128]{2,1,0:T(1,128)} %broadcast_in_dim.2), calls=%async_computation | async-start | bytes 32768 | tf_op jit(solution)/shard_map/all_to_all | solution.py:25
  15.7 1.4 copy-start
  18.9 17.8 %copy-start.1 = (f32[3,16,32,256]{3,2,1,0:T(8,128)S(1)}, f32[3,16,32,256]{3,2,1,0:T(8,128)}, u32[]{:S(2)}) copy-start(f32[3,16,32,256]{3,2,1,0:T(8,128)} %param.6) | copy-start | bytes 4718596
  19.0 10.3 %all-to-all-start.1 = ((bf16[32,8,128]{2,1,0:T(8,128)(2,1)}), bf16[32,8,128]{2,1,0:T(8,128)(2,1)S(1)}, u32[]{:S(2)}, u32[]{:S(2)}) async-start(bf16[32,8,128]{2,1,0:T(8,128)(2,1)} %pick.1), calls=%async_computation.1 | async-start | bytes 131072 | tf_op jit(solution)/shard_map/all_to_all | solution.py:25
  29.2 1.6 %copy-start.2 = (bf16[64,128,128]{2,1,0:T(8,128)(2,1)S(1)}, bf16[64,128,128]{2,1,0:T(8,128)(2,1)}, u32[]{:S(2)}) copy-start(bf16[64,128,128]{2,1,0:T(8,128)(2,1)} %weights_ref.3) | copy-start | bytes 6291460
  34.2 26.4 %all-to-all-start.2 = ((f32[32,8,128]{2,1,0:T(8,128)}), f32[32,8,128]{2,1,0:T(8,128)S(1)}, u32[]{:S(2)}, u32[]{:S(2)}) async-start(f32[32,8,128]{2,1,0:T(8,128)} %get-tuple-element.37), calls=%async_computation.2 | async-start | bytes 262144 | tf_op jit(solution)/shard_map/all_to_all | solution.py:25
  39.1 5.5 %collective-permute-start = (f32[8,512]{1,0:T(8,128)S(1)}, f32[8,512]{1,0:T(8,128)S(1)}, u32[]{:S(2)}, u32[]{:S(2)}) collective-permute-start(f32[8,512]{1,0:T(8,128)S(1)} %get-tuple-element.38), channel_id=1, source_target_pairs={{0,8},{8,16},{16,24},{1,9},{9,17},{17,25},{2,10},{10,18},{18,26},{... | collective-permute-start | bytes 49160 | tf_op jit(solution)/shard_map/ppermute | solution.py:31
  42.7 5.1 %collective-permute-start.1 = (f32[8,512]{1,0:T(8,128)S(1)}, f32[8,512]{1,0:T(8,128)S(1)}, u32[]{:S(2)}, u32[]{:S(2)}) collective-permute-start(f32[8,512]{1,0:T(8,128)S(1)} %get-tuple-element.39), channel_id=1, source_target_pairs={{8,0},{16,8},{24,16},{9,1},{17,9},{25,17},{10,2},{18,10},{26,18},{... | collective-permute-start | bytes 49160 | tf_op jit(solution)/shard_map/ppermute | solution.py:31
  48.0 4.8 %collective-permute-start.2 = (f32[3,32,256]{2,1,0:T(8,128)S(1)}, f32[3,32,256]{2,1,0:T(8,128)S(1)}, u32[]{:S(2)}, u32[]{:S(2)}) collective-permute-start(f32[3,32,256]{2,1,0:T(8,128)S(1)} %get-tuple-element.40), channel_id=1, source_target_pairs={{0,1},{1,2},{2,3},{3,4},{4,5},{5,6},{6,7},{8,9},{9,10},{10,11},{11... | collective-permute-start | bytes 294920 | tf_op jit(solution)/shard_map/ppermute | solution.py:31
  51.1 5.4 %collective-permute-start.3 = (f32[3,32,256]{2,1,0:T(8,128)S(1)}, f32[3,32,256]{2,1,0:T(8,128)S(1)}, u32[]{:S(2)}, u32[]{:S(2)}) collective-permute-start(f32[3,32,256]{2,1,0:T(8,128)S(1)} %get-tuple-element.41), channel_id=1, source_target_pairs={{1,0},{2,1},{3,2},{4,3},{5,4},{6,5},{7,6},{9,8},{10,9},{11,10},{12... | collective-permute-start | bytes 294920 | tf_op jit(solution)/shard_map/ppermute | solution.py:31
  58.7 1.2 copy-start.7
  59.8 0.8 copy-start.12
  60.6 1.4 copy-start.8
  79.4 1.6 %copy-start.3 = (bf16[64,128,128]{2,1,0:T(8,128)(2,1)S(1)}, bf16[64,128,128]{2,1,0:T(8,128)(2,1)}, u32[]{:S(2)}) copy-start(bf16[64,128,128]{2,1,0:T(8,128)(2,1)} %weights_ref.3) | copy-start | bytes 6291460
  84.5 11.4 %copy-start.19 = (f32[8,128]{1,0:T(8,128)}, f32[8,128]{1,0:T(8,128)S(1)}, u32[]{:S(2)}) copy-start(f32[8,128]{1,0:T(8,128)S(1)} %get-tuple-element.62.first_cost_ref) | copy-start | bytes 12292
  84.5 25.1 %all-to-all-start.4 = ((f32[32,8,128]{2,1,0:T(8,128)}), f32[32,8,128]{2,1,0:T(8,128)S(1)}, u32[]{:S(2)}, u32[]{:S(2)}) async-start(f32[32,8,128]{2,1,0:T(8,128)} %get-tuple-element.47), calls=%async_computation.4 | async-start | bytes 262144 | tf_op jit(solution)/shard_map/all_to_all | solution.py:25
  87.0 5.5 %collective-permute-start.4 = (f32[8,512]{1,0:T(8,128)S(1)}, f32[8,512]{1,0:T(8,128)S(1)}, u32[]{:S(2)}, u32[]{:S(2)}) collective-permute-start(f32[8,512]{1,0:T(8,128)S(1)} %get-tuple-element.49), channel_id=1, source_target_pairs={{0,8},{8,16},{16,24},{1,9},{9,17},{17,25},{2,10},{10,18},{18,26},{... | collective-permute-start | bytes 49160 | tf_op jit(solution)/shard_map/ppermute | solution.py:31
  90.6 5.1 %collective-permute-start.5 = (f32[8,512]{1,0:T(8,128)S(1)}, f32[8,512]{1,0:T(8,128)S(1)}, u32[]{:S(2)}, u32[]{:S(2)}) collective-permute-start(f32[8,512]{1,0:T(8,128)S(1)} %get-tuple-element.50), channel_id=1, source_target_pairs={{8,0},{16,8},{24,16},{9,1},{17,9},{25,17},{10,2},{18,10},{26,18},{... | collective-permute-start | bytes 49160 | tf_op jit(solution)/shard_map/ppermute | solution.py:31
  95.7 11.0 %copy-start.9 = (f32[3,512,256]{2,1,0:T(8,128)S(1)}, f32[3,512,256]{2,1,0:T(8,128)}, u32[]{:S(2)}) copy-start(f32[3,512,256]{2,1,0:T(8,128)} %copy-done.7) | copy-start | bytes 4718596
  95.7 11.0 %copy-start.13 = (f32[512,256]{1,0:T(8,128)S(1)}, f32[512,256]{1,0:T(8,128)}, u32[]{:S(2)}) copy-start(f32[512,256]{1,0:T(8,128)} %copy-done.12) | copy-start | bytes 1572868
  95.9 4.9 %collective-permute-start.6 = (f32[3,32,256]{2,1,0:T(8,128)S(1)}, f32[3,32,256]{2,1,0:T(8,128)S(1)}, u32[]{:S(2)}, u32[]{:S(2)}) collective-permute-start(f32[3,32,256]{2,1,0:T(8,128)S(1)} %get-tuple-element.51), channel_id=1, source_target_pairs={{0,1},{1,2},{2,3},{3,4},{4,5},{5,6},{6,7},{8,9},{9,10},{10,11},{11... | collective-permute-start | bytes 294920 | tf_op jit(solution)/shard_map/ppermute | solution.py:31
  99.2 5.4 %collective-permute-start.7 = (f32[3,32,256]{2,1,0:T(8,128)S(1)}, f32[3,32,256]{2,1,0:T(8,128)S(1)}, u32[]{:S(2)}, u32[]{:S(2)}) collective-permute-start(f32[3,32,256]{2,1,0:T(8,128)S(1)} %get-tuple-element.52), channel_id=1, source_target_pairs={{1,0},{2,1},{3,2},{4,3},{5,4},{6,5},{7,6},{9,8},{10,9},{11,10},{12... | collective-permute-start | bytes 294920 | tf_op jit(solution)/shard_map/ppermute | solution.py:31
  107.2 1.1 copy-start.4
  108.4 1.1 copy-start.10
  109.5 1.4 copy-start.5
  110.9 1.4 copy-start.11
  112.4 24.3 %copy-start.6 = (f32[3,512,256]{2,1,0:T(8,128)S(1)}, f32[3,512,256]{2,1,0:T(8,128)}, u32[]{:S(2)}) copy-start(f32[3,512,256]{2,1,0:T(8,128)} %copy-done.4) | copy-start | bytes 4718596
  115.6 4.0 %copy-start.21 = (f32[8,512]{1,0:T(8,128)}, f32[8,512]{1,0:T(8,128)S(1)}, u32[]{:S(2)}) copy-start(f32[8,512]{1,0:T(8,128)S(1)} %get-tuple-element.65) | copy-start | bytes 49156
  115.6 4.0 %copy-start.22 = (f32[8,512]{1,0:T(8,128)}, f32[8,512]{1,0:T(8,128)S(1)}, u32[]{:S(2)}) copy-start(f32[8,512]{1,0:T(8,128)S(1)} %get-tuple-element.64) | copy-start | bytes 49156
  115.6 5.3 %copy-start.18 = (f32[32,128]{1,0:T(8,128)}, f32[32,128]{1,0:T(8,128)S(1)}, u32[]{:S(2)}) copy-start(f32[32,128]{1,0:T(8,128)S(1)} %get-tuple-element.61) | copy-start | bytes 49156
  115.6 21.1 %collective-permute-start.10 = (f32[6,32,256]{2,1,0:T(8,128)}, f32[6,32,256]{2,1,0:T(8,128)S(1)}, u32[]{:S(2)}, u32[]{:S(2)}) collective-permute-start(f32[6,32,256]{2,1,0:T(8,128)} %get-tuple-element.66), channel_id=1, source_target_pairs={{0,1},{1,2},{2,3},{3,4},{4,5},{5,6},{6,7},{8,9},{9,10},{10,11},{11... | collective-permute-start | bytes 589832 | tf_op jit(solution)/shard_map/ppermute | solution.py:31
  119.6 17.0 %collective-permute-start.11 = (f32[6,32,256]{2,1,0:T(8,128)}, f32[6,32,256]{2,1,0:T(8,128)S(1)}, u32[]{:S(2)}, u32[]{:S(2)}) collective-permute-start(f32[6,32,256]{2,1,0:T(8,128)} %get-tuple-element.67), channel_id=1, source_target_pairs={{1,0},{2,1},{3,2},{4,3},{5,4},{6,5},{7,6},{9,8},{10,9},{11,10},{12... | collective-permute-start | bytes 589832 | tf_op jit(solution)/shard_map/ppermute | solution.py:31
  120.9 15.7 %all-to-all-start.5 = ((f32[32,1,128]{2,1,0:T(1,128)}), f32[32,1,128]{2,1,0:T(1,128)S(1)}, u32[]{:S(2)}, u32[]{:S(2)}) async-start(f32[32,1,128]{2,1,0:T(1,128)} %bitcast.33), calls=%async_computation.5 | async-start | bytes 32768 | tf_op jit(solution)/shard_map/all_to_all | solution.py:25
  127.2 5.5 %collective-permute-start.8 = (f32[8,512]{1,0:T(8,128)}, f32[8,512]{1,0:T(8,128)S(1)}, u32[]{:S(2)}, u32[]{:S(2)}) collective-permute-start(f32[8,512]{1,0:T(8,128)} %copy-done.22), channel_id=1, source_target_pairs={{0,8},{8,16},{16,24},{1,9},{9,17},{17,25},{2,10},{10,18},{18,26},{... | collective-permute-start | bytes 49160 | tf_op jit(solution)/shard_map/ppermute | solution.py:31
  130.7 5.3 %collective-permute-start.9 = (f32[8,512]{1,0:T(8,128)}, f32[8,512]{1,0:T(8,128)S(1)}, u32[]{:S(2)}, u32[]{:S(2)}) collective-permute-start(f32[8,512]{1,0:T(8,128)} %copy-done.21), channel_id=1, source_target_pairs={{8,0},{16,8},{24,16},{9,1},{17,9},{25,17},{10,2},{18,10},{26,18},{... | collective-permute-start | bytes 49160 | tf_op jit(solution)/shard_map/ppermute | solution.py:31
  132.7 0.6 copy-start.14
  136.0 0.6 copy-start.16
  136.6 0.7 copy-start.15
  137.4 0.7 copy-start.17
  138.1 0.7 copy-start.20

commit v3 on v2

v3 whole, which is shorter than its diff:
```python
import functools

import jax
import jax.numpy as jnp
from jax import lax
from jax.experimental import pallas as pl
from jax.experimental.pallas import tpu as pltpu
from jax.sharding import PartitionSpec as P


BACKGROUND_WEIGHT = 0.5
DIVERGENCE_WEIGHT = 1.0
STEP_LENGTH = 0.3
EPSILON = 1e-06

AXES = ("radar", "tile")
LANES = 128
PARTS = 4
F32 = jnp.float32
BF16 = jnp.bfloat16

COL_WY, COL_WX, COL_PART = 0, 1, 2
ROW_WX, ROW_PART = 0, 1
CORNERS = ((-1, -1), (-1, 1), (1, -1), (1, 1))


def exchange(x):
    return lax.all_to_all(x, AXES, split_axis=0, concat_axis=0, tiled=True)


def shifted(x, axis, step):
    size = lax.axis_size(axis)
    pairs = [(i, i + step) for i in range(size) if 0 <= i + step < size]
    return lax.ppermute(x, axis, pairs)


class Pieces:
    def __init__(self, source, target, sems, parts, at=0):
        rows = source.shape[-2]
        self.share = rows // parts
        self.copies = []
        self.seen = 0
        for i in range(parts):
            here = pl.ds(i * self.share, self.share)
            there = pl.ds(at + i * self.share, self.share)
            lead = (slice(None),) * (len(source.shape) - 2)
            self.copies.append(pltpu.make_async_copy(source.at[lead + (here,)], target.at[lead + (there,)], sems.at[i]))

    def start(self):
        for copy in self.copies:
            copy.start()
        return self

    def until(self, row):
        while self.seen < len(self.copies) and self.seen * self.share < row:
            self.copies[self.seen].wait()
            self.seen += 1

    def filled(self, row):
        while self.seen < len(self.copies) and (self.seen + 1) * self.share <= row:
            self.copies[self.seen].start()
            self.seen += 1

    def finish(self):
        for copy in self.copies:
            copy.wait()


class OutPieces(Pieces):
    def __init__(self, source, target, sems, parts, at=0):
        rows = target.shape[-2]
        self.share = rows // parts
        self.copies = []
        self.seen = 0
        for i in range(parts):
            here = pl.ds(at + i * self.share, self.share)
            there = pl.ds(i * self.share, self.share)
            lead = (slice(None),) * (len(source.shape) - 2)
            self.copies.append(pltpu.make_async_copy(source.at[lead + (here,)], target.at[lead + (there,)], sems.at[i]))


def iota(shape, dim):
    return lax.broadcasted_iota(jnp.int32, shape, dim)


def diff_levels(a, period):
    rows = a.shape[0]
    level = lax.rem(iota(a.shape, 0), jnp.int32(period))
    above = jnp.where(level == period - 1, 0.0, pltpu.roll(a, rows - 1, 0))
    below = jnp.where(level == 0, 0.0, pltpu.roll(a, 1, 0))
    return above - below


def diff_columns(a, left, right):
    width = a.shape[1]
    lane = iota(a.shape, 1)
    after = jnp.where(lane == width - 1, right, pltpu.roll(a, width - 1, 1))
    before = jnp.where(lane == 0, left, pltpu.roll(a, 1, 1))
    return after - before


def to_rows(columns):
    fill = jnp.zeros((LANES - columns.shape[0], columns.shape[1]), F32)
    return jnp.concatenate([columns, fill], axis=0).T


def sum_rows(a):
    total = a[:, :LANES]
    for start in range(LANES, a.shape[1], LANES):
        total = total + a[:, start : start + LANES]
    return jnp.sum(total, axis=0, keepdims=True)


def paired(first, second):
    half = LANES // 2
    lower = iota((1, LANES), 1) < half
    return jnp.where(lower, first + pltpu.roll(first, half, 1), second + pltpu.roll(second, half, 1))


def halves(line):
    lower = iota((1, LANES), 1) < LANES // 2
    return (
        jnp.sum(jnp.where(lower, line, 0.0), axis=1, keepdims=True),
        jnp.sum(jnp.where(lower, 0.0, line), axis=1, keepdims=True),
    )


def own_place():
    return lax.axis_index("radar") * lax.axis_size("tile") + lax.axis_index("tile")


def neighbour(along_tile, along_radar):
    tile = lax.axis_index("tile") + along_tile
    radar = lax.axis_index("radar") + along_radar
    exists = (tile >= 0) & (tile < lax.axis_size("tile")) & (radar >= 0) & (radar < lax.axis_size("radar"))
    return exists, jnp.where(exists, radar * lax.axis_size("tile") + tile, own_place())


def corner_lines(w_ref, levels):
    rows, width = w_ref.shape[1], w_ref.shape[2]
    lane = iota((levels, LANES), 1)
    packed = jnp.zeros((levels, LANES), F32)
    for c, (along_tile, along_radar) in enumerate(CORNERS):
        here = slice(0, levels) if along_tile < 0 else slice(rows - levels, rows)
        lanes, at = (slice(0, LANES), 0) if along_radar < 0 else (slice(width - LANES, width), LANES - 1)
        for k in range(2):
            packed = lane_column(packed, lane, w_ref[k, here, lanes], at, 2 * c + k)
    turned = jnp.concatenate([packed, jnp.zeros((LANES - levels, LANES), F32)], axis=0).T
    return [
        turned[2 * c : 2 * c + 1] + pltpu.roll(turned[2 * c + 1 : 2 * c + 2], levels, 1) for c in range(len(CORNERS))
    ]


def corner_columns(line_from, levels):
    lines = []
    for along_tile, along_radar in CORNERS:
        exists, place = neighbour(along_tile, along_radar)
        lines.append(jnp.where(exists, line_from(place), 0.0))
    fill = jnp.zeros((LANES - len(CORNERS), LANES), F32)
    turned = jnp.concatenate(lines + [fill], axis=0).T
    return [(turned[0:levels, c : c + 1], turned[levels : 2 * levels, c : c + 1]) for c in range(len(CORNERS))]


def block_at(index, runs):
    if runs & (runs - 1) == 0:
        return lax.shift_right_logical(index, jnp.int32(runs.bit_length() - 1)), index & (runs - 1)
    return lax.div(index, jnp.int32(runs)), lax.rem(index, jnp.int32(runs))


def read_block(ref, k, row, run):
    line = ref[k, pl.ds(row, 1), :]
    out = line[:, :LANES]
    for h in range(1, ref.shape[2] // LANES):
        out = jnp.where(run == h, line[:, h * LANES : (h + 1) * LANES], out)
    return out


def lane_column(packed, lane, tile, at, to):
    moved = tile if at == to else pltpu.roll(tile, (to - at) % LANES, 1)
    return jnp.where(lane == to, moved, packed)


def edges_kernel(levels, w_hbm, left_out, right_out, up_out, down_out, w_ref, scratch, sem):
    copy = pltpu.make_async_copy(w_hbm, w_ref, sem)
    copy.start()
    copy.wait()
    rows, width = w_ref.shape[1], w_ref.shape[2]
    lane = iota((levels, LANES), 1)
    last = slice(width - LANES, width)
    for x in range(rows // levels):
        here = slice(x * levels, (x + 1) * levels)
        packed = jnp.where(lane < LANES // 2, w_ref[1, here, :LANES], w_ref[1, here, last])
        packed = lane_column(packed, lane, w_ref[0, here, :LANES], 0, 2)
        packed = lane_column(packed, lane, w_ref[2, here, :LANES], 0, 3)
        packed = lane_column(packed, lane, w_ref[0, here, last], LANES - 1, LANES - 3)
        packed = lane_column(packed, lane, w_ref[2, here, last], LANES - 1, LANES - 4)
        scratch[here, :] = packed
    turned = scratch[...].T
    place = iota((1, rows), 1)
    level = lax.rem(place, jnp.int32(levels))

    def partial(wx, wz):
        part = jnp.where(level == levels - 1, 0.0, pltpu.roll(wz, rows - 1, 1))
        part = part - jnp.where(level == 0, 0.0, pltpu.roll(wz, 1, 1))
        part = part + jnp.where(place >= rows - levels, 0.0, pltpu.roll(wx, rows - levels, 1))
        return part - jnp.where(place < levels, 0.0, pltpu.roll(wx, levels, 1))

    near, far = turned[0:8], turned[LANES - 8 : LANES]
    for out, wy, inner, wx, wz in (
        (left_out, near[0:1], near[1:2], near[2:3], near[3:4]),
        (right_out, far[7:8], -far[6:7], far[5:6], far[4:5]),
    ):
        out[...] = jnp.zeros_like(out)
        out[COL_WY : COL_WY + 1, :] = wy
        out[COL_WX : COL_WX + 1, :] = wx
        out[COL_PART : COL_PART + 1, :] = 0.5 * (inner + partial(wx, wz))
    for out, first in ((up_out, 0), (down_out, rows - levels)):
        here = slice(first, first + levels)
        part = diff_levels(w_ref[2, here, :], levels) + diff_columns(w_ref[1, here, :], 0.0, 0.0)
        if first > 0:
            part = part - w_ref[0, first - levels : first, :]
        else:
            part = part + w_ref[0, levels : 2 * levels, :]
        out[ROW_WX] = w_ref[0, here, :]
        out[ROW_PART] = 0.5 * part


def cycle(levels, w_ref, left_ref, right_ref, above_ref, below_ref, corners, ring, left_rows, right_rows, need, take_spread, take_push):
    rows, width = w_ref.shape[1], w_ref.shape[2]
    cells = rows // levels
    left_rows[...] = to_rows(left_ref[...])
    right_rows[...] = to_rows(right_ref[...])
    has_left = jnp.where(lax.axis_index("radar") > 0, 1.0, 0.0)
    has_right = jnp.where(lax.axis_index("radar") < lax.axis_size("radar") - 1, 1.0, 0.0)
    has_above = jnp.where(lax.axis_index("tile") > 0, 1.0, 0.0)
    has_below = jnp.where(lax.axis_index("tile") < lax.axis_size("tile") - 1, 1.0, 0.0)
    above_left, above_right, below_left, below_right = corners
    lane = iota((levels, width), 1)

    def ends(left, right):
        return jnp.where(lane == 0, -0.5 * left, jnp.where(lane == width - 1, 0.5 * right, 0.0))

    first, last = slice(0, levels), slice(rows - levels, rows)
    for x in range(cells):
        here = slice(x * levels, (x + 1) * levels)
        need(min(rows, (x + 2) * levels))
        after = w_ref[0, (x + 1) * levels : (x + 2) * levels, :] if x + 1 < cells else below_ref[ROW_WX]
        before = w_ref[0, (x - 1) * levels : x * levels, :] if x > 0 else above_ref[ROW_WX]
        spread = 0.5 * (
            (after - before)
            + diff_columns(
                w_ref[1, here, :],
                left_rows[here, COL_WY : COL_WY + 1],
                right_rows[here, COL_WY : COL_WY + 1],
            )
            + diff_levels(w_ref[2, here, :], levels)
        )
        ring[(x + 1) * levels : (x + 2) * levels, :] = spread
        take_spread(here, spread)
    above = above_ref[ROW_PART] + 0.5 * w_ref[0, first, :] + ends(above_left[1], above_right[1])
    below = below_ref[ROW_PART] - 0.5 * w_ref[0, last, :] + ends(below_left[1], below_right[1])
    ring[0:levels, :] = has_above * above
    ring[rows + levels : rows + 2 * levels, :] = has_below * below
    for x in range(cells):
        here = slice(x * levels, (x + 1) * levels)
        left = left_rows[here, COL_PART : COL_PART + 1] + 0.5 * w_ref[1, here, 0:1]
        right = right_rows[here, COL_PART : COL_PART + 1] - 0.5 * w_ref[1, here, width - 1 : width]
        if x == 0:
            left = left - 0.5 * above_left[0]
            right = right - 0.5 * above_right[0]
        if x == cells - 1:
            left = left + 0.5 * below_left[0]
            right = right + 0.5 * below_right[0]
        spread = ring[(x + 1) * levels : (x + 2) * levels, :]
        after = ring[(x + 2) * levels : (x + 3) * levels, :]
        before = ring[x * levels : (x + 1) * levels, :]
        take_push(0, here, (-0.5 * DIVERGENCE_WEIGHT) * (after - before))
        take_push(1, here, (-0.5 * DIVERGENCE_WEIGHT) * diff_columns(spread, has_left * left, has_right * right))
        take_push(2, here, (-0.5 * DIVERGENCE_WEIGHT) * diff_levels(spread, levels))


def first_cycle_kernel(levels, slots, w_hbm, left_ref, right_ref, above_ref, below_ref, cells_ref, push_hbm, spread_hbm, total_out, w_ref, push, ring, left_rows, right_rows, total, sems):
    fields = Pieces(w_hbm, w_ref, sems.at[0], PARTS).start()
    total[...] = jnp.zeros_like(total)
    spreads = OutPieces(ring, spread_hbm, sems.at[1], PARTS, levels)
    pushes = OutPieces(push, push_hbm, sems.at[2], PARTS)

    def line_from(place):
        block = cells_ref[pl.ds(place, 1)].reshape(cells_ref.shape[1:]).astype(F32)
        first = block[3 * slots : 3 * slots + 1]
        return first + pltpu.roll(first, LANES // 2, 1) + block[3 * slots + 1 : 3 * slots + 2]

    def take_spread(here, spread):
        total[...] += spread * spread
        spreads.filled(here.stop)

    def take_push(k, here, value):
        push[k, here, :] = value
        if k == 2:
            pushes.filled(here.stop)

    corners = corner_columns(line_from, levels)
    cycle(levels, w_ref, left_ref, right_ref, above_ref, below_ref, corners, ring, left_rows, right_rows, fields.until, take_spread, take_push)
    total_out[...] = jnp.broadcast_to(0.5 * DIVERGENCE_WEIGHT * sum_rows(total[...]), total_out.shape)
    spreads.finish()
    pushes.finish()


def second_cycle_kernel(levels, slots, w_hbm, left_ref, right_ref, above_ref, below_ref, got_ref, background_hbm, push_hbm, spread_hbm, step_ref, rest_hbm, wind_hbm, total_out, w_ref, background, push, spread, ring, left_rows, right_rows, total, sems):
    fields = Pieces(w_hbm, w_ref, sems.at[0], PARTS).start()
    spreads = Pieces(spread_hbm, spread, sems.at[1], PARTS).start()
    pushes = Pieces(push_hbm, push, sems.at[2], PARTS).start()
    backgrounds = Pieces(background_hbm, background, sems.at[3], PARTS).start()
    rests = OutPieces(push, rest_hbm, sems.at[4], PARTS)
    winds = OutPieces(background, wind_hbm, sems.at[5], PARTS)
    total[...] = jnp.zeros_like(total)
    step = step_ref[0:1, 0:1]

    def line_from(place):
        return got_ref[place, 3 * slots + 1 : 3 * slots + 2, :]

    def take_spread(here, bent):
        spreads.until(here.stop)
        value = spread[here, :] - step * bent
        total[...] += (0.5 * DIVERGENCE_WEIGHT) * (value * value)

    def take_push(k, here, bent):
        pushes.until(here.stop)
        backgrounds.until(here.stop)
        offset = step * w_ref[k, here, :]
        total[...] += (0.5 * BACKGROUND_WEIGHT) * (offset * offset)
        background[k, here, :] = background[k, here, :] - offset
        push[k, here, :] = push[k, here, :] - (BACKGROUND_WEIGHT * offset + step * bent)
        if k == 2:
            rests.filled(here.stop)
            winds.filled(here.stop)

    corners = corner_columns(line_from, levels)
    cycle(levels, w_ref, left_ref, right_ref, above_ref, below_ref, corners, ring, left_rows, right_rows, fields.until, take_spread, take_push)
    total_out[...] = jnp.broadcast_to(sum_rows(total[...]), total_out.shape)
    rests.finish()
    winds.finish()


def for_slots(count, body, step=4):
    def run(i, carry):
        for j in range(step):
            body(i * step + j)
        return carry

    lax.fori_loop(0, count // step, run, 0)


def ask(asked_hbm, asked_ref, sem):
    return pltpu.make_async_copy(asked_hbm.at[:, 0, :], asked_ref, sem)


def pick_kernel(slots, levels, asked_hbm, w_ref, out_ref, rows_ref, asked_ref, ask_sem):
    asking = ask(asked_hbm, asked_ref, ask_sem)
    asking.start()
    me = own_place()
    runs = w_ref.shape[2] // LANES
    rows_ref[...] = jnp.zeros_like(rows_ref)
    asking.wait()

    def one(s):
        for p in range(slots):
            row, run = block_at(asked_ref[s, me * slots + p], runs)
            for k in range(3):
                rows_ref[s, 3 * p + k : 3 * p + k + 1, :] = read_block(w_ref, k, row, run)

    for_slots(out_ref.shape[0], one)
    for (along_tile, along_radar), line in zip(CORNERS, corner_lines(w_ref, levels)):
        exists, place = neighbour(along_tile, along_radar)
        high = line.astype(BF16).astype(F32)
        middle = (line - high).astype(BF16).astype(F32)

        @pl.when(exists)
        def _():
            rows_ref[place, 3 * slots : 3 * slots + 1, :] = high + pltpu.roll(middle, LANES // 2, 1)
            rows_ref[place, 3 * slots + 1 : 3 * slots + 2, :] = line - high - middle

    out_ref[...] = rows_ref[...].astype(out_ref.dtype)


def project(cells_of, weights_ref, proj_ref, sources, slots, height):
    def one(s):
        weights = weights_ref[pl.ds(s * slots, slots)].reshape(slots * LANES, LANES)
        seen = lax.dot_general(cells_of(s), weights, (((1,), (1,)), ((), ())), preferred_element_type=F32)
        here = pl.ds(pl.multiple_of(s * height, height), height)
        for p in range(slots):
            proj_ref[p, here, :] = seen[:, p * LANES : (p + 1) * LANES]

    for_slots(sources, one)


def radial(proj_ref, sight_ref, p, sources, height):
    total = jnp.zeros((sources, LANES), F32)
    for k in range(3):
        total = total + sight_ref[3 * p + k] * proj_ref[p, pl.ds(3 * p + k, sources, stride=height), :]
    return total


def give_back(misfits, weights_ref, sight_ref, adj_ref, out_ref, sources, slots, height):
    adj_ref[...] = jnp.zeros_like(adj_ref)
    for p in range(slots):
        for k in range(3):
            adj_ref[p, pl.ds(3 * p + k, sources, stride=height), :] = sight_ref[3 * p + k] * misfits[p]

    def one(s):
        weights = weights_ref[pl.ds(s * slots, slots)].reshape(slots * LANES, LANES)
        here = pl.ds(pl.multiple_of(s * height, height), height)
        adjoint = jnp.concatenate([adj_ref[p, here, :] for p in range(slots)], axis=1).astype(BF16)
        out_ref[s] = lax.dot_general(adjoint, weights, (((1,), (0,)), ((), ())), preferred_element_type=F32)

    for_slots(sources, one)


def first_source_kernel(slots, cells_ref, weights_ref, sight_ref, returned_out, misfit_out, cost_out, proj_ref, adj_ref):
    sources, height = cells_ref.shape[0], cells_ref.shape[1]
    project(lambda s: cells_ref[s].astype(BF16), weights_ref, proj_ref, sources, slots, height)
    misfits = []
    cost = jnp.zeros((1, LANES), F32)
    for p in range(slots):
        misfit = radial(proj_ref, sight_ref, p, sources, height) - sight_ref[3 * slots + p]
        misfit_out[p] = misfit
        cost = cost + 0.5 * jnp.sum(misfit * misfit, axis=0, keepdims=True)
        misfits.append(misfit)
    cost_out[...] = jnp.broadcast_to(cost, cost_out.shape)
    give_back(misfits, weights_ref, sight_ref, adj_ref, returned_out, sources, slots, height)


def second_source_kernel(slots, total_cells, total_gates, got_ref, weights_ref, sight_ref, misfit_ref, returned_out, step_out, cost_out, done_out, proj_ref, adj_ref):
    sources, height = got_ref.shape[0], got_ref.shape[1]
    project(lambda s: got_ref[s].astype(BF16), weights_ref, proj_ref, sources, slots, height)
    squares, costs = halves(jnp.sum(got_ref[:, 3 * slots, :], axis=0, keepdims=True))
    step = STEP_LENGTH / jnp.sqrt(squares / total_cells + EPSILON)
    step_out[...] = jnp.broadcast_to(step, step_out.shape)
    done_out[...] = jnp.broadcast_to(costs / total_gates, done_out.shape)
    misfits = []
    cost = jnp.zeros((1, LANES), F32)
    for p in range(slots):
        misfit = misfit_ref[p] - step * radial(proj_ref, sight_ref, p, sources, height)
        cost = cost + 0.5 * jnp.sum(misfit * misfit, axis=0, keepdims=True)
        misfits.append(misfit)
    cost_out[...] = jnp.broadcast_to(cost, cost_out.shape)
    give_back(misfits, weights_ref, sight_ref, adj_ref, returned_out, sources, slots, height)


def scatter_rows(slots, asked_ref, returned_ref, out_ref):
    me = own_place()
    runs = out_ref.shape[2] // LANES
    place = iota((8, LANES), 0)

    def one(s):
        for p in range(slots):
            row, run = block_at(asked_ref[s, me * slots + p], runs)
            within = lax.rem(row, jnp.int32(8))
            base = pl.multiple_of(row - within, 8)
            lanes = pl.ds(pl.multiple_of(run * LANES, LANES), LANES)
            held = [out_ref[k, pl.ds(base, 8), lanes] for k in range(3)]
            for k in range(3):
                line = returned_ref[s, 3 * p + k : 3 * p + k + 1, :]
                held[k] = held[k] + jnp.where(place == within, line, 0.0)
            for k in range(3):
                out_ref[k, pl.ds(base, 8), lanes] = held[k]

    for_slots(returned_ref.shape[0], one)


def gather_gradient(slots, levels, asked_hbm, asked_ref, returned_ref, rest_hbm, rest, gradient_ref, gradient_hbm, sems):
    rows, width = gradient_ref.shape[1], gradient_ref.shape[2]
    cells = rows // levels
    copy = pltpu.make_async_copy(rest_hbm, rest, sems.at[cells])
    asking = ask(asked_hbm, asked_ref, sems.at[cells + 1])
    asking.start()
    copy.start()
    gradient_ref[...] = jnp.zeros_like(gradient_ref)
    asking.wait()
    scatter_rows(slots, asked_ref, returned_ref, gradient_ref)
    copy.wait()
    total = jnp.zeros((levels, width), F32)
    copies = []
    for x in range(cells):
        here = slice(x * levels, (x + 1) * levels)
        for k in range(3):
            piece = gradient_ref[k, here, :] + rest[k, here, :]
            gradient_ref[k, here, :] = piece
            total = total + piece * piece
        if gradient_hbm is not None:
            copies.append(pltpu.make_async_copy(gradient_ref.at[:, here], gradient_hbm.at[:, here], sems.at[x]))
            copies[-1].start()
    return sum_rows(total), copies


def first_owner_kernel(slots, levels, asked_hbm, returned_ref, push_hbm, seen_cost_ref, spread_cost_ref, gradient_hbm, give_out, push, gradient, asked_ref, sems):
    squares, copies = gather_gradient(
        slots, levels, asked_hbm, asked_ref, returned_ref, push_hbm, push, gradient, gradient_hbm, sems
    )
    sources = give_out.shape[0]
    sums = paired(squares, seen_cost_ref[0:1, :] + spread_cost_ref[0:1, :])
    give_out[...] = jnp.zeros_like(give_out)
    give_out[:, 3 * slots, :] = jnp.broadcast_to(sums, (sources, LANES))
    me = own_place()
    runs = gradient.shape[2] // LANES

    def one(s):
        for p in range(slots):
            row, run = block_at(asked_ref[s, me * slots + p], runs)
            for k in range(3):
                give_out[s, 3 * p + k : 3 * p + k + 1, :] = read_block(gradient, k, row, run)

    for_slots(sources, one)
    for (along_tile, along_radar), line in zip(CORNERS, corner_lines(gradient, levels)):
        exists, place = neighbour(along_tile, along_radar)

        @pl.when(exists)
        def _():
            give_out[place, 3 * slots + 1 : 3 * slots + 2, :] = line

    for copy in copies:
        copy.wait()


def second_owner_kernel(slots, levels, asked_hbm, returned_ref, rest_hbm, seen_cost_ref, rest_cost_ref, gradient_out, give_out, rest, asked_ref, sems):
    squares, _ = gather_gradient(
        slots, levels, asked_hbm, asked_ref, returned_ref, rest_hbm, rest, gradient_out, None, sems
    )
    sums = paired(squares, seen_cost_ref[0:1, :] + rest_cost_ref[0:1, :])
    give_out[...] = jnp.broadcast_to(sums, give_out.shape)


def final_edges_kernel(levels, wind_ref, gradient_ref, up_out, down_out, left_out, right_out, scratch):
    rows, width = wind_ref.shape[1], wind_ref.shape[2]
    fields = [(wind_ref, k) for k in range(3)] + [(gradient_ref, k) for k in range(3)]
    for f, (ref, k) in enumerate(fields):
        up_out[f] = ref[k, 0:levels, :]
        down_out[f] = ref[k, rows - levels : rows, :]
    lane = iota((levels, LANES), 1)
    for x in range(rows // levels):
        here = slice(x * levels, (x + 1) * levels)
        packed = jnp.zeros((levels, LANES), F32)
        for f, (ref, k) in enumerate(fields):
            packed = lane_column(packed, lane, ref[k, here, :LANES], 0, f)
            packed = lane_column(packed, lane, ref[k, here, width - LANES :], LANES - 1, LANES - 8 + f)
        scratch[here, :] = packed
    turned = scratch[...].T
    left_out[...] = turned[0:8]
    right_out[...] = turned[LANES - 8 : LANES]


def final_kernel(levels, total_cells, total_gates, sums_ref, first_cost_ref, wind_hbm, gradient_ref, left_ref, right_ref, above_ref, below_ref, wind_out, strain_out, cost_out, left_rows, right_rows, wind, strain, sems):
    rows = gradient_ref.shape[1]
    cells = rows // levels
    winds = Pieces(wind_hbm, wind, sems.at[0], PARTS).start()
    wind_outs = OutPieces(wind, wind_out, sems.at[1], PARTS)
    strain_outs = OutPieces(strain, strain_out, sems.at[2], PARTS)
    squares, cost = halves(jnp.sum(sums_ref[:, 0, :], axis=0, keepdims=True))
    cost = cost / total_gates
    step = STEP_LENGTH / jnp.sqrt(squares / total_cells + EPSILON)
    out_lane = iota(cost_out.shape, 1)
    cost_out[...] = jnp.where(out_lane == 0, first_cost_ref[...], cost)
    left_rows[...] = to_rows(left_ref[...])
    right_rows[...] = to_rows(right_ref[...])

    def settle(x):
        here = slice(x * levels, (x + 1) * levels)
        winds.until(here.stop)
        for k in range(3):
            wind[k, here, :] = wind[k, here, :] - step * gradient_ref[k, here, :]
        wind_outs.filled(here.stop)

    settle(0)
    for x in range(cells):
        here = slice(x * levels, (x + 1) * levels)
        if x + 1 < cells:
            settle(x + 1)
        along = []
        for k in range(3):
            value = wind[k, here, :]
            if x + 1 < cells:
                after = wind[k, (x + 1) * levels : (x + 2) * levels, :]
            else:
                after = below_ref[k] - step * below_ref[3 + k]
            if x > 0:
                before = wind[k, (x - 1) * levels : x * levels, :]
            else:
                before = above_ref[k] - step * above_ref[3 + k]
            left = left_rows[here, k : k + 1] - step * left_rows[here, 3 + k : 4 + k]
            right = right_rows[here, k : k + 1] - step * right_rows[here, 3 + k : 4 + k]
            along.append((after - before, diff_columns(value, left, right), diff_levels(value, levels)))
        (xx, xy, xz), (yx, yy, yz), (zx, zy, zz) = along
        strain[0, here, :] = 0.5 * xx
        strain[1, here, :] = 0.5 * yy
        strain[2, here, :] = 0.5 * zz
        strain[3, here, :] = 0.25 * (xy + yx)
        strain[4, here, :] = 0.25 * (xz + zx)
        strain[5, here, :] = 0.25 * (yz + zy)
        strain_outs.filled(here.stop)
    wind_outs.finish()
    strain_outs.finish()


def shape(*dims, dtype=F32):
    return jax.ShapeDtypeStruct(dims, dtype)


VMEM = pl.BlockSpec(memory_space=pltpu.VMEM)
SMEM = pl.BlockSpec(memory_space=pltpu.SMEM)
ANY = pl.BlockSpec(memory_space=pl.ANY)


def call(kernel, out_shape, args, scratch=(), scalars=0, raw=(), out_raw=(), chip=(), out_chip=(), flops=2000000, limit=16):
    single = not isinstance(out_shape, tuple)
    outs = (out_shape,) if single else out_shape
    held = [
        x if i < scalars or i in chip else pltpu.with_memory_space_constraint(x, pltpu.HBM)
        for i, x in enumerate(args)
    ]
    placed = tuple(o if i in out_chip else pltpu.HBM(o.shape, o.dtype) for i, o in enumerate(outs))
    specs = tuple(ANY if i in out_raw else VMEM for i in range(len(outs)))
    return pl.pallas_call(
        kernel,
        out_shape=placed[0] if single else placed,
        in_specs=[SMEM if i < scalars else ANY if i in raw else VMEM for i in range(len(args))],
        out_specs=specs[0] if single else specs,
        scratch_shapes=list(scratch),
        compiler_params=pltpu.CompilerParams(vmem_limit_bytes=limit * 1024 * 1024),
        cost_estimate=pl.CostEstimate(flops=flops, bytes_accessed=1 << 20, transcendentals=0),
    )(*held)


def shards(background, interp, beam, observed, cell_block, sweep_count):
    radar_count = lax.axis_size("radar")
    tile_count = lax.axis_size("tile")
    devices = radar_count * tile_count
    width_x, levels, width_y = background.shape[1:]
    slots = interp.shape[0] // devices
    gate_size = interp.shape[1]
    rows = width_x * levels
    height = -(-(3 * slots + 2) // 8) * 8
    total_cells = float(3 * rows * width_y * devices)
    total_gates = float(interp.shape[0] * devices * gate_size)
    field = background.reshape(3, rows, width_y)
    lanes = -(-devices * slots // LANES) * LANES
    line = jnp.pad(cell_block, (0, lanes - devices * slots))
    asked = exchange(jnp.broadcast_to(line[None, None, :], (devices, 8, lanes)))

    live = (jnp.arange(slots, dtype=jnp.int32)[:, None, None] < sweep_count.reshape(1, devices, 1)).astype(F32)
    sight = beam.reshape(devices, slots, 3, gate_size).transpose(1, 2, 0, 3).astype(F32) * live[:, None]
    seen = observed.reshape(devices, slots, gate_size).transpose(1, 0, 2).astype(F32) * live
    sight = jnp.concatenate([sight.reshape(3 * slots, devices, gate_size), seen], axis=0)

    edges = (shape(8, rows), shape(8, rows))
    row_edges = (shape(2, levels, width_y), shape(2, levels, width_y))
    grid = shape(3, rows, width_y)
    line_out = shape(8, LANES)
    side = pltpu.VMEM((rows, LANES), F32)
    whole = pltpu.VMEM((3, rows, width_y), F32)
    plane = pltpu.VMEM((rows, width_y), F32)
    ring = pltpu.VMEM((rows + 2 * levels, width_y), F32)
    strip = pltpu.VMEM((levels, width_y), F32)
    semaphores = pltpu.SemaphoreType.DMA
    places = pltpu.SMEM((devices, lanes), jnp.int32)

    def halo(left, right, up, down):
        from_left = shifted(right, "radar", 1)
        from_right = shifted(left, "radar", -1)
        above = shifted(down, "tile", 1)
        below = shifted(up, "tile", -1)
        return from_left, from_right, above, below

    def edges_of(values):
        out = call(
            functools.partial(edges_kernel, levels), edges + row_edges, (values,), (whole, side, semaphores), raw=(0,)
        )
        return halo(*out)

    around = edges_of(field)
    cells = call(
        functools.partial(pick_kernel, slots, levels),
        shape(devices, height, LANES, dtype=BF16),
        (asked, field),
        (pltpu.VMEM((devices, height, LANES), F32), places, semaphores),
        chip=(0, 1),
        raw=(0,),
    )
    cells = exchange(cells)
    products = (
        pltpu.VMEM((slots, devices * height, LANES), F32),
        pltpu.VMEM((slots, devices * height, LANES), F32),
    )
    returned, misfit, seen_cost = call(
        functools.partial(first_source_kernel, slots),
        (shape(devices, height, LANES), shape(slots, devices, LANES), line_out),
        (cells, interp, sight),
        products,
        chip=(0, 1, 2),
        out_chip=(1, 2),
    )
    returned = exchange(returned)
    push, spread, spread_cost = call(
        functools.partial(first_cycle_kernel, levels, slots),
        (grid, shape(rows, width_y), line_out),
        (field,) + around + (cells,),
        (whole, whole, ring, side, side, strip, semaphores((3, PARTS))),
        chip=(1, 2, 3, 4, 5),
        raw=(0,),
        out_raw=(0, 1),
    )
    gradient, give = call(
        functools.partial(first_owner_kernel, slots, levels),
        (grid, shape(devices, height, LANES)),
        (asked, returned, push, seen_cost, spread_cost),
        (whole, whole, places, semaphores((width_x + 2,))),
        chip=(0, 1),
        raw=(0, 2),
        out_raw=(0,),
    )
    got = exchange(give)
    around = edges_of(gradient)
    returned, step, seen_cost, first_cost = call(
        functools.partial(second_source_kernel, slots, total_cells, total_gates),
        (shape(devices, height, LANES), line_out, line_out, line_out),
        (got, interp, sight, misfit),
        products,
        chip=(0, 1, 2, 3),
        out_chip=(1, 2, 3),
    )
    returned = exchange(returned)
    rest, wind, rest_cost = call(
        functools.partial(second_cycle_kernel, levels, slots),
        (grid, grid, line_out),
        (gradient,) + around + (got, field, push, spread, step),
        (whole, whole, whole, plane, ring, side, side, strip, semaphores((6, PARTS))),
        chip=(1, 2, 3, 4, 5, 9),
        raw=(0, 6, 7, 8),
        out_raw=(0, 1),
        out_chip=(2,),
    )
    gradient, give = call(
        functools.partial(second_owner_kernel, slots, levels),
        (grid, shape(devices, 8, LANES)),
        (asked, returned, rest, seen_cost, rest_cost),
        (whole, places, semaphores((width_x + 2,))),
        chip=(0, 1, 3, 4),
        raw=(0, 2),
        out_chip=(0,),
    )
    sums = exchange(give)
    six_rows = (shape(6, levels, width_y), shape(6, levels, width_y))
    up, down, left, right = call(
        functools.partial(final_edges_kernel, levels), six_rows + edges, (wind, gradient), (side,), chip=(0, 1)
    )
    around = halo(left, right, up, down)
    wind, strain, costs = call(
        functools.partial(final_kernel, levels, total_cells, total_gates),
        (grid, shape(6, rows, width_y), line_out),
        (sums, first_cost, wind, gradient) + around,
        (
            side,
            side,
            pltpu.VMEM((3, rows, width_y), F32),
            pltpu.VMEM((6, rows, width_y), F32),
            semaphores((3, PARTS)),
        ),
        chip=(0, 3, 4, 5, 6, 7),
        raw=(2,),
        out_raw=(0, 1),
        out_chip=(2,),
    )
    return (
        wind.reshape(background.shape),
        strain.reshape(6, width_x, levels, width_y),
        costs[0, :2],
    )


def solution(mesh):
    placed = (
        P(None, "tile", None, "radar"),
        P(("radar", "tile"), None, None),
        P(("radar", "tile"), None, None),
        P(("radar", "tile"), None),
        P(("radar", "tile")),
        P(("radar", "tile"), None),
    )

    return jax.shard_map(
        shards,
        mesh=mesh,
        in_specs=placed,
        out_specs=(P(None, "tile", None, "radar"), P(None, "tile", None, "radar"), P()),
        check_vma=False,
    )
```

time: 145 us -> 134 us (0.924); the launches traced: 144 us -> 132 us
  local copies, waits for them, and re-layouts: 18.2 us -> 3.85 us
  Pallas kernels: 28.7 us -> 37.5 us
  waiting for transfers between devices: 28.6 us -> 22.4 us
    unnamed x46 -> x10, local copies, waits for them, and re-layouts: 16.4 us -> 2.01 us
    pallas_call x12 -> x11, Pallas kernels: 28.7 us -> 37.5 us  [call(): pl.pallas_call(kernel, out_shape=placed[0] if single else placed, in_spec...]
    ppermute x12, waiting for transfers between devices: 17.1 us -> 10 us  [shifted(): return lax.ppermute(x, axis, pairs)]
  transfers between devices with their start and end apart: 17 -> 17, of which waited for: 9 -> 5; matrix products, arithmetic and copies ran while one was open for 2% -> 2% of each run, Pallas kernels for 5% -> 12%
where the time goes in v3:
time: 134 us; the launch traced here: 132 us
  starting transfers between devices  51.1 us (38%)
  Pallas kernels  37.5 us (28%)
  waiting for transfers between devices  22.4 us (17%)
  blocking collectives  13.4 us (10%)
  local copies, waits for them, and re-layouts  3.85 us (3%)
  other arithmetic  2.39 us (2%)
    pallas_call x11, Pallas kernels, call(): pl.pallas_call(kernel, out_shape=placed[0] if single else placed, in_spec...  37.5 us
    ppermute x12, starting transfers between devices, shifted(): return lax.ppermute(x, axis, pairs)  30.4 us
    all_to_all x5, starting transfers between devices, exchange(): return lax.all_to_all(x, AXES, split_axis=0, concat_axis=0, tiled=True)  20.6 us
    all_to_all x1, blocking collectives, exchange(): return lax.all_to_all(x, AXES, split_axis=0, concat_axis=0, tiled=True)  13.4 us
    all_to_all x5, waiting for transfers between devices, exchange(): return lax.all_to_all(x, AXES, split_axis=0, concat_axis=0, tiled=True)  12.4 us
    ppermute x12, waiting for transfers between devices, shifted(): return lax.ppermute(x, axis, pairs)  10 us
  transfers between devices with their start and end apart: 17, of which 5 were waited for; matrix products, arithmetic and copies ran while one was open for 2% of the time, Pallas kernels for 12%

profile of v3, /device:TPU:1, one launch (start us, length us, event | category | flops | bytes accessed | tf_op | source)
XLA Modules:
  0.0 131.7 jit_solution(5645886632572012196)
XLA Ops:
  0.6 0.7 pad.4
  1.3 0.7 broadcast_in_dim.2
  2.0 7.1 %all-to-all-start = ((s32[32,8,128]{2,1,0:T(8,128)}), s32[32,8,128]{2,1,0:T(8,128)S(1)}, u32[]{:S(2)}, u32[]{:S(2)}) async-start(s32[32,8,128]{2,1,0:T(8,128)} %broadcast_in_dim.2), calls=%async_computation | async-start | bytes 262144 | tf_op jit(solution)/shard_map/all_to_all | solution.py:28
  9.0 0.7 compare_convert_fusion
  9.7 0.7 convert.8
  10.4 0.8 convert.9
  11.3 0.1 bitcast_multiply_fusion
  11.4 5.4 %all-to-all-done.asked_hbm = s32[32,8,128]{2,1,0:T(8,128)S(1)} async-done(((s32[32,8,128]{2,1,0:T(8,128)}), s32[32,8,128]{2,1,0:T(8,128)S(1)}, u32[]{:S(2)}, u32[]{:S(2)}) %all-to-all-start) | async-done | bytes 131104 | tf_op jit(solution)/shard_map/all_to_all | solution.py:28
  16.7 1.4 %copy-done = f32[3,16,32,256]{3,2,1,0:T(8,128)S(1)} copy-done((f32[3,16,32,256]{3,2,1,0:T(8,128)S(1)}, f32[3,16,32,256]{3,2,1,0:T(8,128)}, u32[]{:S(2)}) %copy-start) | copy-done | bytes 1572888
  18.1 2.1 %shard_map.85 = bf16[32,8,128]{2,1,0:T(8,128)(2,1)} custom-call(s32[32,8,128]{2,1,0:T(8,128)S(1)} %all-to-all-done.asked_hbm, f32[3,512,256]{2,1,0:T(8,128)S(1)} %bitcast.22), custom_call_target="tpu_custom_call" | custom-call | flops 2000000 | bytes 1048576 | tf_op jit(solution)/shard_map/pallas_call | solution.py:622
  20.2 2.6 %all-to-all-start.1 = ((bf16[32,8,128]{2,1,0:T(8,128)(2,1)}), bf16[32,8,128]{2,1,0:T(8,128)(2,1)S(1)}, u32[]{:S(2)}, u32[]{:S(2)}) async-start(bf16[32,8,128]{2,1,0:T(8,128)(2,1)} %shard_map.85), calls=%async_computation.1 | async-start | bytes 131072 | tf_op jit(solution)/shard_map/all_to_all | solution.py:28
  22.9 0.1 bitcast_multiply_fusion.1
  23.0 7.1 %all-to-all-done.1.cells_ref = bf16[32,8,128]{2,1,0:T(8,128)(2,1)S(1)} async-done(((bf16[32,8,128]{2,1,0:T(8,128)(2,1)}), bf16[32,8,128]{2,1,0:T(8,128)(2,1)S(1)}, u32[]{:S(2)}, u32[]{:S(2)}) %all-to-all-start.1) | async-done | bytes 65568 | tf_op jit(solution)/shard_map/all_to_all | solution.py:28
  30.1 3.4 %shard_map.86 = (f32[32,8,128]{2,1,0:T(8,128)}, f32[2,32,128]{2,1,0:T(8,128)S(1)}, f32[8,128]{1,0:T(8,128)S(1)}) custom-call(bf16[32,8,128]{2,1,0:T(8,128)(2,1)S(1)} %all-to-all-done.1.cells_ref, bf16[64,128,128]{2,1,0:T(8,128)(2,1)S(1)} %copy-done.1, f32[8,32,128]{2,1,0:T(8,128)S(1)} %pad_maximum_fusion.sight_ref), custom_call_target="tpu_custom_call" | custom-call | flops 2000000 | bytes 1048576 | tf_op jit(solution)/shard_map/pallas_call | solution.py:622
  33.4 0.6 copy-done.3
  34.0 2.6 %all-to-all-start.2 = ((f32[32,8,128]{2,1,0:T(8,128)}), f32[32,8,128]{2,1,0:T(8,128)S(1)}, u32[]{:S(2)}, u32[]{:S(2)}) async-start(f32[32,8,128]{2,1,0:T(8,128)} %get-tuple-element.35), calls=%async_computation.2 | async-start | bytes 262144 | tf_op jit(solution)/shard_map/all_to_all | solution.py:28
  36.6 2.6 %shard_map.87 = (f32[8,512]{1,0:T(8,128)}, f32[8,512]{1,0:T(8,128)}, f32[2,32,256]{2,1,0:T(8,128)}, f32[2,32,256]{2,1,0:T(8,128)}) custom-call(f32[3,512,256]{2,1,0:T(8,128)} %bitcast.19), custom_call_target="tpu_custom_call" | custom-call | flops 2000000 | bytes 1048576 | tf_op jit(solution)/shard_map/pallas_call | solution.py:622
  39.2 3.3 %collective-permute-start.2 = (f32[2,32,256]{2,1,0:T(8,128)}, f32[2,32,256]{2,1,0:T(8,128)S(1)}, u32[]{:S(2)}, u32[]{:S(2)}) collective-permute-start(f32[2,32,256]{2,1,0:T(8,128)} %get-tuple-element.38), channel_id=1, source_target_pairs={{0,1},{1,2},{2,3},{3,4},{4,5},{5,6},{6,7},{8,9},{9,10},{10,11},{11... | collective-permute-start | bytes 196616 | tf_op jit(solution)/shard_map/ppermute | solution.py:34
  42.5 1.3 collective-permute-start.3
  43.8 3.7 %collective-permute-start = (f32[8,512]{1,0:T(8,128)}, f32[8,512]{1,0:T(8,128)S(1)}, u32[]{:S(2)}, u32[]{:S(2)}) collective-permute-start(f32[8,512]{1,0:T(8,128)} %get-tuple-element.36), channel_id=1, source_target_pairs={{0,8},{8,16},{16,24},{1,9},{9,17},{17,25},{2,10},{10,18},{18,26},{... | collective-permute-start | bytes 49160 | tf_op jit(solution)/shard_map/ppermute | solution.py:34
  47.5 1.9 %collective-permute-start.1 = (f32[8,512]{1,0:T(8,128)}, f32[8,512]{1,0:T(8,128)S(1)}, u32[]{:S(2)}, u32[]{:S(2)}) collective-permute-start(f32[8,512]{1,0:T(8,128)} %get-tuple-element.37), channel_id=1, source_target_pairs={{8,0},{16,8},{24,16},{9,1},{17,9},{25,17},{10,2},{18,10},{26,18},{... | collective-permute-start | bytes 49160 | tf_op jit(solution)/shard_map/ppermute | solution.py:34
  49.4 3.3 %collective-permute-done.1.right_ref = f32[8,512]{1,0:T(8,128)S(1)} collective-permute-done((f32[8,512]{1,0:T(8,128)}, f32[8,512]{1,0:T(8,128)S(1)}, u32[]{:S(2)}, u32[]{:S(2)}) %collective-permute-start.1) | collective-permute-done | bytes 16416 | tf_op jit(solution)/shard_map/ppermute | solution.py:34
  52.7 0.0 collective-permute-done.2.above_ref
  52.7 4.7 %shard_map.88 = (f32[3,512,256]{2,1,0:T(8,128)}, f32[512,256]{1,0:T(8,128)}, f32[8,128]{1,0:T(8,128)}) custom-call(f32[3,512,256]{2,1,0:T(8,128)} %bitcast.20, f32[8,512]{1,0:T(8,128)S(1)} %collective-permute-done.left_ref, f32[8,512]{1,0:T(8,128)S(1)} %collective-permute-done.1.right_ref, f32[2,32,256]{2,1,0:T(8,128)S(1)} %collective-permute-done.2.above_ref, ...), custom_call_target="tpu_custom_call" | custom-call | flops 2000000 | bytes 1048576 | tf_op jit(solution)/shard_map/pallas_call | solution.py:622
  57.5 4.1 %shard_map.89 = (f32[3,512,256]{2,1,0:T(8,128)}, f32[32,8,128]{2,1,0:T(8,128)}) custom-call(s32[32,8,128]{2,1,0:T(8,128)S(1)} %all-to-all-done.asked_hbm, f32[32,8,128]{2,1,0:T(8,128)S(1)} %all-to-all-done.2.returned_ref, f32[3,512,256]{2,1,0:T(8,128)} %get-tuple-element.40.push_hbm, f32[8,128]{1,0:T(8,128)} %copy-done.3, ...), custom_call_target="tpu_custom_call" | custom-call | flops 2000000 | bytes 1048576 | tf_op jit(solution)/shard_map/pallas_call | solution.py:622
  61.6 13.4 %all_to_all.30.got_ref = f32[32,8,128]{2,1,0:T(8,128)S(1)} all-to-all(f32[32,8,128]{2,1,0:T(8,128)} %get-tuple-element.43), channel_id=1, replica_groups=mesh['radar'=4,'tile'=8] {'radar','tile'}, dimensions={0} | all-to-all | bytes 262144 | tf_op jit(solution)/shard_map/all_to_all | solution.py:28
  75.0 3.4 %shard_map.90 = (f32[32,8,128]{2,1,0:T(8,128)}, f32[8,128]{1,0:T(8,128)S(1)}, f32[8,128]{1,0:T(8,128)S(1)}, f32[8,128]{1,0:T(8,128)S(1)}) custom-call(f32[32,8,128]{2,1,0:T(8,128)S(1)} %all_to_all.30.got_ref, bf16[64,128,128]{2,1,0:T(8,128)(2,1)S(1)} %copy-done.1, f32[8,32,128]{2,1,0:T(8,128)S(1)} %pad_maximum_fusion.sight_ref, ...), custom_call_target="tpu_custom_call" | custom-call | flops 2000000 | bytes 1048576 | tf_op jit(solution)/shard_map/pallas_call | solution.py:622
  78.5 2.6 %all-to-all-start.4 = ((f32[32,8,128]{2,1,0:T(8,128)}), f32[32,8,128]{2,1,0:T(8,128)S(1)}, u32[]{:S(2)}, u32[]{:S(2)}) async-start(f32[32,8,128]{2,1,0:T(8,128)} %get-tuple-element.45), calls=%async_computation.4 | async-start | bytes 262144 | tf_op jit(solution)/shard_map/all_to_all | solution.py:28
  81.1 2.6 %shard_map.91 = (f32[8,512]{1,0:T(8,128)}, f32[8,512]{1,0:T(8,128)}, f32[2,32,256]{2,1,0:T(8,128)}, f32[2,32,256]{2,1,0:T(8,128)}) custom-call(f32[3,512,256]{2,1,0:T(8,128)} %get-tuple-element.46.w_hbm), custom_call_target="tpu_custom_call" | custom-call | flops 2000000 | bytes 1048576 | tf_op jit(solution)/shard_map/pallas_call | solution.py:622
  83.7 3.3 %collective-permute-start.6 = (f32[2,32,256]{2,1,0:T(8,128)}, f32[2,32,256]{2,1,0:T(8,128)S(1)}, u32[]{:S(2)}, u32[]{:S(2)}) collective-permute-start(f32[2,32,256]{2,1,0:T(8,128)} %get-tuple-element.49), channel_id=1, source_target_pairs={{0,1},{1,2},{2,3},{3,4},{4,5},{5,6},{6,7},{8,9},{9,10},{10,11},{11... | collective-permute-start | bytes 196616 | tf_op jit(solution)/shard_map/ppermute | solution.py:34
  87.0 1.3 collective-permute-start.7
  88.3 3.7 %collective-permute-start.4 = (f32[8,512]{1,0:T(8,128)}, f32[8,512]{1,0:T(8,128)S(1)}, u32[]{:S(2)}, u32[]{:S(2)}) collective-permute-start(f32[8,512]{1,0:T(8,128)} %get-tuple-element.47), channel_id=1, source_target_pairs={{0,8},{8,16},{16,24},{1,9},{9,17},{17,25},{2,10},{10,18},{18,26},{... | collective-permute-start | bytes 49160 | tf_op jit(solution)/shard_map/ppermute | solution.py:34
  91.9 1.9 %collective-permute-start.5 = (f32[8,512]{1,0:T(8,128)}, f32[8,512]{1,0:T(8,128)S(1)}, u32[]{:S(2)}, u32[]{:S(2)}) collective-permute-start(f32[8,512]{1,0:T(8,128)} %get-tuple-element.48), channel_id=1, source_target_pairs={{8,0},{16,8},{24,16},{9,1},{17,9},{25,17},{10,2},{18,10},{26,18},{... | collective-permute-start | bytes 49160 | tf_op jit(solution)/shard_map/ppermute | solution.py:34
  93.9 0.0 collective-permute-done.4.left_ref
  93.9 3.3 %collective-permute-done.5.right_ref = f32[8,512]{1,0:T(8,128)S(1)} collective-permute-done((f32[8,512]{1,0:T(8,128)}, f32[8,512]{1,0:T(8,128)S(1)}, u32[]{:S(2)}, u32[]{:S(2)}) %collective-permute-start.5) | collective-permute-done | bytes 16416 | tf_op jit(solution)/shard_map/ppermute | solution.py:34
  97.2 4.6 %shard_map.92 = (f32[3,512,256]{2,1,0:T(8,128)}, f32[3,512,256]{2,1,0:T(8,128)}, f32[8,128]{1,0:T(8,128)S(1)}) custom-call(f32[3,512,256]{2,1,0:T(8,128)} %get-tuple-element.46.w_hbm, f32[8,512]{1,0:T(8,128)S(1)} %collective-permute-done.4.left_ref, f32[8,512]{1,0:T(8,128)S(1)} %collective-permute-done.5.right_ref, ...), custom_call_target="tpu_custom_call" | custom-call | flops 2000000 | bytes 1048576 | tf_op jit(solution)/shard_map/pallas_call | solution.py:622
  101.8 0.0 all-to-all-done.4.returned_ref
  101.8 2.7 %shard_map.93 = (f32[3,512,256]{2,1,0:T(8,128)S(1)}, f32[32,8,128]{2,1,0:T(8,128)}) custom-call(s32[32,8,128]{2,1,0:T(8,128)S(1)} %all-to-all-done.asked_hbm, f32[32,8,128]{2,1,0:T(8,128)S(1)} %all-to-all-done.4.returned_ref, f32[3,512,256]{2,1,0:T(8,128)} %get-tuple-element.53.rest_hbm, f32[8,128]{1,0:T(8,128)S(1)} %get-tuple-element.54.seen_cost_ref, ...), custom_call_target="tpu_custom_call" | custom-call | flops 2000000 | bytes 1048576 | tf_op jit(solution)/shard_map/pallas_call | solution.py:622
  104.5 5.8 %all-to-all-start.5 = ((f32[32,8,128]{2,1,0:T(8,128)}), f32[32,8,128]{2,1,0:T(8,128)S(1)}, u32[]{:S(2)}, u32[]{:S(2)}) async-start(f32[32,8,128]{2,1,0:T(8,128)} %get-tuple-element.56), calls=%async_computation.5 | async-start | bytes 262144 | tf_op jit(solution)/shard_map/all_to_all | solution.py:28
  110.3 1.5 %shard_map.94 = (f32[6,32,256]{2,1,0:T(8,128)}, f32[6,32,256]{2,1,0:T(8,128)}, f32[8,512]{1,0:T(8,128)}, f32[8,512]{1,0:T(8,128)}) custom-call(f32[3,512,256]{2,1,0:T(8,128)S(1)} %copy-done.2, f32[3,512,256]{2,1,0:T(8,128)S(1)} %get-tuple-element.59.gradient_ref), custom_call_target="tpu_custom_call" | custom-call | flops 2000000 | bytes 1048576 | tf_op jit(solution)/shard_map/pallas_call | solution.py:622
  111.8 3.3 %collective-permute-start.10 = (f32[6,32,256]{2,1,0:T(8,128)}, f32[6,32,256]{2,1,0:T(8,128)S(1)}, u32[]{:S(2)}, u32[]{:S(2)}) collective-permute-start(f32[6,32,256]{2,1,0:T(8,128)} %get-tuple-element.62), channel_id=1, source_target_pairs={{0,1},{1,2},{2,3},{3,4},{4,5},{5,6},{6,7},{8,9},{9,10},{10,11},{11... | collective-permute-start | bytes 589832 | tf_op jit(solution)/shard_map/ppermute | solution.py:34
  115.1 1.3 collective-permute-start.11
  116.4 3.7 %collective-permute-start.8 = (f32[8,512]{1,0:T(8,128)}, f32[8,512]{1,0:T(8,128)S(1)}, u32[]{:S(2)}, u32[]{:S(2)}) collective-permute-start(f32[8,512]{1,0:T(8,128)} %get-tuple-element.60), channel_id=1, source_target_pairs={{0,8},{8,16},{16,24},{1,9},{9,17},{17,25},{2,10},{10,18},{18,26},{... | collective-permute-start | bytes 49160 | tf_op jit(solution)/shard_map/ppermute | solution.py:34
  120.0 1.9 %collective-permute-start.9 = (f32[8,512]{1,0:T(8,128)}, f32[8,512]{1,0:T(8,128)S(1)}, u32[]{:S(2)}, u32[]{:S(2)}) collective-permute-start(f32[8,512]{1,0:T(8,128)} %get-tuple-element.61), channel_id=1, source_target_pairs={{8,0},{16,8},{24,16},{9,1},{17,9},{25,17},{10,2},{18,10},{26,18},{... | collective-permute-start | bytes 49160 | tf_op jit(solution)/shard_map/ppermute | solution.py:34
  122.0 0.0 collective-permute-done.8.left_ref
  122.0 3.3 %collective-permute-done.9.right_ref = f32[8,512]{1,0:T(8,128)S(1)} collective-permute-done((f32[8,512]{1,0:T(8,128)}, f32[8,512]{1,0:T(8,128)S(1)}, u32[]{:S(2)}, u32[]{:S(2)}) %collective-permute-start.9) | collective-permute-done | bytes 16416 | tf_op jit(solution)/shard_map/ppermute | solution.py:34
  125.3 5.8 %shard_map.95 = (f32[3,512,256]{2,1,0:T(8,128)}, f32[6,512,256]{2,1,0:T(8,128)}, f32[8,128]{1,0:T(8,128)S(1)}) custom-call(f32[32,8,128]{2,1,0:T(8,128)S(1)} %all-to-all-done.5.sums_ref, f32[8,128]{1,0:T(8,128)} %copy-done.4, f32[3,512,256]{2,1,0:T(8,128)} %get-tuple-element.58.wind_ref.wind_hbm, f32[3,512,256]{2,1,0:T(8,128)S(1)} %get-tuple-element.59.gradient_ref, ...), custom_call_target="tpu_custom_call" | custom-call | flops 2000000 | bytes 1048576 | tf_op jit(solution)/shard_map/pallas_call | solution.py:622
  131.1 0.5 slice_bitcast_fusion
  (17 shorter events, 0.0 us)
Async XLA Ops:
  2.0 14.8 %all-to-all-start = ((s32[32,8,128]{2,1,0:T(8,128)}), s32[32,8,128]{2,1,0:T(8,128)S(1)}, u32[]{:S(2)}, u32[]{:S(2)}) async-start(s32[32,8,128]{2,1,0:T(8,128)} %broadcast_in_dim.2), calls=%async_computation | async-start | bytes 262144 | tf_op jit(solution)/shard_map/all_to_all | solution.py:28
  16.7 1.4 %copy-start = (f32[3,16,32,256]{3,2,1,0:T(8,128)S(1)}, f32[3,16,32,256]{3,2,1,0:T(8,128)}, u32[]{:S(2)}) copy-start(f32[3,16,32,256]{3,2,1,0:T(8,128)} %param.6) | copy-start | bytes 4718596
  18.1 11.9 %copy-start.1 = (bf16[64,128,128]{2,1,0:T(8,128)(2,1)S(1)}, bf16[64,128,128]{2,1,0:T(8,128)(2,1)}, u32[]{:S(2)}) copy-start(bf16[64,128,128]{2,1,0:T(8,128)(2,1)} %weights_ref.3) | copy-start | bytes 6291460
  20.2 9.8 %all-to-all-start.1 = ((bf16[32,8,128]{2,1,0:T(8,128)(2,1)}), bf16[32,8,128]{2,1,0:T(8,128)(2,1)S(1)}, u32[]{:S(2)}, u32[]{:S(2)}) async-start(bf16[32,8,128]{2,1,0:T(8,128)(2,1)} %shard_map.85), calls=%async_computation.1 | async-start | bytes 131072 | tf_op jit(solution)/shard_map/all_to_all | solution.py:28
  33.4 0.6 copy-start.3
  34.0 23.4 %all-to-all-start.2 = ((f32[32,8,128]{2,1,0:T(8,128)}), f32[32,8,128]{2,1,0:T(8,128)S(1)}, u32[]{:S(2)}, u32[]{:S(2)}) async-start(f32[32,8,128]{2,1,0:T(8,128)} %get-tuple-element.35), calls=%async_computation.2 | async-start | bytes 262144 | tf_op jit(solution)/shard_map/all_to_all | solution.py:28
  39.2 13.5 %collective-permute-start.2 = (f32[2,32,256]{2,1,0:T(8,128)}, f32[2,32,256]{2,1,0:T(8,128)S(1)}, u32[]{:S(2)}, u32[]{:S(2)}) collective-permute-start(f32[2,32,256]{2,1,0:T(8,128)} %get-tuple-element.38), channel_id=1, source_target_pairs={{0,1},{1,2},{2,3},{3,4},{4,5},{5,6},{6,7},{8,9},{9,10},{10,11},{11... | collective-permute-start | bytes 196616 | tf_op jit(solution)/shard_map/ppermute | solution.py:34
  42.5 10.2 %collective-permute-start.3 = (f32[2,32,256]{2,1,0:T(8,128)}, f32[2,32,256]{2,1,0:T(8,128)S(1)}, u32[]{:S(2)}, u32[]{:S(2)}) collective-permute-start(f32[2,32,256]{2,1,0:T(8,128)} %get-tuple-element.39), channel_id=1, source_target_pairs={{1,0},{2,1},{3,2},{4,3},{5,4},{6,5},{7,6},{9,8},{10,9},{11,10},{12... | collective-permute-start | bytes 196616 | tf_op jit(solution)/shard_map/ppermute | solution.py:34
  43.8 5.6 %collective-permute-start = (f32[8,512]{1,0:T(8,128)}, f32[8,512]{1,0:T(8,128)S(1)}, u32[]{:S(2)}, u32[]{:S(2)}) collective-permute-start(f32[8,512]{1,0:T(8,128)} %get-tuple-element.36), channel_id=1, source_target_pairs={{0,8},{8,16},{16,24},{1,9},{9,17},{17,25},{2,10},{10,18},{18,26},{... | collective-permute-start | bytes 49160 | tf_op jit(solution)/shard_map/ppermute | solution.py:34
  47.5 5.3 %collective-permute-start.1 = (f32[8,512]{1,0:T(8,128)}, f32[8,512]{1,0:T(8,128)S(1)}, u32[]{:S(2)}, u32[]{:S(2)}) collective-permute-start(f32[8,512]{1,0:T(8,128)} %get-tuple-element.37), channel_id=1, source_target_pairs={{8,0},{16,8},{24,16},{9,1},{17,9},{25,17},{10,2},{18,10},{26,18},{... | collective-permute-start | bytes 49160 | tf_op jit(solution)/shard_map/ppermute | solution.py:34
  78.5 23.3 %copy-start.4 = (f32[8,128]{1,0:T(8,128)}, f32[8,128]{1,0:T(8,128)S(1)}, u32[]{:S(2)}) copy-start(f32[8,128]{1,0:T(8,128)S(1)} %get-tuple-element.57.first_cost_ref) | copy-start | bytes 12292
  78.5 23.3 %all-to-all-start.4 = ((f32[32,8,128]{2,1,0:T(8,128)}), f32[32,8,128]{2,1,0:T(8,128)S(1)}, u32[]{:S(2)}, u32[]{:S(2)}) async-start(f32[32,8,128]{2,1,0:T(8,128)} %get-tuple-element.45), calls=%async_computation.4 | async-start | bytes 262144 | tf_op jit(solution)/shard_map/all_to_all | solution.py:28
  83.7 13.5 %collective-permute-start.6 = (f32[2,32,256]{2,1,0:T(8,128)}, f32[2,32,256]{2,1,0:T(8,128)S(1)}, u32[]{:S(2)}, u32[]{:S(2)}) collective-permute-start(f32[2,32,256]{2,1,0:T(8,128)} %get-tuple-element.49), channel_id=1, source_target_pairs={{0,1},{1,2},{2,3},{3,4},{4,5},{5,6},{6,7},{8,9},{9,10},{10,11},{11... | collective-permute-start | bytes 196616 | tf_op jit(solution)/shard_map/ppermute | solution.py:34
  87.0 10.2 %collective-permute-start.7 = (f32[2,32,256]{2,1,0:T(8,128)}, f32[2,32,256]{2,1,0:T(8,128)S(1)}, u32[]{:S(2)}, u32[]{:S(2)}) collective-permute-start(f32[2,32,256]{2,1,0:T(8,128)} %get-tuple-element.50), channel_id=1, source_target_pairs={{1,0},{2,1},{3,2},{4,3},{5,4},{6,5},{7,6},{9,8},{10,9},{11,10},{12... | collective-permute-start | bytes 196616 | tf_op jit(solution)/shard_map/ppermute | solution.py:34
  88.3 5.6 %collective-permute-start.4 = (f32[8,512]{1,0:T(8,128)}, f32[8,512]{1,0:T(8,128)S(1)}, u32[]{:S(2)}, u32[]{:S(2)}) collective-permute-start(f32[8,512]{1,0:T(8,128)} %get-tuple-element.47), channel_id=1, source_target_pairs={{0,8},{8,16},{16,24},{1,9},{9,17},{17,25},{2,10},{10,18},{18,26},{... | collective-permute-start | bytes 49160 | tf_op jit(solution)/shard_map/ppermute | solution.py:34
  91.9 5.3 %collective-permute-start.5 = (f32[8,512]{1,0:T(8,128)}, f32[8,512]{1,0:T(8,128)S(1)}, u32[]{:S(2)}, u32[]{:S(2)}) collective-permute-start(f32[8,512]{1,0:T(8,128)} %get-tuple-element.48), channel_id=1, source_target_pairs={{8,0},{16,8},{24,16},{9,1},{17,9},{25,17},{10,2},{18,10},{26,18},{... | collective-permute-start | bytes 49160 | tf_op jit(solution)/shard_map/ppermute | solution.py:34
  101.8 8.5 %copy-start.2 = (f32[3,512,256]{2,1,0:T(8,128)S(1)}, f32[3,512,256]{2,1,0:T(8,128)}, u32[]{:S(2)}) copy-start(f32[3,512,256]{2,1,0:T(8,128)} %get-tuple-element.58.wind_ref.wind_hbm) | copy-start | bytes 4718596
  104.5 20.8 %all-to-all-start.5 = ((f32[32,8,128]{2,1,0:T(8,128)}), f32[32,8,128]{2,1,0:T(8,128)S(1)}, u32[]{:S(2)}, u32[]{:S(2)}) async-start(f32[32,8,128]{2,1,0:T(8,128)} %get-tuple-element.56), calls=%async_computation.5 | async-start | bytes 262144 | tf_op jit(solution)/shard_map/all_to_all | solution.py:28
  111.8 13.5 %collective-permute-start.10 = (f32[6,32,256]{2,1,0:T(8,128)}, f32[6,32,256]{2,1,0:T(8,128)S(1)}, u32[]{:S(2)}, u32[]{:S(2)}) collective-permute-start(f32[6,32,256]{2,1,0:T(8,128)} %get-tuple-element.62), channel_id=1, source_target_pairs={{0,1},{1,2},{2,3},{3,4},{4,5},{5,6},{6,7},{8,9},{9,10},{10,11},{11... | collective-permute-start | bytes 589832 | tf_op jit(solution)/shard_map/ppermute | solution.py:34
  115.1 10.2 %collective-permute-start.11 = (f32[6,32,256]{2,1,0:T(8,128)}, f32[6,32,256]{2,1,0:T(8,128)S(1)}, u32[]{:S(2)}, u32[]{:S(2)}) collective-permute-start(f32[6,32,256]{2,1,0:T(8,128)} %get-tuple-element.63), channel_id=1, source_target_pairs={{1,0},{2,1},{3,2},{4,3},{5,4},{6,5},{7,6},{9,8},{10,9},{11,10},{12... | collective-permute-start | bytes 589832 | tf_op jit(solution)/shard_map/ppermute | solution.py:34
  116.4 5.6 %collective-permute-start.8 = (f32[8,512]{1,0:T(8,128)}, f32[8,512]{1,0:T(8,128)S(1)}, u32[]{:S(2)}, u32[]{:S(2)}) collective-permute-start(f32[8,512]{1,0:T(8,128)} %get-tuple-element.60), channel_id=1, source_target_pairs={{0,8},{8,16},{16,24},{1,9},{9,17},{17,25},{2,10},{10,18},{18,26},{... | collective-permute-start | bytes 49160 | tf_op jit(solution)/shard_map/ppermute | solution.py:34
  120.0 5.3 %collective-permute-start.9 = (f32[8,512]{1,0:T(8,128)}, f32[8,512]{1,0:T(8,128)S(1)}, u32[]{:S(2)}, u32[]{:S(2)}) collective-permute-start(f32[8,512]{1,0:T(8,128)} %get-tuple-element.61), channel_id=1, source_target_pairs={{8,0},{16,8},{24,16},{9,1},{17,9},{25,17},{10,2},{18,10},{26,18},{... | collective-permute-start | bytes 49160 | tf_op jit(solution)/shard_map/ppermute | solution.py:34

commit v4 on v3

--- a/solution.py
+++ b/solution.py
@@ -16,6 +16,7 @@
 AXES = ("radar", "tile")
 LANES = 128
 PARTS = 4
+FINAL_PARTS = 8
 F32 = jnp.float32
 BF16 = jnp.bfloat16
 
@@ -180,10 +181,7 @@
     return jnp.where(lane == to, moved, packed)
 
 
-def edges_kernel(levels, w_hbm, left_out, right_out, up_out, down_out, w_ref, scratch, sem):
-    copy = pltpu.make_async_copy(w_hbm, w_ref, sem)
-    copy.start()
-    copy.wait()
+def edges_kernel(levels, w_ref, left_out, right_out, up_out, down_out, scratch):
     rows, width = w_ref.shape[1], w_ref.shape[2]
     lane = iota((levels, LANES), 1)
     last = slice(width - LANES, width)
@@ -342,13 +340,22 @@
     winds.finish()
 
 
-def for_slots(count, body, step=4):
+def for_slots(count, body, step=8):
+    step = min(step, count)
+
     def run(i, carry):
         for j in range(step):
             body(i * step + j)
         return carry
 
     lax.fori_loop(0, count // step, run, 0)
+
+
+def ask_kernel(places_ref, out_ref):
+    line = places_ref[...]
+    if line.shape[1] < out_ref.shape[2]:
+        line = jnp.concatenate([line, jnp.zeros((1, out_ref.shape[2] - line.shape[1]), jnp.int32)], axis=1)
+    out_ref[...] = jnp.broadcast_to(line[None], out_ref.shape)
 
 
 def ask(asked_hbm, asked_ref, sem):
@@ -383,6 +390,12 @@
     out_ref[...] = rows_ref[...].astype(out_ref.dtype)
 
 
+def weights_kernel(source, target, sem):
+    copy = pltpu.make_async_copy(source, target, sem)
+    copy.start()
+    copy.wait()
+
+
 def project(cells_of, weights_ref, proj_ref, sources, slots, height):
     def one(s):
         weights = weights_ref[pl.ds(s * slots, slots)].reshape(slots * LANES, LANES)
@@ -391,7 +404,7 @@
         for p in range(slots):
             proj_ref[p, here, :] = seen[:, p * LANES : (p + 1) * LANES]
 
-    for_slots(sources, one)
+    for_slots(sources, one, 16)
 
 
 def radial(proj_ref, sight_ref, p, sources, height):
@@ -401,50 +414,50 @@
     return total
 
 
-def give_back(misfits, weights_ref, sight_ref, adj_ref, out_ref, sources, slots, height):
+def give_back(misfits, weights_ref, sight_ref, adj_ref, line_ref, out_ref, sources, slots, height):
     adj_ref[...] = jnp.zeros_like(adj_ref)
+    cost = jnp.zeros((sources, LANES), F32)
     for p in range(slots):
+        cost = cost + 0.5 * (misfits[p] * misfits[p])
         for k in range(3):
             adj_ref[p, pl.ds(3 * p + k, sources, stride=height), :] = sight_ref[3 * p + k] * misfits[p]
+    high = cost.astype(BF16).astype(F32)
+    line_ref[...] = jnp.zeros_like(line_ref)
+    line_ref[pl.ds(3 * slots, sources, stride=height), :] = high
+    line_ref[pl.ds(3 * slots + 1, sources, stride=height), :] = cost - high
 
     def one(s):
         weights = weights_ref[pl.ds(s * slots, slots)].reshape(slots * LANES, LANES)
         here = pl.ds(pl.multiple_of(s * height, height), height)
         adjoint = jnp.concatenate([adj_ref[p, here, :] for p in range(slots)], axis=1).astype(BF16)
-        out_ref[s] = lax.dot_general(adjoint, weights, (((1,), (0,)), ((), ())), preferred_element_type=F32)
-
-    for_slots(sources, one)
-
-
-def first_source_kernel(slots, cells_ref, weights_ref, sight_ref, returned_out, misfit_out, cost_out, proj_ref, adj_ref):
+        product = lax.dot_general(adjoint, weights, (((1,), (0,)), ((), ())), preferred_element_type=F32)
+        out_ref[s] = (product + line_ref[here, :]).astype(out_ref.dtype)
+
+    for_slots(sources, one, 16)
+
+
+def first_source_kernel(slots, cells_ref, weights_ref, sight_ref, returned_out, misfit_out, proj_ref, adj_ref, line_ref):
     sources, height = cells_ref.shape[0], cells_ref.shape[1]
     project(lambda s: cells_ref[s].astype(BF16), weights_ref, proj_ref, sources, slots, height)
     misfits = []
-    cost = jnp.zeros((1, LANES), F32)
     for p in range(slots):
         misfit = radial(proj_ref, sight_ref, p, sources, height) - sight_ref[3 * slots + p]
         misfit_out[p] = misfit
-        cost = cost + 0.5 * jnp.sum(misfit * misfit, axis=0, keepdims=True)
         misfits.append(misfit)
-    cost_out[...] = jnp.broadcast_to(cost, cost_out.shape)
-    give_back(misfits, weights_ref, sight_ref, adj_ref, returned_out, sources, slots, height)
-
-
-def second_source_kernel(slots, total_cells, total_gates, got_ref, weights_ref, sight_ref, misfit_ref, returned_out, step_out, cost_out, done_out, proj_ref, adj_ref):
+    give_back(misfits, weights_ref, sight_ref, adj_ref, line_ref, returned_out, sources, slots, height)
+
+
+def second_source_kernel(slots, total_cells, total_gates, got_ref, weights_ref, sight_ref, misfit_ref, returned_out, step_out, cost_out, proj_ref, adj_ref, line_ref):
     sources, height = got_ref.shape[0], got_ref.shape[1]
     project(lambda s: got_ref[s].astype(BF16), weights_ref, proj_ref, sources, slots, height)
     squares, costs = halves(jnp.sum(got_ref[:, 3 * slots, :], axis=0, keepdims=True))
     step = STEP_LENGTH / jnp.sqrt(squares / total_cells + EPSILON)
     step_out[...] = jnp.broadcast_to(step, step_out.shape)
-    done_out[...] = jnp.broadcast_to(costs / total_gates, done_out.shape)
-    misfits = []
-    cost = jnp.zeros((1, LANES), F32)
-    for p in range(slots):
-        misfit = misfit_ref[p] - step * radial(proj_ref, sight_ref, p, sources, height)
-        cost = cost + 0.5 * jnp.sum(misfit * misfit, axis=0, keepdims=True)
-        misfits.append(misfit)
-    cost_out[...] = jnp.broadcast_to(cost, cost_out.shape)
-    give_back(misfits, weights_ref, sight_ref, adj_ref, returned_out, sources, slots, height)
+    cost_out[...] = jnp.broadcast_to(costs / total_gates, cost_out.shape)
+    misfits = [
+        misfit_ref[p] - step * radial(proj_ref, sight_ref, p, sources, height) for p in range(slots)
+    ]
+    give_back(misfits, weights_ref, sight_ref, adj_ref, line_ref, returned_out, sources, slots, height)
 
 
 def scatter_rows(slots, asked_ref, returned_ref, out_ref):
@@ -453,6 +466,7 @@
     place = iota((8, LANES), 0)
 
     def one(s):
+        block = returned_ref[s].astype(F32)
         for p in range(slots):
             row, run = block_at(asked_ref[s, me * slots + p], runs)
             within = lax.rem(row, jnp.int32(8))
@@ -460,7 +474,7 @@
             lanes = pl.ds(pl.multiple_of(run * LANES, LANES), LANES)
             held = [out_ref[k, pl.ds(base, 8), lanes] for k in range(3)]
             for k in range(3):
-                line = returned_ref[s, 3 * p + k : 3 * p + k + 1, :]
+                line = block[3 * p + k : 3 * p + k + 1, :]
                 held[k] = held[k] + jnp.where(place == within, line, 0.0)
             for k in range(3):
                 out_ref[k, pl.ds(base, 8), lanes] = held[k]
@@ -493,12 +507,17 @@
     return sum_rows(total), copies
 
 
-def first_owner_kernel(slots, levels, asked_hbm, returned_ref, push_hbm, seen_cost_ref, spread_cost_ref, gradient_hbm, give_out, push, gradient, asked_ref, sems):
+def seen_cost(returned_ref, slots):
+    cost = returned_ref[:, 3 * slots : 3 * slots + 2, :].astype(F32)
+    return jnp.sum(jnp.sum(cost, axis=0), axis=0, keepdims=True)
+
+
+def first_owner_kernel(slots, levels, asked_hbm, returned_ref, push_hbm, spread_cost_ref, gradient_hbm, give_out, left_out, right_out, up_out, down_out, push, gradient, asked_ref, scratch, sems):
     squares, copies = gather_gradient(
         slots, levels, asked_hbm, asked_ref, returned_ref, push_hbm, push, gradient, gradient_hbm, sems
     )
     sources = give_out.shape[0]
-    sums = paired(squares, seen_cost_ref[0:1, :] + spread_cost_ref[0:1, :])
+    sums = paired(squares, seen_cost(returned_ref, slots) + spread_cost_ref[0:1, :])
     give_out[...] = jnp.zeros_like(give_out)
     give_out[:, 3 * slots, :] = jnp.broadcast_to(sums, (sources, LANES))
     me = own_place()
@@ -518,15 +537,16 @@
         def _():
             give_out[place, 3 * slots + 1 : 3 * slots + 2, :] = line
 
+    edges_kernel(levels, gradient, left_out, right_out, up_out, down_out, scratch)
     for copy in copies:
         copy.wait()
 
 
-def second_owner_kernel(slots, levels, asked_hbm, returned_ref, rest_hbm, seen_cost_ref, rest_cost_ref, gradient_out, give_out, rest, asked_ref, sems):
+def second_owner_kernel(slots, levels, asked_hbm, returned_ref, rest_hbm, rest_cost_ref, gradient_out, give_out, rest, asked_ref, sems):
     squares, _ = gather_gradient(
         slots, levels, asked_hbm, asked_ref, returned_ref, rest_hbm, rest, gradient_out, None, sems
     )
-    sums = paired(squares, seen_cost_ref[0:1, :] + rest_cost_ref[0:1, :])
+    sums = paired(squares, seen_cost(returned_ref, slots) + rest_cost_ref[0:1, :])
     give_out[...] = jnp.broadcast_to(sums, give_out.shape)
 
 
@@ -549,17 +569,17 @@
     right_out[...] = turned[LANES - 8 : LANES]
 
 
-def final_kernel(levels, total_cells, total_gates, sums_ref, first_cost_ref, wind_hbm, gradient_ref, left_ref, right_ref, above_ref, below_ref, wind_out, strain_out, cost_out, left_rows, right_rows, wind, strain, sems):
+def final_kernel(levels, total_cells, total_gates, sums_ref, first_cost_hbm, wind_hbm, gradient_ref, left_ref, right_ref, above_ref, below_ref, wind_out, strain_out, cost_out, left_rows, right_rows, wind, strain, first_cost_ref, sems, cost_sem):
     rows = gradient_ref.shape[1]
     cells = rows // levels
-    winds = Pieces(wind_hbm, wind, sems.at[0], PARTS).start()
-    wind_outs = OutPieces(wind, wind_out, sems.at[1], PARTS)
-    strain_outs = OutPieces(strain, strain_out, sems.at[2], PARTS)
+    winds = Pieces(wind_hbm, wind, sems.at[0], FINAL_PARTS).start()
+    cost_copy = pltpu.make_async_copy(first_cost_hbm, first_cost_ref, cost_sem)
+    cost_copy.start()
+    wind_outs = OutPieces(wind, wind_out, sems.at[1], FINAL_PARTS)
+    strain_outs = OutPieces(strain, strain_out, sems.at[2], FINAL_PARTS)
     squares, cost = halves(jnp.sum(sums_ref[:, 0, :], axis=0, keepdims=True))
-    cost = cost / total_gates
     step = STEP_LENGTH / jnp.sqrt(squares / total_cells + EPSILON)
-    out_lane = iota(cost_out.shape, 1)
-    cost_out[...] = jnp.where(out_lane == 0, first_cost_ref[...], cost)
+    cost_out[1] = (cost / total_gates)[0, 0]
     left_rows[...] = to_rows(left_ref[...])
     right_rows[...] = to_rows(right_ref[...])
 
@@ -597,6 +617,8 @@
         strain[4, here, :] = 0.25 * (xz + zx)
         strain[5, here, :] = 0.25 * (yz + zy)
         strain_outs.filled(here.stop)
+    cost_copy.wait()
+    cost_out[0] = first_cost_ref[0, 0]
     wind_outs.finish()
     strain_outs.finish()
 
@@ -610,15 +632,17 @@
 ANY = pl.BlockSpec(memory_space=pl.ANY)
 
 
-def call(kernel, out_shape, args, scratch=(), scalars=0, raw=(), out_raw=(), chip=(), out_chip=(), flops=2000000, limit=16):
+def call(kernel, out_shape, args, scratch=(), scalars=0, raw=(), out_raw=(), chip=(), out_chip=(), out_smem=(), out_vmem=False, flops=2000000, limit=16):
     single = not isinstance(out_shape, tuple)
     outs = (out_shape,) if single else out_shape
     held = [
         x if i < scalars or i in chip else pltpu.with_memory_space_constraint(x, pltpu.HBM)
         for i, x in enumerate(args)
     ]
-    placed = tuple(o if i in out_chip else pltpu.HBM(o.shape, o.dtype) for i, o in enumerate(outs))
-    specs = tuple(ANY if i in out_raw else VMEM for i in range(len(outs)))
+    placed = tuple(o if i in out_chip or i in out_smem else pltpu.HBM(o.shape, o.dtype) for i, o in enumerate(outs))
+    if out_vmem:
+        placed = tuple(pltpu.VMEM(o.shape, o.dtype) for o in outs)
+    specs = tuple(ANY if i in out_raw else SMEM if i in out_smem else VMEM for i in range(len(outs)))
     return pl.pallas_call(
         kernel,
         out_shape=placed[0] if single else placed,
@@ -643,8 +667,8 @@
     total_gates = float(interp.shape[0] * devices * gate_size)
     field = background.reshape(3, rows, width_y)
     lanes = -(-devices * slots // LANES) * LANES
-    line = jnp.pad(cell_block, (0, lanes - devices * slots))
-    asked = exchange(jnp.broadcast_to(line[None, None, :], (devices, 8, lanes)))
+    asked = call(ask_kernel, shape(devices, 8, lanes, dtype=jnp.int32), (cell_block.reshape(1, -1),), chip=(0,))
+    asked = exchange(asked)
 
     live = (jnp.arange(slots, dtype=jnp.int32)[:, None, None] < sweep_count.reshape(1, devices, 1)).astype(F32)
     sight = beam.reshape(devices, slots, 3, gate_size).transpose(1, 2, 0, 3).astype(F32) * live[:, None]
@@ -671,9 +695,7 @@
         return from_left, from_right, above, below
 
     def edges_of(values):
-        out = call(
-            functools.partial(edges_kernel, levels), edges + row_edges, (values,), (whole, side, semaphores), raw=(0,)
-        )
+        out = call(functools.partial(edges_kernel, levels), edges + row_edges, (values,), (side,), chip=(0,))
         return halo(*out)
 
     around = edges_of(field)
@@ -689,14 +711,16 @@
     products = (
         pltpu.VMEM((slots, devices * height, LANES), F32),
         pltpu.VMEM((slots, devices * height, LANES), F32),
-    )
-    returned, misfit, seen_cost = call(
+        pltpu.VMEM((devices * height, LANES), F32),
+    )
+    weights = call(weights_kernel, shape(*interp.shape, dtype=BF16), (interp,), (semaphores,), raw=(0,), out_vmem=True)
+    returned, misfit = call(
         functools.partial(first_source_kernel, slots),
-        (shape(devices, height, LANES), shape(slots, devices, LANES), line_out),
-        (cells, interp, sight),
+        (shape(devices, height, LANES, dtype=BF16), shape(slots, devices, LANES)),
+        (cells, weights, sight),
         products,
         chip=(0, 1, 2),
-        out_chip=(1, 2),
+        out_chip=(1,),
     )
     returned = exchange(returned)
     push, spread, spread_cost = call(
@@ -707,25 +731,26 @@
         chip=(1, 2, 3, 4, 5),
         raw=(0,),
         out_raw=(0, 1),
-    )
-    gradient, give = call(
+        out_chip=(2,),
+    )
+    gradient, give, *sides = call(
         functools.partial(first_owner_kernel, slots, levels),
-        (grid, shape(devices, height, LANES)),
-        (asked, returned, push, seen_cost, spread_cost),
-        (whole, whole, places, semaphores((width_x + 2,))),
-        chip=(0, 1),
+        (grid, shape(devices, height, LANES)) + edges + row_edges,
+        (asked, returned, push, spread_cost),
+        (whole, whole, places, side, semaphores((width_x + 2,))),
+        chip=(0, 1, 3),
         raw=(0, 2),
         out_raw=(0,),
     )
     got = exchange(give)
-    around = edges_of(gradient)
-    returned, step, seen_cost, first_cost = call(
+    around = halo(*sides)
+    returned, step, first_cost = call(
         functools.partial(second_source_kernel, slots, total_cells, total_gates),
-        (shape(devices, height, LANES), line_out, line_out, line_out),
-        (got, interp, sight, misfit),
+        (shape(devices, height, LANES, dtype=BF16), line_out, line_out),
+        (got, weights, sight, misfit),
         products,
         chip=(0, 1, 2, 3),
-        out_chip=(1, 2, 3),
+        out_chip=(1,),
     )
     returned = exchange(returned)
     rest, wind, rest_cost = call(
@@ -741,9 +766,9 @@
     gradient, give = call(
         functools.partial(second_owner_kernel, slots, levels),
         (grid, shape(devices, 8, LANES)),
-        (asked, returned, rest, seen_cost, rest_cost),
+        (asked, returned, rest, rest_cost),
         (whole, places, semaphores((width_x + 2,))),
-        chip=(0, 1, 3, 4),
+        chip=(0, 1, 3),
         raw=(0, 2),
         out_chip=(0,),
     )
@@ -755,24 +780,26 @@
     around = halo(left, right, up, down)
     wind, strain, costs = call(
         functools.partial(final_kernel, levels, total_cells, total_gates),
-        (grid, shape(6, rows, width_y), line_out),
+        (grid, shape(6, rows, width_y), shape(2)),
         (sums, first_cost, wind, gradient) + around,
         (
             side,
             side,
             pltpu.VMEM((3, rows, width_y), F32),
             pltpu.VMEM((6, rows, width_y), F32),
-            semaphores((3, PARTS)),
+            pltpu.SMEM((8, LANES), F32),
+            semaphores((3, FINAL_PARTS)),
+            semaphores,
         ),
         chip=(0, 3, 4, 5, 6, 7),
-        raw=(2,),
+        raw=(1, 2),
         out_raw=(0, 1),
-        out_chip=(2,),
+        out_smem=(2,),
     )
     return (
         wind.reshape(background.shape),
         strain.reshape(6, width_x, levels, width_y),
-        costs[0, :2],
+        costs,
     )
 
 

time: 134 us -> 126 us (0.940)
  Pallas kernels: 37.5 us -> 31.4 us
  waiting for transfers between devices: 22.4 us -> 19.3 us
    pallas_call x11 -> x12, Pallas kernels: 37.5 us -> 31.4 us  [call(): pl.pallas_call(kernel, out_shape=placed[0] if single else placed, in_spec...]
    unnamed x10 -> x22, local copies, waits for them, and re-layouts: 2.01 us -> 4.99 us
    all_to_all x5, waiting for transfers between devices: 12.4 us -> 9.5 us  [exchange(): return lax.all_to_all(x, AXES, split_axis=0, concat_axis=0, tiled=True)]
  transfers between devices with their start and end apart: 17 -> 17, of which waited for: 5 -> 5; matrix products, arithmetic and copies ran while one was open for 2% -> 2% of each run, Pallas kernels for 12% -> 10%
where the time goes in v4:
time: 126 us; the launch traced here: 124 us
  starting transfers between devices  51.2 us (41%)
  Pallas kernels  31.4 us (25%)
  waiting for transfers between devices  19.3 us (15%)
  blocking collectives  13.4 us (11%)
  local copies, waits for them, and re-layouts  4.99 us (4%)
  other arithmetic  2.39 us (2%)
    pallas_call x12, Pallas kernels, call(): pl.pallas_call(kernel, out_shape=placed[0] if single else placed, in_spec...  31.4 us
    ppermute x12, starting transfers between devices, shifted(): return lax.ppermute(x, axis, pairs)  30.6 us
    all_to_all x5, starting transfers between devices, exchange(): return lax.all_to_all(x, AXES, split_axis=0, concat_axis=0, tiled=True)  20.6 us
    all_to_all x1, blocking collectives, exchange(): return lax.all_to_all(x, AXES, split_axis=0, concat_axis=0, tiled=True)  13.4 us
    ppermute x12, waiting for transfers between devices, shifted(): return lax.ppermute(x, axis, pairs)  9.8 us
    all_to_all x5, waiting for transfers between devices, exchange(): return lax.all_to_all(x, AXES, split_axis=0, concat_axis=0, tiled=True)  9.5 us
    unnamed x22, local copies, waits for them, and re-layouts  4.99 us
  transfers between devices with their start and end apart: 17, of which 5 were waited for; matrix products, arithmetic and copies ran while one was open for 2% of the time, Pallas kernels for 10%

profile of v4, /device:TPU:1, one launch (start us, length us, event | category | flops | bytes accessed | tf_op | source)
XLA Modules:
  0.0 123.7 jit_solution(6852933479822239248)
XLA Ops:
  0.6 0.6 copy-done.6
  1.3 0.7 shard_map.85
  2.0 7.1 %all-to-all-start = ((s32[32,8,128]{2,1,0:T(8,128)}), s32[32,8,128]{2,1,0:T(8,128)S(1)}, u32[]{:S(2)}, u32[]{:S(2)}) async-start(s32[32,8,128]{2,1,0:T(8,128)} %shard_map.85), calls=%async_computation | async-start | bytes 262144 | tf_op jit(solution)/shard_map/all_to_all | solution.py:29
  9.0 0.7 compare_convert_fusion
  9.7 0.7 convert.8
  10.4 0.8 convert.9
  11.3 0.1 bitcast_multiply_fusion
  11.4 5.4 %all-to-all-done.asked_hbm = s32[32,8,128]{2,1,0:T(8,128)S(1)} async-done(((s32[32,8,128]{2,1,0:T(8,128)}), s32[32,8,128]{2,1,0:T(8,128)S(1)}, u32[]{:S(2)}, u32[]{:S(2)}) %all-to-all-start) | async-done | bytes 131104 | tf_op jit(solution)/shard_map/all_to_all | solution.py:29
  16.7 1.4 %copy-done = f32[3,16,32,256]{3,2,1,0:T(8,128)S(1)} copy-done((f32[3,16,32,256]{3,2,1,0:T(8,128)S(1)}, f32[3,16,32,256]{3,2,1,0:T(8,128)}, u32[]{:S(2)}) %copy-start) | copy-done | bytes 1572888
  18.1 2.1 %shard_map.86 = bf16[32,8,128]{2,1,0:T(8,128)(2,1)} custom-call(s32[32,8,128]{2,1,0:T(8,128)S(1)} %all-to-all-done.asked_hbm, f32[3,512,256]{2,1,0:T(8,128)S(1)} %bitcast.20), custom_call_target="tpu_custom_call" | custom-call | flops 2000000 | bytes 1048576 | tf_op jit(solution)/shard_map/pallas_call | solution.py:646
  20.2 2.6 %all-to-all-start.1 = ((bf16[32,8,128]{2,1,0:T(8,128)(2,1)}), bf16[32,8,128]{2,1,0:T(8,128)(2,1)S(1)}, u32[]{:S(2)}, u32[]{:S(2)}) async-start(bf16[32,8,128]{2,1,0:T(8,128)(2,1)} %shard_map.86), calls=%async_computation.1 | async-start | bytes 131072 | tf_op jit(solution)/shard_map/all_to_all | solution.py:29
  22.9 0.1 bitcast_multiply_fusion.1
  22.9 1.6 %shard_map.87.weights_ref = bf16[64,128,128]{2,1,0:T(8,128)(2,1)S(1)} custom-call(bf16[64,128,128]{2,1,0:T(8,128)(2,1)} %source.1), custom_call_target="tpu_custom_call" | custom-call | flops 2000000 | bytes 1048576 | tf_op jit(solution)/shard_map/pallas_call | solution.py:646
  24.5 0.0 copy-start.2
  24.6 1.3 %copy-done.2 = bf16[64,128,128]{2,1,0:T(8,128)(2,1)} copy-done((bf16[64,128,128]{2,1,0:T(8,128)(2,1)}, bf16[64,128,128]{2,1,0:T(8,128)(2,1)S(1)}, u32[]{:S(2)}) %copy-start.2) | copy-done | bytes 2097176
  25.9 4.1 %all-to-all-done.1.cells_ref = bf16[32,8,128]{2,1,0:T(8,128)(2,1)S(1)} async-done(((bf16[32,8,128]{2,1,0:T(8,128)(2,1)}), bf16[32,8,128]{2,1,0:T(8,128)(2,1)S(1)}, u32[]{:S(2)}, u32[]{:S(2)}) %all-to-all-start.1) | async-done | bytes 65568 | tf_op jit(solution)/shard_map/all_to_all | solution.py:29
  30.0 1.6 %copy-done.3 = bf16[64,128,128]{2,1,0:T(8,128)(2,1)S(1)} copy-done((bf16[64,128,128]{2,1,0:T(8,128)(2,1)S(1)}, bf16[64,128,128]{2,1,0:T(8,128)(2,1)}, u32[]{:S(2)}) %copy-start.3) | copy-done | bytes 2097176
  31.6 1.9 %shard_map.88 = (bf16[32,8,128]{2,1,0:T(8,128)(2,1)}, f32[2,32,128]{2,1,0:T(8,128)S(1)}) custom-call(bf16[32,8,128]{2,1,0:T(8,128)(2,1)S(1)} %all-to-all-done.1.cells_ref, bf16[64,128,128]{2,1,0:T(8,128)(2,1)S(1)} %copy-done.3, f32[8,32,128]{2,1,0:T(8,128)S(1)} %pad_maximum_fusion.sight_ref), custom_call_target="tpu_custom_call" | custom-call | flops 2000000 | bytes 1048576 | tf_op jit(solution)/shard_map/pallas_call | solution.py:646
  33.6 2.5 %all-to-all-start.2 = ((bf16[32,8,128]{2,1,0:T(8,128)(2,1)}), bf16[32,8,128]{2,1,0:T(8,128)(2,1)S(1)}, u32[]{:S(2)}, u32[]{:S(2)}) async-start(bf16[32,8,128]{2,1,0:T(8,128)(2,1)} %get-tuple-element.33), calls=%async_computation.2 | async-start | bytes 131072 | tf_op jit(solution)/shard_map/all_to_all | solution.py:29
  36.1 1.2 shard_map.89
  37.3 3.3 %collective-permute-start.2 = (f32[2,32,256]{2,1,0:T(8,128)}, f32[2,32,256]{2,1,0:T(8,128)S(1)}, u32[]{:S(2)}, u32[]{:S(2)}) collective-permute-start(f32[2,32,256]{2,1,0:T(8,128)} %get-tuple-element.36), channel_id=1, source_target_pairs={{0,1},{1,2},{2,3},{3,4},{4,5},{5,6},{6,7},{8,9},{9,10},{10,11},{11... | collective-permute-start | bytes 196616 | tf_op jit(solution)/shard_map/ppermute | solution.py:35
  40.6 1.3 %collective-permute-start.3 = (f32[2,32,256]{2,1,0:T(8,128)}, f32[2,32,256]{2,1,0:T(8,128)S(1)}, u32[]{:S(2)}, u32[]{:S(2)}) collective-permute-start(f32[2,32,256]{2,1,0:T(8,128)} %get-tuple-element.37), channel_id=1, source_target_pairs={{1,0},{2,1},{3,2},{4,3},{5,4},{6,5},{7,6},{9,8},{10,9},{11,10},{12... | collective-permute-start | bytes 196616 | tf_op jit(solution)/shard_map/ppermute | solution.py:35
  41.9 3.7 %collective-permute-start = (f32[8,512]{1,0:T(8,128)}, f32[8,512]{1,0:T(8,128)S(1)}, u32[]{:S(2)}, u32[]{:S(2)}) collective-permute-start(f32[8,512]{1,0:T(8,128)} %get-tuple-element.34), channel_id=1, source_target_pairs={{0,8},{8,16},{16,24},{1,9},{9,17},{17,25},{2,10},{10,18},{18,26},{... | collective-permute-start | bytes 49160 | tf_op jit(solution)/shard_map/ppermute | solution.py:35
  45.5 0.0 copy-start.4
  45.5 2.1 %collective-permute-start.1 = (f32[8,512]{1,0:T(8,128)}, f32[8,512]{1,0:T(8,128)S(1)}, u32[]{:S(2)}, u32[]{:S(2)}) collective-permute-start(f32[8,512]{1,0:T(8,128)} %get-tuple-element.35), channel_id=1, source_target_pairs={{8,0},{16,8},{24,16},{9,1},{17,9},{25,17},{10,2},{18,10},{26,18},{... | collective-permute-start | bytes 49160 | tf_op jit(solution)/shard_map/ppermute | solution.py:35
  47.6 0.0 collective-permute-done.left_ref
  47.6 3.3 %collective-permute-done.1.right_ref = f32[8,512]{1,0:T(8,128)S(1)} collective-permute-done((f32[8,512]{1,0:T(8,128)}, f32[8,512]{1,0:T(8,128)S(1)}, u32[]{:S(2)}, u32[]{:S(2)}) %collective-permute-start.1) | collective-permute-done | bytes 16416 | tf_op jit(solution)/shard_map/ppermute | solution.py:35
  51.0 0.0 collective-permute-done.3.below_ref
  51.0 4.1 %shard_map.90 = (f32[3,512,256]{2,1,0:T(8,128)}, f32[512,256]{1,0:T(8,128)}, f32[8,128]{1,0:T(8,128)S(1)}) custom-call(f32[3,512,256]{2,1,0:T(8,128)} %bitcast.18, f32[8,512]{1,0:T(8,128)S(1)} %collective-permute-done.left_ref, f32[8,512]{1,0:T(8,128)S(1)} %collective-permute-done.1.right_ref, f32[2,32,256]{2,1,0:T(8,128)S(1)} %collective-permute-done.2.above_ref, ...), custom_call_target="tpu_custom_call" | custom-call | flops 2000000 | bytes 1048576 | tf_op jit(solution)/shard_map/pallas_call | solution.py:646
  55.1 3.6 %shard_map.91 = (f32[3,512,256]{2,1,0:T(8,128)}, f32[32,8,128]{2,1,0:T(8,128)}, f32[8,512]{1,0:T(8,128)}, f32[8,512]{1,0:T(8,128)}, f32[2,32,256]{2,1,0:T(8,128)}, /*index=5*/f32[2,32,256]{2,1,0:T(8,128)}) custom-call(s32[32,8,128]{2,1,0:T(8,128)S(1)} %all-to-all-done.asked_hbm, bf16[32,8,128]{2,1,0:T(8,128)(2,1)S(1)} %all-to-all-done.2.returned_ref, ...), custom_call_target="tpu_custom_call" | custom-call | flops 2000000 | bytes 1048576 | tf_op jit(solution)/shard_map/pallas_call | solution.py:646
  58.8 13.4 %all_to_all.30.got_ref = f32[32,8,128]{2,1,0:T(8,128)S(1)} all-to-all(f32[32,8,128]{2,1,0:T(8,128)} %get-tuple-element.40), channel_id=1, replica_groups=mesh['radar'=4,'tile'=8] {'radar','tile'}, dimensions={0} | all-to-all | bytes 262144 | tf_op jit(solution)/shard_map/all_to_all | solution.py:29
  72.2 2.0 %shard_map.92 = (bf16[32,8,128]{2,1,0:T(8,128)(2,1)}, f32[8,128]{1,0:T(8,128)S(1)}, f32[8,128]{1,0:T(8,128)}) custom-call(f32[32,8,128]{2,1,0:T(8,128)S(1)} %all_to_all.30.got_ref, bf16[64,128,128]{2,1,0:T(8,128)(2,1)S(1)} %copy-done.4, f32[8,32,128]{2,1,0:T(8,128)S(1)} %pad_maximum_fusion.sight_ref, f32[2,32,128]{2,1,0:T(8,128)S(1)} %get-tuple-element.41.misfit_ref), custom_call_target="tpu_custom_call" | custom-call | flops 2000000 | bytes 1048576 | tf_op jit(solution)/shard_map/pallas_call | solution.py:646
  74.3 2.6 %all-to-all-start.4 = ((bf16[32,8,128]{2,1,0:T(8,128)(2,1)}), bf16[32,8,128]{2,1,0:T(8,128)(2,1)S(1)}, u32[]{:S(2)}, u32[]{:S(2)}) async-start(bf16[32,8,128]{2,1,0:T(8,128)(2,1)} %get-tuple-element.42), calls=%async_computation.4 | async-start | bytes 131072 | tf_op jit(solution)/shard_map/all_to_all | solution.py:29
  76.9 3.3 %collective-permute-start.6 = (f32[2,32,256]{2,1,0:T(8,128)S(1)}, f32[2,32,256]{2,1,0:T(8,128)S(1)}, u32[]{:S(2)}, u32[]{:S(2)}) collective-permute-start(f32[2,32,256]{2,1,0:T(8,128)S(1)} %copy-done.8), channel_id=1, source_target_pairs={{0,1},{1,2},{2,3},{3,4},{4,5},{5,6},{6,7},{8,9},{9,10},{10,11},{11... | collective-permute-start | bytes 196616 | tf_op jit(solution)/shard_map/ppermute | solution.py:35
  80.2 1.3 %collective-permute-start.7 = (f32[2,32,256]{2,1,0:T(8,128)S(1)}, f32[2,32,256]{2,1,0:T(8,128)S(1)}, u32[]{:S(2)}, u32[]{:S(2)}) collective-permute-start(f32[2,32,256]{2,1,0:T(8,128)S(1)} %copy-done.7), channel_id=1, source_target_pairs={{1,0},{2,1},{3,2},{4,3},{5,4},{6,5},{7,6},{9,8},{10,9},{11,10},{12... | collective-permute-start | bytes 196616 | tf_op jit(solution)/shard_map/ppermute | solution.py:35
  81.5 3.7 %collective-permute-start.4 = (f32[8,512]{1,0:T(8,128)S(1)}, f32[8,512]{1,0:T(8,128)S(1)}, u32[]{:S(2)}, u32[]{:S(2)}) collective-permute-start(f32[8,512]{1,0:T(8,128)S(1)} %copy-done.10), channel_id=1, source_target_pairs={{0,8},{8,16},{16,24},{1,9},{9,17},{17,25},{2,10},{10,18},{18,26},{... | collective-permute-start | bytes 49160 | tf_op jit(solution)/shard_map/ppermute | solution.py:35
  85.2 1.9 %collective-permute-start.5 = (f32[8,512]{1,0:T(8,128)S(1)}, f32[8,512]{1,0:T(8,128)S(1)}, u32[]{:S(2)}, u32[]{:S(2)}) collective-permute-start(f32[8,512]{1,0:T(8,128)S(1)} %copy-done.9), channel_id=1, source_target_pairs={{8,0},{16,8},{24,16},{9,1},{17,9},{25,17},{10,2},{18,10},{26,18},{... | collective-permute-start | bytes 49160 | tf_op jit(solution)/shard_map/ppermute | solution.py:35
  87.1 3.1 %collective-permute-done.5.right_ref = f32[8,512]{1,0:T(8,128)S(1)} collective-permute-done((f32[8,512]{1,0:T(8,128)S(1)}, f32[8,512]{1,0:T(8,128)S(1)}, u32[]{:S(2)}, u32[]{:S(2)}) %collective-permute-start.5) | collective-permute-done | bytes 16416 | tf_op jit(solution)/shard_map/ppermute | solution.py:35
  90.2 4.5 %shard_map.93 = (f32[3,512,256]{2,1,0:T(8,128)}, f32[3,512,256]{2,1,0:T(8,128)}, f32[8,128]{1,0:T(8,128)S(1)}) custom-call(f32[3,512,256]{2,1,0:T(8,128)} %get-tuple-element.43.w_hbm, f32[8,512]{1,0:T(8,128)S(1)} %collective-permute-done.4.left_ref, f32[8,512]{1,0:T(8,128)S(1)} %collective-permute-done.5.right_ref, ...), custom_call_target="tpu_custom_call" | custom-call | flops 2000000 | bytes 1048576 | tf_op jit(solution)/shard_map/pallas_call | solution.py:646
  94.8 2.7 %shard_map.94 = (f32[3,512,256]{2,1,0:T(8,128)S(1)}, f32[32,8,128]{2,1,0:T(8,128)}) custom-call(s32[32,8,128]{2,1,0:T(8,128)S(1)} %all-to-all-done.asked_hbm, bf16[32,8,128]{2,1,0:T(8,128)(2,1)S(1)} %all-to-all-done.4.returned_ref, f32[3,512,256]{2,1,0:T(8,128)} %get-tuple-element.50.rest_hbm, f32[8,128]{1,0:T(8,128)S(1)} %get-tuple-element.51.rest_cost_ref), custom_call_target="tpu_custom_call" | custom-call | flops 2000000 | bytes 1048576 | tf_op jit(solution)/shard_map/pallas_call | solution.py:646
  97.5 5.8 %all-to-all-start.5 = ((f32[32,8,128]{2,1,0:T(8,128)}), f32[32,8,128]{2,1,0:T(8,128)S(1)}, u32[]{:S(2)}, u32[]{:S(2)}) async-start(f32[32,8,128]{2,1,0:T(8,128)} %get-tuple-element.52), calls=%async_computation.5 | async-start | bytes 262144 | tf_op jit(solution)/shard_map/all_to_all | solution.py:29
  103.3 1.5 %shard_map.95 = (f32[6,32,256]{2,1,0:T(8,128)}, f32[6,32,256]{2,1,0:T(8,128)}, f32[8,512]{1,0:T(8,128)}, f32[8,512]{1,0:T(8,128)}) custom-call(f32[3,512,256]{2,1,0:T(8,128)S(1)} %copy-done.5, f32[3,512,256]{2,1,0:T(8,128)S(1)} %get-tuple-element.55.gradient_ref), custom_call_target="tpu_custom_call" | custom-call | flops 2000000 | bytes 1048576 | tf_op jit(solution)/shard_map/pallas_call | solution.py:646
  104.8 3.3 %collective-permute-start.10 = (f32[6,32,256]{2,1,0:T(8,128)}, f32[6,32,256]{2,1,0:T(8,128)S(1)}, u32[]{:S(2)}, u32[]{:S(2)}) collective-permute-start(f32[6,32,256]{2,1,0:T(8,128)} %get-tuple-element.58), channel_id=1, source_target_pairs={{0,1},{1,2},{2,3},{3,4},{4,5},{5,6},{6,7},{8,9},{9,10},{10,11},{11... | collective-permute-start | bytes 589832 | tf_op jit(solution)/shard_map/ppermute | solution.py:35
  108.1 1.3 %collective-permute-start.11 = (f32[6,32,256]{2,1,0:T(8,128)}, f32[6,32,256]{2,1,0:T(8,128)S(1)}, u32[]{:S(2)}, u32[]{:S(2)}) collective-permute-start(f32[6,32,256]{2,1,0:T(8,128)} %get-tuple-element.59), channel_id=1, source_target_pairs={{1,0},{2,1},{3,2},{4,3},{5,4},{6,5},{7,6},{9,8},{10,9},{11,10},{12... | collective-permute-start | bytes 589832 | tf_op jit(solution)/shard_map/ppermute | solution.py:35
  109.4 3.7 %collective-permute-start.8 = (f32[8,512]{1,0:T(8,128)}, f32[8,512]{1,0:T(8,128)S(1)}, u32[]{:S(2)}, u32[]{:S(2)}) collective-permute-start(f32[8,512]{1,0:T(8,128)} %get-tuple-element.56), channel_id=1, source_target_pairs={{0,8},{8,16},{16,24},{1,9},{9,17},{17,25},{2,10},{10,18},{18,26},{... | collective-permute-start | bytes 49160 | tf_op jit(solution)/shard_map/ppermute | solution.py:35
  113.1 1.9 %collective-permute-start.9 = (f32[8,512]{1,0:T(8,128)}, f32[8,512]{1,0:T(8,128)S(1)}, u32[]{:S(2)}, u32[]{:S(2)}) collective-permute-start(f32[8,512]{1,0:T(8,128)} %get-tuple-element.57), channel_id=1, source_target_pairs={{8,0},{16,8},{24,16},{9,1},{17,9},{25,17},{10,2},{18,10},{26,18},{... | collective-permute-start | bytes 49160 | tf_op jit(solution)/shard_map/ppermute | solution.py:35
  115.0 3.3 %collective-permute-done.9.right_ref = f32[8,512]{1,0:T(8,128)S(1)} collective-permute-done((f32[8,512]{1,0:T(8,128)}, f32[8,512]{1,0:T(8,128)S(1)}, u32[]{:S(2)}, u32[]{:S(2)}) %collective-permute-start.9) | collective-permute-done | bytes 16416 | tf_op jit(solution)/shard_map/ppermute | solution.py:35
  118.3 5.4 %shard_map.96 = (f32[3,512,256]{2,1,0:T(8,128)}, f32[6,512,256]{2,1,0:T(8,128)}, f32[2]{0:T(128)}) custom-call(f32[32,8,128]{2,1,0:T(8,128)S(1)} %all-to-all-done.5.sums_ref, f32[8,128]{1,0:T(8,128)} %get-tuple-element.53.first_cost_hbm, f32[3,512,256]{2,1,0:T(8,128)} %get-tuple-element.54.wind_ref.wind_hbm, ...), custom_call_target="tpu_custom_call" | custom-call | flops 2000000 | bytes 1048576 | tf_op jit(solution)/shard_map/pallas_call | solution.py:646
  (27 shorter events, 0.1 us)
Async XLA Ops:
  0.6 0.7 copy-start.6
  2.0 14.8 %all-to-all-start = ((s32[32,8,128]{2,1,0:T(8,128)}), s32[32,8,128]{2,1,0:T(8,128)S(1)}, u32[]{:S(2)}, u32[]{:S(2)}) async-start(s32[32,8,128]{2,1,0:T(8,128)} %shard_map.85), calls=%async_computation | async-start | bytes 262144 | tf_op jit(solution)/shard_map/all_to_all | solution.py:29
  16.7 1.4 %copy-start = (f32[3,16,32,256]{3,2,1,0:T(8,128)S(1)}, f32[3,16,32,256]{3,2,1,0:T(8,128)}, u32[]{:S(2)}) copy-start(f32[3,16,32,256]{3,2,1,0:T(8,128)} %param.6) | copy-start | bytes 4718596
  20.2 9.8 %all-to-all-start.1 = ((bf16[32,8,128]{2,1,0:T(8,128)(2,1)}), bf16[32,8,128]{2,1,0:T(8,128)(2,1)S(1)}, u32[]{:S(2)}, u32[]{:S(2)}) async-start(bf16[32,8,128]{2,1,0:T(8,128)(2,1)} %shard_map.86), calls=%async_computation.1 | async-start | bytes 131072 | tf_op jit(solution)/shard_map/all_to_all | solution.py:29
  24.5 1.3 %copy-start.2 = (bf16[64,128,128]{2,1,0:T(8,128)(2,1)}, bf16[64,128,128]{2,1,0:T(8,128)(2,1)S(1)}, u32[]{:S(2)}) copy-start(bf16[64,128,128]{2,1,0:T(8,128)(2,1)S(1)} %shard_map.87.weights_ref) | copy-start | bytes 6291460
  25.9 10.2 %copy-start.1 = (f32[3,16,32,256]{3,2,1,0:T(8,128)S(1)}, f32[3,16,32,256]{3,2,1,0:T(8,128)}, u32[]{:S(2)}) copy-start(f32[3,16,32,256]{3,2,1,0:T(8,128)} %param.6) | copy-start | bytes 4718596
  30.0 1.6 %copy-start.3 = (bf16[64,128,128]{2,1,0:T(8,128)(2,1)S(1)}, bf16[64,128,128]{2,1,0:T(8,128)(2,1)}, u32[]{:S(2)}) copy-start(bf16[64,128,128]{2,1,0:T(8,128)(2,1)} %copy-done.2) | copy-start | bytes 6291460
  33.6 21.5 %all-to-all-start.2 = ((bf16[32,8,128]{2,1,0:T(8,128)(2,1)}), bf16[32,8,128]{2,1,0:T(8,128)(2,1)S(1)}, u32[]{:S(2)}, u32[]{:S(2)}) async-start(bf16[32,8,128]{2,1,0:T(8,128)(2,1)} %get-tuple-element.33), calls=%async_computation.2 | async-start | bytes 131072 | tf_op jit(solution)/shard_map/all_to_all | solution.py:29
  37.3 13.7 %collective-permute-start.2 = (f32[2,32,256]{2,1,0:T(8,128)}, f32[2,32,256]{2,1,0:T(8,128)S(1)}, u32[]{:S(2)}, u32[]{:S(2)}) collective-permute-start(f32[2,32,256]{2,1,0:T(8,128)} %get-tuple-element.36), channel_id=1, source_target_pairs={{0,1},{1,2},{2,3},{3,4},{4,5},{5,6},{6,7},{8,9},{9,10},{10,11},{11... | collective-permute-start | bytes 196616 | tf_op jit(solution)/shard_map/ppermute | solution.py:35
  40.6 10.4 %collective-permute-start.3 = (f32[2,32,256]{2,1,0:T(8,128)}, f32[2,32,256]{2,1,0:T(8,128)S(1)}, u32[]{:S(2)}, u32[]{:S(2)}) collective-permute-start(f32[2,32,256]{2,1,0:T(8,128)} %get-tuple-element.37), channel_id=1, source_target_pairs={{1,0},{2,1},{3,2},{4,3},{5,4},{6,5},{7,6},{9,8},{10,9},{11,10},{12... | collective-permute-start | bytes 196616 | tf_op jit(solution)/shard_map/ppermute | solution.py:35
  41.9 5.7 %collective-permute-start = (f32[8,512]{1,0:T(8,128)}, f32[8,512]{1,0:T(8,128)S(1)}, u32[]{:S(2)}, u32[]{:S(2)}) collective-permute-start(f32[8,512]{1,0:T(8,128)} %get-tuple-element.34), channel_id=1, source_target_pairs={{0,8},{8,16},{16,24},{1,9},{9,17},{17,25},{2,10},{10,18},{18,26},{... | collective-permute-start | bytes 49160 | tf_op jit(solution)/shard_map/ppermute | solution.py:35
  45.5 26.7 %copy-start.4 = (bf16[64,128,128]{2,1,0:T(8,128)(2,1)S(1)}, bf16[64,128,128]{2,1,0:T(8,128)(2,1)}, u32[]{:S(2)}) copy-start(bf16[64,128,128]{2,1,0:T(8,128)(2,1)} %copy-done.2) | copy-start | bytes 6291460
  45.5 5.4 %collective-permute-start.1 = (f32[8,512]{1,0:T(8,128)}, f32[8,512]{1,0:T(8,128)S(1)}, u32[]{:S(2)}, u32[]{:S(2)}) collective-permute-start(f32[8,512]{1,0:T(8,128)} %get-tuple-element.35), channel_id=1, source_target_pairs={{8,0},{16,8},{24,16},{9,1},{17,9},{25,17},{10,2},{18,10},{26,18},{... | collective-permute-start | bytes 49160 | tf_op jit(solution)/shard_map/ppermute | solution.py:35
  58.8 18.1 %copy-start.8 = (f32[2,32,256]{2,1,0:T(8,128)S(1)}, f32[2,32,256]{2,1,0:T(8,128)}, u32[]{:S(2)}) copy-start(f32[2,32,256]{2,1,0:T(8,128)} %get-tuple-element.46) | copy-start | bytes 196612
  58.8 21.4 %copy-start.7 = (f32[2,32,256]{2,1,0:T(8,128)S(1)}, f32[2,32,256]{2,1,0:T(8,128)}, u32[]{:S(2)}) copy-start(f32[2,32,256]{2,1,0:T(8,128)} %get-tuple-element.47) | copy-start | bytes 196612
  58.8 22.7 %copy-start.10 = (f32[8,512]{1,0:T(8,128)S(1)}, f32[8,512]{1,0:T(8,128)}, u32[]{:S(2)}) copy-start(f32[8,512]{1,0:T(8,128)} %get-tuple-element.44) | copy-start | bytes 49156
  58.8 26.4 %copy-start.9 = (f32[8,512]{1,0:T(8,128)S(1)}, f32[8,512]{1,0:T(8,128)}, u32[]{:S(2)}) copy-start(f32[8,512]{1,0:T(8,128)} %get-tuple-element.45) | copy-start | bytes 49156
  74.3 20.5 %all-to-all-start.4 = ((bf16[32,8,128]{2,1,0:T(8,128)(2,1)}), bf16[32,8,128]{2,1,0:T(8,128)(2,1)S(1)}, u32[]{:S(2)}, u32[]{:S(2)}) async-start(bf16[32,8,128]{2,1,0:T(8,128)(2,1)} %get-tuple-element.42), calls=%async_computation.4 | async-start | bytes 131072 | tf_op jit(solution)/shard_map/all_to_all | solution.py:29
  76.9 13.4 %collective-permute-start.6 = (f32[2,32,256]{2,1,0:T(8,128)S(1)}, f32[2,32,256]{2,1,0:T(8,128)S(1)}, u32[]{:S(2)}, u32[]{:S(2)}) collective-permute-start(f32[2,32,256]{2,1,0:T(8,128)S(1)} %copy-done.8), channel_id=1, source_target_pairs={{0,1},{1,2},{2,3},{3,4},{4,5},{5,6},{6,7},{8,9},{9,10},{10,11},{11... | collective-permute-start | bytes 196616 | tf_op jit(solution)/shard_map/ppermute | solution.py:35
  80.2 10.1 %collective-permute-start.7 = (f32[2,32,256]{2,1,0:T(8,128)S(1)}, f32[2,32,256]{2,1,0:T(8,128)S(1)}, u32[]{:S(2)}, u32[]{:S(2)}) collective-permute-start(f32[2,32,256]{2,1,0:T(8,128)S(1)} %copy-done.7), channel_id=1, source_target_pairs={{1,0},{2,1},{3,2},{4,3},{5,4},{6,5},{7,6},{9,8},{10,9},{11,10},{12... | collective-permute-start | bytes 196616 | tf_op jit(solution)/shard_map/ppermute | solution.py:35
  81.5 5.6 %collective-permute-start.4 = (f32[8,512]{1,0:T(8,128)S(1)}, f32[8,512]{1,0:T(8,128)S(1)}, u32[]{:S(2)}, u32[]{:S(2)}) collective-permute-start(f32[8,512]{1,0:T(8,128)S(1)} %copy-done.10), channel_id=1, source_target_pairs={{0,8},{8,16},{16,24},{1,9},{9,17},{17,25},{2,10},{10,18},{18,26},{... | collective-permute-start | bytes 49160 | tf_op jit(solution)/shard_map/ppermute | solution.py:35
  85.2 5.1 %collective-permute-start.5 = (f32[8,512]{1,0:T(8,128)S(1)}, f32[8,512]{1,0:T(8,128)S(1)}, u32[]{:S(2)}, u32[]{:S(2)}) collective-permute-start(f32[8,512]{1,0:T(8,128)S(1)} %copy-done.9), channel_id=1, source_target_pairs={{8,0},{16,8},{24,16},{9,1},{17,9},{25,17},{10,2},{18,10},{26,18},{... | collective-permute-start | bytes 49160 | tf_op jit(solution)/shard_map/ppermute | solution.py:35
  94.8 8.5 %copy-start.5 = (f32[3,512,256]{2,1,0:T(8,128)S(1)}, f32[3,512,256]{2,1,0:T(8,128)}, u32[]{:S(2)}) copy-start(f32[3,512,256]{2,1,0:T(8,128)} %get-tuple-element.54.wind_ref.wind_hbm) | copy-start | bytes 4718596
  97.5 20.8 %all-to-all-start.5 = ((f32[32,8,128]{2,1,0:T(8,128)}), f32[32,8,128]{2,1,0:T(8,128)S(1)}, u32[]{:S(2)}, u32[]{:S(2)}) async-start(f32[32,8,128]{2,1,0:T(8,128)} %get-tuple-element.52), calls=%async_computation.5 | async-start | bytes 262144 | tf_op jit(solution)/shard_map/all_to_all | solution.py:29
  104.8 13.5 %collective-permute-start.10 = (f32[6,32,256]{2,1,0:T(8,128)}, f32[6,32,256]{2,1,0:T(8,128)S(1)}, u32[]{:S(2)}, u32[]{:S(2)}) collective-permute-start(f32[6,32,256]{2,1,0:T(8,128)} %get-tuple-element.58), channel_id=1, source_target_pairs={{0,1},{1,2},{2,3},{3,4},{4,5},{5,6},{6,7},{8,9},{9,10},{10,11},{11... | collective-permute-start | bytes 589832 | tf_op jit(solution)/shard_map/ppermute | solution.py:35
  108.1 10.2 %collective-permute-start.11 = (f32[6,32,256]{2,1,0:T(8,128)}, f32[6,32,256]{2,1,0:T(8,128)S(1)}, u32[]{:S(2)}, u32[]{:S(2)}) collective-permute-start(f32[6,32,256]{2,1,0:T(8,128)} %get-tuple-element.59), channel_id=1, source_target_pairs={{1,0},{2,1},{3,2},{4,3},{5,4},{6,5},{7,6},{9,8},{10,9},{11,10},{12... | collective-permute-start | bytes 589832 | tf_op jit(solution)/shard_map/ppermute | solution.py:35
  109.4 5.6 %collective-permute-start.8 = (f32[8,512]{1,0:T(8,128)}, f32[8,512]{1,0:T(8,128)S(1)}, u32[]{:S(2)}, u32[]{:S(2)}) collective-permute-start(f32[8,512]{1,0:T(8,128)} %get-tuple-element.56), channel_id=1, source_target_pairs={{0,8},{8,16},{16,24},{1,9},{9,17},{17,25},{2,10},{10,18},{18,26},{... | collective-permute-start | bytes 49160 | tf_op jit(solution)/shard_map/ppermute | solution.py:35
  113.1 5.3 %collective-permute-start.9 = (f32[8,512]{1,0:T(8,128)}, f32[8,512]{1,0:T(8,128)S(1)}, u32[]{:S(2)}, u32[]{:S(2)}) collective-permute-start(f32[8,512]{1,0:T(8,128)} %get-tuple-element.57), channel_id=1, source_target_pairs={{8,0},{16,8},{24,16},{9,1},{17,9},{25,17},{10,2},{18,10},{26,18},{... | collective-permute-start | bytes 49160 | tf_op jit(solution)/shard_map/ppermute | solution.py:35

commit v5 on v4

--- a/solution.py
+++ b/solution.py
@@ -16,12 +16,15 @@
 AXES = ("radar", "tile")
 LANES = 128
 PARTS = 4
+SPLIT = 3
 FINAL_PARTS = 8
 F32 = jnp.float32
 BF16 = jnp.bfloat16
 
-COL_WY, COL_WX, COL_PART = 0, 1, 2
-ROW_WX, ROW_PART = 0, 1
+COL_WY, COL_WX, COL_PART, COL_WZ = 0, 1, 2, 3
+COL_WIND = (COL_WX, COL_WY, COL_WZ)
+ROW_WX, ROW_PART, ROW_WY, ROW_WZ = 0, 1, 2, 3
+ROW_WIND = (ROW_WX, ROW_WY, ROW_WZ)
 CORNERS = ((-1, -1), (-1, 1), (1, -1), (1, 1))
 
 
@@ -181,12 +184,18 @@
     return jnp.where(lane == to, moved, packed)
 
 
-def edges_kernel(levels, w_ref, left_out, right_out, up_out, down_out, scratch):
+def streamed_edges_kernel(levels, w_hbm, left_out, right_out, up_out, down_out, scratch, w_ref, sems):
+    fields = Pieces(w_hbm, w_ref, sems, PARTS).start()
+    edges_kernel(levels, w_ref, left_out, right_out, up_out, down_out, scratch, fields.until)
+
+
+def edges_kernel(levels, w_ref, left_out, right_out, up_out, down_out, scratch, need=lambda row: None):
     rows, width = w_ref.shape[1], w_ref.shape[2]
     lane = iota((levels, LANES), 1)
     last = slice(width - LANES, width)
     for x in range(rows // levels):
         here = slice(x * levels, (x + 1) * levels)
+        need(here.stop)
         packed = jnp.where(lane < LANES // 2, w_ref[1, here, :LANES], w_ref[1, here, last])
         packed = lane_column(packed, lane, w_ref[0, here, :LANES], 0, 2)
         packed = lane_column(packed, lane, w_ref[2, here, :LANES], 0, 3)
@@ -212,6 +221,7 @@
         out[COL_WY : COL_WY + 1, :] = wy
         out[COL_WX : COL_WX + 1, :] = wx
         out[COL_PART : COL_PART + 1, :] = 0.5 * (inner + partial(wx, wz))
+        out[COL_WZ : COL_WZ + 1, :] = wz
     for out, first in ((up_out, 0), (down_out, rows - levels)):
         here = slice(first, first + levels)
         part = diff_levels(w_ref[2, here, :], levels) + diff_columns(w_ref[1, here, :], 0.0, 0.0)
@@ -221,6 +231,8 @@
             part = part + w_ref[0, levels : 2 * levels, :]
         out[ROW_WX] = w_ref[0, here, :]
         out[ROW_PART] = 0.5 * part
+        out[ROW_WY] = w_ref[1, here, :]
+        out[ROW_WZ] = w_ref[2, here, :]
 
 
 def cycle(levels, w_ref, left_ref, right_ref, above_ref, below_ref, corners, ring, left_rows, right_rows, need, take_spread, take_push):
@@ -390,10 +402,27 @@
     out_ref[...] = rows_ref[...].astype(out_ref.dtype)
 
 
-def weights_kernel(source, target, sem):
-    copy = pltpu.make_async_copy(source, target, sem)
-    copy.start()
-    copy.wait()
+def source_kernel(slots, weights_hbm, beam_hbm, observed_hbm, count_hbm, weights_out, sight_out, beam_ref, observed_ref, count_ref, wide_ref, sems):
+    pairs = (
+        (count_hbm, count_ref),
+        (beam_hbm, beam_ref),
+        (observed_hbm, observed_ref),
+        (weights_hbm, weights_out),
+    )
+    copies = [pltpu.make_async_copy(source, target, sems.at[i]) for i, (source, target) in enumerate(pairs)]
+    for copy in copies:
+        copy.start()
+    sources = sight_out.shape[1]
+    diagonal = iota((sources, sources), 0) == iota((sources, sources), 1)
+    for copy in copies[:3]:
+        copy.wait()
+    counts = jnp.sum(jnp.where(diagonal, count_ref[...].astype(F32), 0.0), axis=1, keepdims=True)
+    for k in range(4):
+        wide_ref[k] = (beam_ref[k] if k < 3 else observed_ref[...]).astype(F32)
+        for p in range(slots):
+            live = jnp.where(counts > p, wide_ref[k, pl.ds(p, sources, stride=slots), :], 0.0)
+            sight_out[3 * p + k if k < 3 else 3 * slots + p] = live
+    copies[3].wait()
 
 
 def project(cells_of, weights_ref, proj_ref, sources, slots, height):
@@ -542,34 +571,45 @@
         copy.wait()
 
 
-def second_owner_kernel(slots, levels, asked_hbm, returned_ref, rest_hbm, rest_cost_ref, gradient_out, give_out, rest, asked_ref, sems):
+def second_owner_kernel(slots, levels, asked_hbm, returned_ref, rest_hbm, rest_cost_ref, gradient_out, give_out, up_out, down_out, rest, asked_ref, scratch, give_ref, sems):
+    rows, width = gradient_out.shape[1], gradient_out.shape[2]
     squares, _ = gather_gradient(
         slots, levels, asked_hbm, asked_ref, returned_ref, rest_hbm, rest, gradient_out, None, sems
     )
     sums = paired(squares, seen_cost(returned_ref, slots) + rest_cost_ref[0:1, :])
-    give_out[...] = jnp.broadcast_to(sums, give_out.shape)
-
-
-def final_edges_kernel(levels, wind_ref, gradient_ref, up_out, down_out, left_out, right_out, scratch):
-    rows, width = wind_ref.shape[1], wind_ref.shape[2]
-    fields = [(wind_ref, k) for k in range(3)] + [(gradient_ref, k) for k in range(3)]
-    for f, (ref, k) in enumerate(fields):
-        up_out[f] = ref[k, 0:levels, :]
-        down_out[f] = ref[k, rows - levels : rows, :]
+    give_ref[...] = jnp.zeros_like(give_ref)
+    for i in range(SPLIT):
+        part = sums.astype(BF16).astype(F32)
+        give_ref[:, i, :] = jnp.broadcast_to(part, (give_ref.shape[0], LANES))
+        sums = sums - part
+    for k in range(3):
+        up_out[k] = gradient_out[k, 0:levels, :].astype(BF16)
+        down_out[k] = gradient_out[k, rows - levels : rows, :].astype(BF16)
     lane = iota((levels, LANES), 1)
     for x in range(rows // levels):
         here = slice(x * levels, (x + 1) * levels)
         packed = jnp.zeros((levels, LANES), F32)
-        for f, (ref, k) in enumerate(fields):
-            packed = lane_column(packed, lane, ref[k, here, :LANES], 0, f)
-            packed = lane_column(packed, lane, ref[k, here, width - LANES :], LANES - 1, LANES - 8 + f)
+        for k in range(3):
+            packed = lane_column(packed, lane, gradient_out[k, here, :LANES], 0, k)
+            packed = lane_column(packed, lane, gradient_out[k, here, width - LANES :], LANES - 1, LANES - 8 + k)
         scratch[here, :] = packed
     turned = scratch[...].T
-    left_out[...] = turned[0:8]
-    right_out[...] = turned[LANES - 8 : LANES]
-
-
-def final_kernel(levels, total_cells, total_gates, sums_ref, first_cost_hbm, wind_hbm, gradient_ref, left_ref, right_ref, above_ref, below_ref, wind_out, strain_out, cost_out, left_rows, right_rows, wind, strain, first_cost_ref, sems, cost_sem):
+    lines = rows // LANES
+    for along_radar, first in ((-1, 0), (1, LANES - 8)):
+        exists, place = neighbour(0, along_radar)
+
+        @pl.when(exists)
+        def _():
+            for k in range(3):
+                for q in range(lines):
+                    row = SPLIT + k * lines + q
+                    piece = turned[first + k : first + k + 1, q * LANES : (q + 1) * LANES]
+                    give_ref[place, row : row + 1, :] = piece
+
+    give_out[...] = give_ref[...].astype(BF16)
+
+
+def final_kernel(levels, total_cells, total_gates, sums_ref, first_cost_hbm, step_ref, wind_hbm, gradient_ref, left_0, right_0, above_0, below_0, left_1, right_1, above_1, below_1, above_ref, below_ref, wind_out, strain_out, cost_out, left_rows, right_rows, wind, strain, first_cost_ref, sems, cost_sem):
     rows = gradient_ref.shape[1]
     cells = rows // levels
     winds = Pieces(wind_hbm, wind, sems.at[0], FINAL_PARTS).start()
@@ -577,11 +617,21 @@
     cost_copy.start()
     wind_outs = OutPieces(wind, wind_out, sems.at[1], FINAL_PARTS)
     strain_outs = OutPieces(strain, strain_out, sems.at[2], FINAL_PARTS)
-    squares, cost = halves(jnp.sum(sums_ref[:, 0, :], axis=0, keepdims=True))
+    squares, cost = halves(jnp.sum(jnp.sum(sums_ref[:, 0:SPLIT, :].astype(F32), axis=0), axis=0, keepdims=True))
     step = STEP_LENGTH / jnp.sqrt(squares / total_cells + EPSILON)
     cost_out[1] = (cost / total_gates)[0, 0]
-    left_rows[...] = to_rows(left_ref[...])
-    right_rows[...] = to_rows(right_ref[...])
+    first_step = step_ref[0:1, 0:1]
+    lines = rows // LANES
+    for along_radar, out, background, bent in ((-1, left_rows, left_0, left_1), (1, right_rows, right_0, right_1)):
+        exists, place = neighbour(0, along_radar)
+        columns = []
+        block = sums_ref[pl.ds(place, 1)].reshape(sums_ref.shape[1:]).astype(F32)
+        for k in range(3):
+            at = slice(COL_WIND[k], COL_WIND[k] + 1)
+            sent = [block[SPLIT + k * lines + q : SPLIT + 1 + k * lines + q] for q in range(lines)]
+            sent = jnp.where(exists, jnp.concatenate(sent, axis=1), 0.0)
+            columns.append(background[at, :] - first_step * bent[at, :] - step * sent)
+        out[...] = to_rows(jnp.concatenate(columns + [jnp.zeros((5, rows), F32)], axis=0))
 
     def settle(x):
         here = slice(x * levels, (x + 1) * levels)
@@ -601,13 +651,13 @@
             if x + 1 < cells:
                 after = wind[k, (x + 1) * levels : (x + 2) * levels, :]
             else:
-                after = below_ref[k] - step * below_ref[3 + k]
+                after = below_0[ROW_WIND[k]] - first_step * below_1[ROW_WIND[k]] - step * below_ref[k].astype(F32)
             if x > 0:
                 before = wind[k, (x - 1) * levels : x * levels, :]
             else:
-                before = above_ref[k] - step * above_ref[3 + k]
-            left = left_rows[here, k : k + 1] - step * left_rows[here, 3 + k : 4 + k]
-            right = right_rows[here, k : k + 1] - step * right_rows[here, 3 + k : 4 + k]
+                before = above_0[ROW_WIND[k]] - first_step * above_1[ROW_WIND[k]] - step * above_ref[k].astype(F32)
+            left = left_rows[here, k : k + 1]
+            right = right_rows[here, k : k + 1]
             along.append((after - before, diff_columns(value, left, right), diff_levels(value, levels)))
         (xx, xy, xz), (yx, yy, yz), (zx, zy, zz) = along
         strain[0, here, :] = 0.5 * xx
@@ -667,16 +717,11 @@
     total_gates = float(interp.shape[0] * devices * gate_size)
     field = background.reshape(3, rows, width_y)
     lanes = -(-devices * slots // LANES) * LANES
-    asked = call(ask_kernel, shape(devices, 8, lanes, dtype=jnp.int32), (cell_block.reshape(1, -1),), chip=(0,))
+    asked = call(ask_kernel, shape(devices, 1, lanes, dtype=jnp.int32), (cell_block.reshape(1, -1),), chip=(0,))
     asked = exchange(asked)
 
-    live = (jnp.arange(slots, dtype=jnp.int32)[:, None, None] < sweep_count.reshape(1, devices, 1)).astype(F32)
-    sight = beam.reshape(devices, slots, 3, gate_size).transpose(1, 2, 0, 3).astype(F32) * live[:, None]
-    seen = observed.reshape(devices, slots, gate_size).transpose(1, 0, 2).astype(F32) * live
-    sight = jnp.concatenate([sight.reshape(3 * slots, devices, gate_size), seen], axis=0)
-
     edges = (shape(8, rows), shape(8, rows))
-    row_edges = (shape(2, levels, width_y), shape(2, levels, width_y))
+    row_edges = (shape(4, levels, width_y), shape(4, levels, width_y))
     grid = shape(3, rows, width_y)
     line_out = shape(8, LANES)
     side = pltpu.VMEM((rows, LANES), F32)
@@ -695,10 +740,17 @@
         return from_left, from_right, above, below
 
     def edges_of(values):
-        out = call(functools.partial(edges_kernel, levels), edges + row_edges, (values,), (side,), chip=(0,))
+        out = call(
+            functools.partial(streamed_edges_kernel, levels),
+            edges + row_edges,
+            (values,),
+            (side, whole, semaphores((PARTS,))),
+            raw=(0,),
+        )
         return halo(*out)
 
     around = edges_of(field)
+    around_0 = around
     cells = call(
         functools.partial(pick_kernel, slots, levels),
         shape(devices, height, LANES, dtype=BF16),
@@ -713,7 +765,20 @@
         pltpu.VMEM((slots, devices * height, LANES), F32),
         pltpu.VMEM((devices * height, LANES), F32),
     )
-    weights = call(weights_kernel, shape(*interp.shape, dtype=BF16), (interp,), (semaphores,), raw=(0,), out_vmem=True)
+    weights, sight = call(
+        functools.partial(source_kernel, slots),
+        (shape(*interp.shape, dtype=BF16), shape(4 * slots, devices, gate_size)),
+        (interp, beam.transpose(1, 0, 2), observed, sweep_count),
+        (
+            pltpu.VMEM((3,) + observed.shape, BF16),
+            pltpu.VMEM(observed.shape, BF16),
+            pltpu.VMEM(sweep_count.shape, jnp.int32),
+            pltpu.VMEM((4,) + observed.shape, F32),
+            semaphores((4,)),
+        ),
+        raw=(0, 1, 2, 3),
+        out_vmem=True,
+    )
     returned, misfit = call(
         functools.partial(first_source_kernel, slots),
         (shape(devices, height, LANES, dtype=BF16), shape(slots, devices, LANES)),
@@ -744,6 +809,7 @@
     )
     got = exchange(give)
     around = halo(*sides)
+    around_1 = around
     returned, step, first_cost = call(
         functools.partial(second_source_kernel, slots, total_cells, total_gates),
         (shape(devices, height, LANES, dtype=BF16), line_out, line_out),
@@ -763,25 +829,24 @@
         out_raw=(0, 1),
         out_chip=(2,),
     )
-    gradient, give = call(
+    last_rows = (shape(3, levels, width_y, dtype=BF16), shape(3, levels, width_y, dtype=BF16))
+    sent = -(-(SPLIT + 3 * rows // LANES) // 8) * 8
+    gradient, give, up, down = call(
         functools.partial(second_owner_kernel, slots, levels),
-        (grid, shape(devices, 8, LANES)),
+        (grid, shape(devices, sent, LANES, dtype=BF16)) + last_rows,
         (asked, returned, rest, rest_cost),
-        (whole, places, semaphores((width_x + 2,))),
+        (whole, places, side, pltpu.VMEM((devices, sent, LANES), F32), semaphores((width_x + 2,))),
         chip=(0, 1, 3),
         raw=(0, 2),
         out_chip=(0,),
     )
     sums = exchange(give)
-    six_rows = (shape(6, levels, width_y), shape(6, levels, width_y))
-    up, down, left, right = call(
-        functools.partial(final_edges_kernel, levels), six_rows + edges, (wind, gradient), (side,), chip=(0, 1)
-    )
-    around = halo(left, right, up, down)
+    above = shifted(down, "tile", 1)
+    below = shifted(up, "tile", -1)
     wind, strain, costs = call(
         functools.partial(final_kernel, levels, total_cells, total_gates),
         (grid, shape(6, rows, width_y), shape(2)),
-        (sums, first_cost, wind, gradient) + around,
+        (sums, first_cost, step, wind, gradient) + around_0 + around_1 + (above, below),
         (
             side,
             side,
@@ -791,8 +856,8 @@
             semaphores((3, FINAL_PARTS)),
             semaphores,
         ),
-        chip=(0, 3, 4, 5, 6, 7),
-        raw=(1, 2),
+        chip=(0, 4, 13, 14),
+        raw=(1, 3),
         out_raw=(0, 1),
         out_smem=(2,),
     )

time: 126 us -> 112 us (0.89)
  the two profiles are of different devices: /device:TPU:1 before, /device:TPU:0 now
where the time goes in v5:
time: 112 us; the launch traced here: 111 us
  starting transfers between devices  48.4 us (43%)
  Pallas kernels  31.8 us (28%)
  blocking collectives  14.4 us (13%)
  waiting for transfers between devices  13.5 us (12%)
  local copies, waits for them, and re-layouts  2.11 us (2%)
    pallas_call x11, Pallas kernels, call(): pl.pallas_call(kernel, out_shape=placed[0] if single else placed, in_spec...  31.8 us
    all_to_all x5, starting transfers between devices, exchange(): return lax.all_to_all(x, AXES, split_axis=0, concat_axis=0, tiled=True)  26.7 us
    ppermute x10, starting transfers between devices, shifted(): return lax.ppermute(x, axis, pairs)  21.7 us
    all_to_all x1, blocking collectives, exchange(): return lax.all_to_all(x, AXES, split_axis=0, concat_axis=0, tiled=True)  14.4 us
    ppermute x10, waiting for transfers between devices, shifted(): return lax.ppermute(x, axis, pairs)  10.7 us
    all_to_all x5, waiting for transfers between devices, exchange(): return lax.all_to_all(x, AXES, split_axis=0, concat_axis=0, tiled=True)  2.83 us
  transfers between devices with their start and end apart: 15, of which 5 were waited for; matrix products, arithmetic and copies ran while one was open for 0% of the time, Pallas kernels for 15%

profile of v5, /device:TPU:0, one launch (start us, length us, event | category | flops | bytes accessed | tf_op | source)
XLA Modules:
  0.0 111.3 jit_solution(780377796639364017)
XLA Ops:
  0.6 0.6 copy-done.10
  1.3 0.6 shard_map.85
  1.9 14.4 %all_to_all.30.asked_hbm = s32[32,1,128]{2,1,0:T(1,128)S(1)} all-to-all(s32[32,1,128]{2,1,0:T(1,128)} %shard_map.85), channel_id=1, replica_groups=mesh['radar'=4,'tile'=8] {'radar','tile'}, dimensions={0} | all-to-all | bytes 32768 | tf_op jit(solution)/shard_map/all_to_all | solution.py:32
  16.3 1.4 %copy-done = f32[3,16,32,256]{3,2,1,0:T(8,128)S(1)} copy-done((f32[3,16,32,256]{3,2,1,0:T(8,128)S(1)}, f32[3,16,32,256]{3,2,1,0:T(8,128)}, u32[]{:S(2)}) %copy-start) | copy-done | bytes 1572888
  17.7 2.0 %shard_map.86 = bf16[32,8,128]{2,1,0:T(8,128)(2,1)} custom-call(s32[32,1,128]{2,1,0:T(1,128)S(1)} %all_to_all.30.asked_hbm, f32[3,512,256]{2,1,0:T(8,128)S(1)} %bitcast.8), custom_call_target="tpu_custom_call" | custom-call | flops 2000000 | bytes 1048576 | tf_op jit(solution)/shard_map/pallas_call | solution.py:696
  19.7 2.6 %all-to-all-start.1 = ((bf16[32,8,128]{2,1,0:T(8,128)(2,1)}), bf16[32,8,128]{2,1,0:T(8,128)(2,1)S(1)}, u32[]{:S(2)}, u32[]{:S(2)}) async-start(bf16[32,8,128]{2,1,0:T(8,128)(2,1)} %shard_map.86), calls=%async_computation.1 | async-start | bytes 131072 | tf_op jit(solution)/shard_map/all_to_all | solution.py:32
  22.3 2.5 %shard_map.89 = (f32[8,512]{1,0:T(8,128)}, f32[8,512]{1,0:T(8,128)}, f32[4,32,256]{2,1,0:T(8,128)}, f32[4,32,256]{2,1,0:T(8,128)}) custom-call(f32[3,512,256]{2,1,0:T(8,128)} %bitcast.5), custom_call_target="tpu_custom_call" | custom-call | flops 2000000 | bytes 1048576 | tf_op jit(solution)/shard_map/pallas_call | solution.py:696
  24.8 3.6 %collective-permute-start.2 = (f32[4,32,256]{2,1,0:T(8,128)}, f32[4,32,256]{2,1,0:T(8,128)S(1)}, u32[]{:S(2)}, u32[]{:S(2)}) collective-permute-start(f32[4,32,256]{2,1,0:T(8,128)} %get-tuple-element.38), channel_id=1, source_target_pairs={{0,1},{1,2},{2,3},{3,4},{4,5},{5,6},{6,7},{8,9},{9,10},{10,11},{11... | collective-permute-start | bytes 393224 | tf_op jit(solution)/shard_map/ppermute | solution.py:38
  28.3 1.3 %collective-permute-start.3 = (f32[4,32,256]{2,1,0:T(8,128)}, f32[4,32,256]{2,1,0:T(8,128)S(1)}, u32[]{:S(2)}, u32[]{:S(2)}) collective-permute-start(f32[4,32,256]{2,1,0:T(8,128)} %get-tuple-element.39), channel_id=1, source_target_pairs={{1,0},{2,1},{3,2},{4,3},{5,4},{6,5},{7,6},{9,8},{10,9},{11,10},{12... | collective-permute-start | bytes 393224 | tf_op jit(solution)/shard_map/ppermute | solution.py:38
  29.6 1.7 %shard_map.87 = (bf16[64,128,128]{2,1,0:T(8,128)(2,1)S(1)}, f32[8,32,128]{2,1,0:T(8,128)S(1)}) custom-call(bf16[64,128,128]{2,1,0:T(8,128)(2,1)} %weights_hbm.1, bf16[3,64,128]{2,1,0:T(8,128)(2,1)} %bitcast.10, bf16[64,128]{1,0:T(8,128)(2,1)} %observed_hbm.1, s32[1,32]{1,0:T(1,128)} %count_hbm.1), custom_call_target="tpu_custom_call" | custom-call | flops 2000000 | bytes 1048576 | tf_op jit(solution)/shard_map/pallas_call | solution.py:696
  31.3 0.0 copy-start.14
  31.4 0.0 copy-start.13
  31.4 0.0 all-to-all-done.1.cells_ref
  31.4 1.9 %shard_map.88 = (bf16[32,8,128]{2,1,0:T(8,128)(2,1)}, f32[2,32,128]{2,1,0:T(8,128)S(1)}) custom-call(bf16[32,8,128]{2,1,0:T(8,128)(2,1)S(1)} %all-to-all-done.1.cells_ref, bf16[64,128,128]{2,1,0:T(8,128)(2,1)S(1)} %get-tuple-element.33.weights_ref, f32[8,32,128]{2,1,0:T(8,128)S(1)} %get-tuple-element.34.sight_ref), custom_call_target="tpu_custom_call" | custom-call | flops 2000000 | bytes 1048576 | tf_op jit(solution)/shard_map/pallas_call | solution.py:696
  33.3 6.8 %all-to-all-start.2 = ((bf16[32,8,128]{2,1,0:T(8,128)(2,1)}), bf16[32,8,128]{2,1,0:T(8,128)(2,1)S(1)}, u32[]{:S(2)}, u32[]{:S(2)}) async-start(bf16[32,8,128]{2,1,0:T(8,128)(2,1)} %get-tuple-element.35), calls=%async_computation.2 | async-start | bytes 131072 | tf_op jit(solution)/shard_map/all_to_all | solution.py:32
  40.2 2.2 %collective-permute-start = (f32[8,512]{1,0:T(8,128)S(1)}, f32[8,512]{1,0:T(8,128)S(1)}, u32[]{:S(2)}, u32[]{:S(2)}) collective-permute-start(f32[8,512]{1,0:T(8,128)S(1)} %copy-done.14), channel_id=1, source_target_pairs={{0,8},{8,16},{16,24},{1,9},{9,17},{17,25},{2,10},{10,18},{18,26},{... | collective-permute-start | bytes 49160 | tf_op jit(solution)/shard_map/ppermute | solution.py:38
  42.3 1.3 %collective-permute-start.1 = (f32[8,512]{1,0:T(8,128)S(1)}, f32[8,512]{1,0:T(8,128)S(1)}, u32[]{:S(2)}, u32[]{:S(2)}) collective-permute-start(f32[8,512]{1,0:T(8,128)S(1)} %copy-done.13), channel_id=1, source_target_pairs={{8,0},{16,8},{24,16},{9,1},{17,9},{25,17},{10,2},{18,10},{26,18},{... | collective-permute-start | bytes 49160 | tf_op jit(solution)/shard_map/ppermute | solution.py:38
  43.6 0.0 collective-permute-done.left_ref.left_0
  43.6 2.9 %collective-permute-done.1.right_ref.right_0 = f32[8,512]{1,0:T(8,128)S(1)} collective-permute-done((f32[8,512]{1,0:T(8,128)S(1)}, f32[8,512]{1,0:T(8,128)S(1)}, u32[]{:S(2)}, u32[]{:S(2)}) %collective-permute-start.1) | collective-permute-done | bytes 16416 | tf_op jit(solution)/shard_map/ppermute | solution.py:38
  46.5 0.0 collective-permute-done.2.above_ref.above_0
  46.6 0.0 collective-permute-done.3.below_ref.below_0
  46.6 4.1 %shard_map.90 = (f32[3,512,256]{2,1,0:T(8,128)}, f32[512,256]{1,0:T(8,128)}, f32[8,128]{1,0:T(8,128)S(1)}) custom-call(f32[3,512,256]{2,1,0:T(8,128)} %bitcast.6, f32[8,512]{1,0:T(8,128)S(1)} %collective-permute-done.left_ref.left_0, f32[8,512]{1,0:T(8,128)S(1)} %collective-permute-done.1.right_ref.right_0, ...), custom_call_target="tpu_custom_call" | custom-call | flops 2000000 | bytes 1048576 | tf_op jit(solution)/shard_map/pallas_call | solution.py:696
  50.7 0.0 all-to-all-done.2.returned_ref
  50.7 3.7 %shard_map.91 = (f32[3,512,256]{2,1,0:T(8,128)}, f32[32,8,128]{2,1,0:T(8,128)}, f32[8,512]{1,0:T(8,128)}, f32[8,512]{1,0:T(8,128)}, f32[4,32,256]{2,1,0:T(8,128)}, /*index=5*/f32[4,32,256]{2,1,0:T(8,128)}) custom-call(s32[32,1,128]{2,1,0:T(1,128)S(1)} %all_to_all.30.asked_hbm, bf16[32,8,128]{2,1,0:T(8,128)(2,1)S(1)} %all-to-all-done.2.returned_ref, ...), custom_call_target="tpu_custom_call" | custom-call | flops 2000000 | bytes 1048576 | tf_op jit(solution)/shard_map/pallas_call | solution.py:696
  54.5 6.7 %all-to-all-start.3 = ((f32[32,8,128]{2,1,0:T(8,128)}), f32[32,8,128]{2,1,0:T(8,128)S(1)}, u32[]{:S(2)}, u32[]{:S(2)}) async-start(f32[32,8,128]{2,1,0:T(8,128)} %get-tuple-element.42), calls=%async_computation.3 | async-start | bytes 262144 | tf_op jit(solution)/shard_map/all_to_all | solution.py:32
  61.2 3.7 %collective-permute-start.6 = (f32[4,32,256]{2,1,0:T(8,128)}, f32[4,32,256]{2,1,0:T(8,128)S(1)}, u32[]{:S(2)}, u32[]{:S(2)}) collective-permute-start(f32[4,32,256]{2,1,0:T(8,128)} %get-tuple-element.48), channel_id=1, source_target_pairs={{0,1},{1,2},{2,3},{3,4},{4,5},{5,6},{6,7},{8,9},{9,10},{10,11},{11... | collective-permute-start | bytes 393224 | tf_op jit(solution)/shard_map/ppermute | solution.py:38
  64.9 1.3 %collective-permute-start.7 = (f32[4,32,256]{2,1,0:T(8,128)}, f32[4,32,256]{2,1,0:T(8,128)S(1)}, u32[]{:S(2)}, u32[]{:S(2)}) collective-permute-start(f32[4,32,256]{2,1,0:T(8,128)} %get-tuple-element.49), channel_id=1, source_target_pairs={{1,0},{2,1},{3,2},{4,3},{5,4},{6,5},{7,6},{9,8},{10,9},{11,10},{12... | collective-permute-start | bytes 393224 | tf_op jit(solution)/shard_map/ppermute | solution.py:38
  66.2 2.8 %all-to-all-done.3.got_ref = f32[32,8,128]{2,1,0:T(8,128)S(1)} async-done(((f32[32,8,128]{2,1,0:T(8,128)}), f32[32,8,128]{2,1,0:T(8,128)S(1)}, u32[]{:S(2)}, u32[]{:S(2)}) %all-to-all-start.3) | async-done | bytes 131104 | tf_op jit(solution)/shard_map/all_to_all | solution.py:32
  69.0 2.0 %shard_map.92 = (bf16[32,8,128]{2,1,0:T(8,128)(2,1)}, f32[8,128]{1,0:T(8,128)S(1)}, f32[8,128]{1,0:T(8,128)}) custom-call(f32[32,8,128]{2,1,0:T(8,128)S(1)} %all-to-all-done.3.got_ref, bf16[64,128,128]{2,1,0:T(8,128)(2,1)S(1)} %get-tuple-element.33.weights_ref, f32[8,32,128]{2,1,0:T(8,128)S(1)} %get-tuple-element.34.sight_ref, ...), custom_call_target="tpu_custom_call" | custom-call | flops 2000000 | bytes 1048576 | tf_op jit(solution)/shard_map/pallas_call | solution.py:696
  71.0 3.9 %all-to-all-start.4 = ((bf16[32,8,128]{2,1,0:T(8,128)(2,1)}), bf16[32,8,128]{2,1,0:T(8,128)(2,1)S(1)}, u32[]{:S(2)}, u32[]{:S(2)}) async-start(bf16[32,8,128]{2,1,0:T(8,128)(2,1)} %get-tuple-element.44), calls=%async_computation.4 | async-start | bytes 131072 | tf_op jit(solution)/shard_map/all_to_all | solution.py:32
  74.9 0.0 copy-done.12
  75.0 2.2 %collective-permute-start.4 = (f32[8,512]{1,0:T(8,128)S(1)}, f32[8,512]{1,0:T(8,128)S(1)}, u32[]{:S(2)}, u32[]{:S(2)}) collective-permute-start(f32[8,512]{1,0:T(8,128)S(1)} %copy-done.12), channel_id=1, source_target_pairs={{0,8},{8,16},{16,24},{1,9},{9,17},{17,25},{2,10},{10,18},{18,26},{... | collective-permute-start | bytes 49160 | tf_op jit(solution)/shard_map/ppermute | solution.py:38
  77.1 1.3 %collective-permute-start.5 = (f32[8,512]{1,0:T(8,128)S(1)}, f32[8,512]{1,0:T(8,128)S(1)}, u32[]{:S(2)}, u32[]{:S(2)}) collective-permute-start(f32[8,512]{1,0:T(8,128)S(1)} %copy-done.11), channel_id=1, source_target_pairs={{8,0},{16,8},{24,16},{9,1},{17,9},{25,17},{10,2},{18,10},{26,18},{... | collective-permute-start | bytes 49160 | tf_op jit(solution)/shard_map/ppermute | solution.py:38
  78.4 0.0 collective-permute-done.4.left_ref.left_1
  78.4 2.9 %collective-permute-done.5.right_ref.right_1 = f32[8,512]{1,0:T(8,128)S(1)} collective-permute-done((f32[8,512]{1,0:T(8,128)S(1)}, f32[8,512]{1,0:T(8,128)S(1)}, u32[]{:S(2)}, u32[]{:S(2)}) %collective-permute-start.5) | collective-permute-done | bytes 16416 | tf_op jit(solution)/shard_map/ppermute | solution.py:38
  81.3 0.0 collective-permute-done.6.above_ref.above_1
  81.4 0.0 collective-permute-done.7.below_ref.below_1
  81.4 0.0 copy-start.2
  81.4 4.6 %shard_map.93 = (f32[3,512,256]{2,1,0:T(8,128)}, f32[3,512,256]{2,1,0:T(8,128)}, f32[8,128]{1,0:T(8,128)S(1)}) custom-call(f32[3,512,256]{2,1,0:T(8,128)} %get-tuple-element.45.w_hbm, f32[8,512]{1,0:T(8,128)S(1)} %collective-permute-done.4.left_ref.left_1, f32[8,512]{1,0:T(8,128)S(1)} %collective-permute-done.5.right_ref.right_1, ...), custom_call_target="tpu_custom_call" | custom-call | flops 2000000 | bytes 1048576 | tf_op jit(solution)/shard_map/pallas_call | solution.py:696
  86.0 0.0 all-to-all-done.4.returned_ref
  86.1 2.9 %shard_map.94 = (f32[3,512,256]{2,1,0:T(8,128)S(1)}, bf16[32,16,128]{2,1,0:T(8,128)(2,1)}, bf16[3,32,256]{2,1,0:T(8,128)(2,1)}, bf16[3,32,256]{2,1,0:T(8,128)(2,1)}) custom-call(s32[32,1,128]{2,1,0:T(1,128)S(1)} %all_to_all.30.asked_hbm, bf16[32,8,128]{2,1,0:T(8,128)(2,1)S(1)} %all-to-all-done.4.returned_ref, f32[3,512,256]{2,1,0:T(8,128)} %get-tuple-element.52.rest_hbm, ...), custom_call_target="tpu_custom_call" | custom-call | flops 2000000 | bytes 1048576 | tf_op jit(solution)/shard_map/pallas_call | solution.py:696
  89.0 6.7 %all-to-all-start.5 = ((bf16[32,16,128]{2,1,0:T(8,128)(2,1)}), bf16[32,16,128]{2,1,0:T(8,128)(2,1)S(1)}, u32[]{:S(2)}, u32[]{:S(2)}) async-start(bf16[32,16,128]{2,1,0:T(8,128)(2,1)} %get-tuple-element.54), calls=%async_computation.5 | async-start | bytes 262144 | tf_op jit(solution)/shard_map/all_to_all | solution.py:32
  95.7 3.7 %collective-permute-start.8 = (bf16[3,32,256]{2,1,0:T(8,128)(2,1)}, bf16[3,32,256]{2,1,0:T(8,128)(2,1)S(1)}, u32[]{:S(2)}, u32[]{:S(2)}) collective-permute-start(bf16[3,32,256]{2,1,0:T(8,128)(2,1)} %get-tuple-element.58), channel_id=1, source_target_pairs={{0,1},{1,2},{2,3},{3,4},{4,5},{5,6},{6,7},{8,9},{9,10},{10,11},{11... | collective-permute-start | bytes 147464 | tf_op jit(solution)/shard_map/ppermute | solution.py:38
  99.4 1.3 %collective-permute-start.9 = (bf16[3,32,256]{2,1,0:T(8,128)(2,1)}, bf16[3,32,256]{2,1,0:T(8,128)(2,1)S(1)}, u32[]{:S(2)}, u32[]{:S(2)}) collective-permute-start(bf16[3,32,256]{2,1,0:T(8,128)(2,1)} %get-tuple-element.59), channel_id=1, source_target_pairs={{1,0},{2,1},{3,2},{4,3},{5,4},{6,5},{7,6},{9,8},{10,9},{11,10},{12... | collective-permute-start | bytes 147464 | tf_op jit(solution)/shard_map/ppermute | solution.py:38
  100.7 0.7 collective-permute-done.8.above_ref
  101.5 4.1 %collective-permute-done.9.below_ref = bf16[3,32,256]{2,1,0:T(8,128)(2,1)S(1)} collective-permute-done((bf16[3,32,256]{2,1,0:T(8,128)(2,1)}, bf16[3,32,256]{2,1,0:T(8,128)(2,1)S(1)}, u32[]{:S(2)}, u32[]{:S(2)}) %collective-permute-start.9) | collective-permute-done | bytes 49184 | tf_op jit(solution)/shard_map/ppermute | solution.py:38
  105.6 0.0 all-to-all-done.5.sums_ref
  105.6 5.7 %shard_map.95 = (f32[3,512,256]{2,1,0:T(8,128)}, f32[6,512,256]{2,1,0:T(8,128)}, f32[2]{0:T(128)}) custom-call(bf16[32,16,128]{2,1,0:T(8,128)(2,1)S(1)} %all-to-all-done.5.sums_ref, f32[8,128]{1,0:T(8,128)} %get-tuple-element.55.first_cost_hbm, f32[8,128]{1,0:T(8,128)} %copy-done.9, f32[3,512,256]{2,1,0:T(8,128)} %get-tuple-element.56.wind_hbm, ...), custom_call_target="tpu_custom_call" | custom-call | flops 2000000 | bytes 1048576 | tf_op jit(solution)/shard_map/pallas_call | solution.py:696
  (24 shorter events, 0.0 us)
Async XLA Ops:
  0.6 0.7 copy-start.10
  16.3 1.4 %copy-start = (f32[3,16,32,256]{3,2,1,0:T(8,128)S(1)}, f32[3,16,32,256]{3,2,1,0:T(8,128)}, u32[]{:S(2)}) copy-start(f32[3,16,32,256]{3,2,1,0:T(8,128)} %param.6) | copy-start | bytes 4718596
  19.7 11.6 %all-to-all-start.1 = ((bf16[32,8,128]{2,1,0:T(8,128)(2,1)}), bf16[32,8,128]{2,1,0:T(8,128)(2,1)S(1)}, u32[]{:S(2)}, u32[]{:S(2)}) async-start(bf16[32,8,128]{2,1,0:T(8,128)(2,1)} %shard_map.86), calls=%async_computation.1 | async-start | bytes 131072 | tf_op jit(solution)/shard_map/all_to_all | solution.py:32
  24.8 21.8 %collective-permute-start.2 = (f32[4,32,256]{2,1,0:T(8,128)}, f32[4,32,256]{2,1,0:T(8,128)S(1)}, u32[]{:S(2)}, u32[]{:S(2)}) collective-permute-start(f32[4,32,256]{2,1,0:T(8,128)} %get-tuple-element.38), channel_id=1, source_target_pairs={{0,1},{1,2},{2,3},{3,4},{4,5},{5,6},{6,7},{8,9},{9,10},{10,11},{11... | collective-permute-start | bytes 393224 | tf_op jit(solution)/shard_map/ppermute | solution.py:38
  28.3 18.2 %collective-permute-start.3 = (f32[4,32,256]{2,1,0:T(8,128)}, f32[4,32,256]{2,1,0:T(8,128)S(1)}, u32[]{:S(2)}, u32[]{:S(2)}) collective-permute-start(f32[4,32,256]{2,1,0:T(8,128)} %get-tuple-element.39), channel_id=1, source_target_pairs={{1,0},{2,1},{3,2},{4,3},{5,4},{6,5},{7,6},{9,8},{10,9},{11,10},{12... | collective-permute-start | bytes 393224 | tf_op jit(solution)/shard_map/ppermute | solution.py:38
  31.3 8.8 %copy-start.14 = (f32[8,512]{1,0:T(8,128)S(1)}, f32[8,512]{1,0:T(8,128)}, u32[]{:S(2)}) copy-start(f32[8,512]{1,0:T(8,128)} %get-tuple-element.36) | copy-start | bytes 49156
  31.4 11.0 %copy-start.13 = (f32[8,512]{1,0:T(8,128)S(1)}, f32[8,512]{1,0:T(8,128)}, u32[]{:S(2)}) copy-start(f32[8,512]{1,0:T(8,128)} %get-tuple-element.37) | copy-start | bytes 49156
  33.3 17.4 %all-to-all-start.2 = ((bf16[32,8,128]{2,1,0:T(8,128)(2,1)}), bf16[32,8,128]{2,1,0:T(8,128)(2,1)S(1)}, u32[]{:S(2)}, u32[]{:S(2)}) async-start(bf16[32,8,128]{2,1,0:T(8,128)(2,1)} %get-tuple-element.35), calls=%async_computation.2 | async-start | bytes 131072 | tf_op jit(solution)/shard_map/all_to_all | solution.py:32
  40.2 3.5 %collective-permute-start = (f32[8,512]{1,0:T(8,128)S(1)}, f32[8,512]{1,0:T(8,128)S(1)}, u32[]{:S(2)}, u32[]{:S(2)}) collective-permute-start(f32[8,512]{1,0:T(8,128)S(1)} %copy-done.14), channel_id=1, source_target_pairs={{0,8},{8,16},{16,24},{1,9},{9,17},{17,25},{2,10},{10,18},{18,26},{... | collective-permute-start | bytes 49160 | tf_op jit(solution)/shard_map/ppermute | solution.py:38
  42.3 4.2 %collective-permute-start.1 = (f32[8,512]{1,0:T(8,128)S(1)}, f32[8,512]{1,0:T(8,128)S(1)}, u32[]{:S(2)}, u32[]{:S(2)}) collective-permute-start(f32[8,512]{1,0:T(8,128)S(1)} %copy-done.13), channel_id=1, source_target_pairs={{8,0},{16,8},{24,16},{9,1},{17,9},{25,17},{10,2},{18,10},{26,18},{... | collective-permute-start | bytes 49160 | tf_op jit(solution)/shard_map/ppermute | solution.py:38
  43.6 10.8 %copy-start.5 = (f32[8,512]{1,0:T(8,128)}, f32[8,512]{1,0:T(8,128)S(1)}, u32[]{:S(2)}) copy-start(f32[8,512]{1,0:T(8,128)S(1)} %collective-permute-done.left_ref.left_0) | copy-start | bytes 49156
  46.5 7.9 %copy-start.6 = (f32[8,512]{1,0:T(8,128)}, f32[8,512]{1,0:T(8,128)S(1)}, u32[]{:S(2)}) copy-start(f32[8,512]{1,0:T(8,128)S(1)} %collective-permute-done.1.right_ref.right_0) | copy-start | bytes 49156
  46.5 7.9 %copy-start.3 = (f32[4,32,256]{2,1,0:T(8,128)}, f32[4,32,256]{2,1,0:T(8,128)S(1)}, u32[]{:S(2)}) copy-start(f32[4,32,256]{2,1,0:T(8,128)S(1)} %collective-permute-done.2.above_ref.above_0) | copy-start | bytes 393220
  46.6 7.9 %copy-start.4 = (f32[4,32,256]{2,1,0:T(8,128)}, f32[4,32,256]{2,1,0:T(8,128)S(1)}, u32[]{:S(2)}) copy-start(f32[4,32,256]{2,1,0:T(8,128)S(1)} %collective-permute-done.3.below_ref.below_0) | copy-start | bytes 393220
  54.4 20.5 %copy-start.12 = (f32[8,512]{1,0:T(8,128)S(1)}, f32[8,512]{1,0:T(8,128)}, u32[]{:S(2)}) copy-start(f32[8,512]{1,0:T(8,128)} %get-tuple-element.46) | copy-start | bytes 49156
  54.5 22.7 %copy-start.11 = (f32[8,512]{1,0:T(8,128)S(1)}, f32[8,512]{1,0:T(8,128)}, u32[]{:S(2)}) copy-start(f32[8,512]{1,0:T(8,128)} %get-tuple-element.47) | copy-start | bytes 49156
  54.5 14.5 %all-to-all-start.3 = ((f32[32,8,128]{2,1,0:T(8,128)}), f32[32,8,128]{2,1,0:T(8,128)S(1)}, u32[]{:S(2)}, u32[]{:S(2)}) async-start(f32[32,8,128]{2,1,0:T(8,128)} %get-tuple-element.42), calls=%async_computation.3 | async-start | bytes 262144 | tf_op jit(solution)/shard_map/all_to_all | solution.py:32
  61.2 20.2 %collective-permute-start.6 = (f32[4,32,256]{2,1,0:T(8,128)}, f32[4,32,256]{2,1,0:T(8,128)S(1)}, u32[]{:S(2)}, u32[]{:S(2)}) collective-permute-start(f32[4,32,256]{2,1,0:T(8,128)} %get-tuple-element.48), channel_id=1, source_target_pairs={{0,1},{1,2},{2,3},{3,4},{4,5},{5,6},{6,7},{8,9},{9,10},{10,11},{11... | collective-permute-start | bytes 393224 | tf_op jit(solution)/shard_map/ppermute | solution.py:38
  64.9 16.5 %collective-permute-start.7 = (f32[4,32,256]{2,1,0:T(8,128)}, f32[4,32,256]{2,1,0:T(8,128)S(1)}, u32[]{:S(2)}, u32[]{:S(2)}) collective-permute-start(f32[4,32,256]{2,1,0:T(8,128)} %get-tuple-element.49), channel_id=1, source_target_pairs={{1,0},{2,1},{3,2},{4,3},{5,4},{6,5},{7,6},{9,8},{10,9},{11,10},{12... | collective-permute-start | bytes 393224 | tf_op jit(solution)/shard_map/ppermute | solution.py:38
  71.0 15.0 %copy-start.9 = (f32[8,128]{1,0:T(8,128)}, f32[8,128]{1,0:T(8,128)S(1)}, u32[]{:S(2)}) copy-start(f32[8,128]{1,0:T(8,128)S(1)} %get-tuple-element.51.step_ref) | copy-start | bytes 12292
  71.0 15.0 %all-to-all-start.4 = ((bf16[32,8,128]{2,1,0:T(8,128)(2,1)}), bf16[32,8,128]{2,1,0:T(8,128)(2,1)S(1)}, u32[]{:S(2)}, u32[]{:S(2)}) async-start(bf16[32,8,128]{2,1,0:T(8,128)(2,1)} %get-tuple-element.44), calls=%async_computation.4 | async-start | bytes 131072 | tf_op jit(solution)/shard_map/all_to_all | solution.py:32
  75.0 3.5 %collective-permute-start.4 = (f32[8,512]{1,0:T(8,128)S(1)}, f32[8,512]{1,0:T(8,128)S(1)}, u32[]{:S(2)}, u32[]{:S(2)}) collective-permute-start(f32[8,512]{1,0:T(8,128)S(1)} %copy-done.12), channel_id=1, source_target_pairs={{0,8},{8,16},{16,24},{1,9},{9,17},{17,25},{2,10},{10,18},{18,26},{... | collective-permute-start | bytes 49160 | tf_op jit(solution)/shard_map/ppermute | solution.py:38
  77.1 4.2 %collective-permute-start.5 = (f32[8,512]{1,0:T(8,128)S(1)}, f32[8,512]{1,0:T(8,128)S(1)}, u32[]{:S(2)}, u32[]{:S(2)}) collective-permute-start(f32[8,512]{1,0:T(8,128)S(1)} %copy-done.11), channel_id=1, source_target_pairs={{8,0},{16,8},{24,16},{9,1},{17,9},{25,17},{10,2},{18,10},{26,18},{... | collective-permute-start | bytes 49160 | tf_op jit(solution)/shard_map/ppermute | solution.py:38
  78.4 7.6 %copy-start.7 = (f32[8,512]{1,0:T(8,128)}, f32[8,512]{1,0:T(8,128)S(1)}, u32[]{:S(2)}) copy-start(f32[8,512]{1,0:T(8,128)S(1)} %collective-permute-done.4.left_ref.left_1) | copy-start | bytes 49156
  81.3 4.7 %copy-start.8 = (f32[8,512]{1,0:T(8,128)}, f32[8,512]{1,0:T(8,128)S(1)}, u32[]{:S(2)}) copy-start(f32[8,512]{1,0:T(8,128)S(1)} %collective-permute-done.5.right_ref.right_1) | copy-start | bytes 49156
  81.3 4.7 %copy-start.1 = (f32[4,32,256]{2,1,0:T(8,128)}, f32[4,32,256]{2,1,0:T(8,128)S(1)}, u32[]{:S(2)}) copy-start(f32[4,32,256]{2,1,0:T(8,128)S(1)} %collective-permute-done.6.above_ref.above_1) | copy-start | bytes 393220
  81.4 4.7 %copy-start.2 = (f32[4,32,256]{2,1,0:T(8,128)}, f32[4,32,256]{2,1,0:T(8,128)S(1)}, u32[]{:S(2)}) copy-start(f32[4,32,256]{2,1,0:T(8,128)S(1)} %collective-permute-done.7.below_ref.below_1) | copy-start | bytes 393220
  89.0 16.6 %all-to-all-start.5 = ((bf16[32,16,128]{2,1,0:T(8,128)(2,1)}), bf16[32,16,128]{2,1,0:T(8,128)(2,1)S(1)}, u32[]{:S(2)}, u32[]{:S(2)}) async-start(bf16[32,16,128]{2,1,0:T(8,128)(2,1)} %get-tuple-element.54), calls=%async_computation.5 | async-start | bytes 262144 | tf_op jit(solution)/shard_map/all_to_all | solution.py:32
  95.7 5.7 %collective-permute-start.8 = (bf16[3,32,256]{2,1,0:T(8,128)(2,1)}, bf16[3,32,256]{2,1,0:T(8,128)(2,1)S(1)}, u32[]{:S(2)}, u32[]{:S(2)}) collective-permute-start(bf16[3,32,256]{2,1,0:T(8,128)(2,1)} %get-tuple-element.58), channel_id=1, source_target_pairs={{0,1},{1,2},{2,3},{3,4},{4,5},{5,6},{6,7},{8,9},{9,10},{10,11},{11... | collective-permute-start | bytes 147464 | tf_op jit(solution)/shard_map/ppermute | solution.py:38
  99.4 6.2 %collective-permute-start.9 = (bf16[3,32,256]{2,1,0:T(8,128)(2,1)}, bf16[3,32,256]{2,1,0:T(8,128)(2,1)S(1)}, u32[]{:S(2)}, u32[]{:S(2)}) collective-permute-start(bf16[3,32,256]{2,1,0:T(8,128)(2,1)} %get-tuple-element.59), channel_id=1, source_target_pairs={{1,0},{2,1},{3,2},{4,3},{5,4},{6,5},{7,6},{9,8},{10,9},{11,10},{12... | collective-permute-start | bytes 147464 | tf_op jit(solution)/shard_map/ppermute | solution.py:38

commit v6 on v5

--- a/solution.py
+++ b/solution.py
@@ -127,6 +127,32 @@
         jnp.sum(jnp.where(lower, line, 0.0), axis=1, keepdims=True),
         jnp.sum(jnp.where(lower, 0.0, line), axis=1, keepdims=True),
     )
+
+
+def in_parts(line, count):
+    parts = []
+    for _ in range(count):
+        parts.append(line.astype(BF16).astype(F32))
+        line = line - parts[-1]
+    return parts
+
+
+def put_columns(ref, place, row, columns, lines):
+    for i, column in enumerate(columns):
+        for q in range(lines):
+            at = row + i * lines + q
+            ref[place, at : at + 1, :] = column[:, q * LANES : (q + 1) * LANES]
+
+
+def take_columns(block, row, count, lines):
+    return [
+        jnp.concatenate([block[row + i * lines + q : row + i * lines + q + 1] for q in range(lines)], axis=1)
+        for i in range(count)
+    ]
+
+
+def block_of(ref, place):
+    return ref[pl.ds(place, 1)].reshape(ref.shape[1:]).astype(F32)
 
 
 def own_place():
@@ -235,11 +261,11 @@
         out[ROW_WZ] = w_ref[2, here, :]
 
 
-def cycle(levels, w_ref, left_ref, right_ref, above_ref, below_ref, corners, ring, left_rows, right_rows, need, take_spread, take_push):
+def cycle(levels, w_ref, left, right, above_ref, below_ref, corners, ring, left_rows, right_rows, need, take_spread, take_push):
     rows, width = w_ref.shape[1], w_ref.shape[2]
     cells = rows // levels
-    left_rows[...] = to_rows(left_ref[...])
-    right_rows[...] = to_rows(right_ref[...])
+    left_rows[...] = to_rows(left)
+    right_rows[...] = to_rows(right)
     has_left = jnp.where(lax.axis_index("radar") > 0, 1.0, 0.0)
     has_right = jnp.where(lax.axis_index("radar") < lax.axis_size("radar") - 1, 1.0, 0.0)
     has_above = jnp.where(lax.axis_index("tile") > 0, 1.0, 0.0)
@@ -310,13 +336,13 @@
             pushes.filled(here.stop)
 
     corners = corner_columns(line_from, levels)
-    cycle(levels, w_ref, left_ref, right_ref, above_ref, below_ref, corners, ring, left_rows, right_rows, fields.until, take_spread, take_push)
+    cycle(levels, w_ref, left_ref[...], right_ref[...], above_ref, below_ref, corners, ring, left_rows, right_rows, fields.until, take_spread, take_push)
     total_out[...] = jnp.broadcast_to(0.5 * DIVERGENCE_WEIGHT * sum_rows(total[...]), total_out.shape)
     spreads.finish()
     pushes.finish()
 
 
-def second_cycle_kernel(levels, slots, w_hbm, left_ref, right_ref, above_ref, below_ref, got_ref, background_hbm, push_hbm, spread_hbm, step_ref, rest_hbm, wind_hbm, total_out, w_ref, background, push, spread, ring, left_rows, right_rows, total, sems):
+def second_cycle_kernel(levels, slots, w_hbm, above_ref, below_ref, got_ref, background_hbm, push_hbm, spread_hbm, step_ref, rest_hbm, wind_hbm, total_out, w_ref, background, push, spread, ring, left_rows, right_rows, total, sems):
     fields = Pieces(w_hbm, w_ref, sems.at[0], PARTS).start()
     spreads = Pieces(spread_hbm, spread, sems.at[1], PARTS).start()
     pushes = Pieces(push_hbm, push, sems.at[2], PARTS).start()
@@ -327,7 +353,19 @@
     step = step_ref[0:1, 0:1]
 
     def line_from(place):
-        return got_ref[place, 3 * slots + 1 : 3 * slots + 2, :]
+        block = block_of(got_ref, place)
+        first = block[3 * slots + SPLIT : 3 * slots + SPLIT + 1]
+        return first + pltpu.roll(first, LANES // 2, 1) + block[3 * slots + SPLIT + 1 : 3 * slots + SPLIT + 2]
+
+    lines = w_ref.shape[1] // LANES
+    sides = []
+    for along_radar in (-1, 1):
+        exists, place = neighbour(0, along_radar)
+        wy, part = take_columns(block_of(got_ref, place), 3 * slots + SPLIT + 2, 2, lines)
+        fill = jnp.zeros_like(wy)
+        columns = [fill] * 8
+        columns[COL_WY], columns[COL_PART] = jnp.where(exists, wy, 0.0), jnp.where(exists, part, 0.0)
+        sides.append(jnp.concatenate(columns, axis=0))
 
     def take_spread(here, bent):
         spreads.until(here.stop)
@@ -346,7 +384,7 @@
             winds.filled(here.stop)
 
     corners = corner_columns(line_from, levels)
-    cycle(levels, w_ref, left_ref, right_ref, above_ref, below_ref, corners, ring, left_rows, right_rows, fields.until, take_spread, take_push)
+    cycle(levels, w_ref, *sides, above_ref, below_ref, corners, ring, left_rows, right_rows, fields.until, take_spread, take_push)
     total_out[...] = jnp.broadcast_to(sum_rows(total[...]), total_out.shape)
     rests.finish()
     winds.finish()
@@ -477,9 +515,11 @@
 
 
 def second_source_kernel(slots, total_cells, total_gates, got_ref, weights_ref, sight_ref, misfit_ref, returned_out, step_out, cost_out, proj_ref, adj_ref, line_ref):
-    sources, height = got_ref.shape[0], got_ref.shape[1]
-    project(lambda s: got_ref[s].astype(BF16), weights_ref, proj_ref, sources, slots, height)
-    squares, costs = halves(jnp.sum(got_ref[:, 3 * slots, :], axis=0, keepdims=True))
+    sources, height = returned_out.shape[0], returned_out.shape[1]
+    project(lambda s: got_ref[s, 0:height], weights_ref, proj_ref, sources, slots, height)
+    squares, costs = halves(
+        jnp.sum(jnp.sum(got_ref[:, 3 * slots : 3 * slots + SPLIT, :].astype(F32), axis=0), axis=0, keepdims=True)
+    )
     step = STEP_LENGTH / jnp.sqrt(squares / total_cells + EPSILON)
     step_out[...] = jnp.broadcast_to(step, step_out.shape)
     cost_out[...] = jnp.broadcast_to(costs / total_gates, cost_out.shape)
@@ -541,14 +581,15 @@
     return jnp.sum(jnp.sum(cost, axis=0), axis=0, keepdims=True)
 
 
-def first_owner_kernel(slots, levels, asked_hbm, returned_ref, push_hbm, spread_cost_ref, gradient_hbm, give_out, left_out, right_out, up_out, down_out, push, gradient, asked_ref, scratch, sems):
+def first_owner_kernel(slots, levels, asked_hbm, returned_ref, push_hbm, spread_cost_ref, gradient_hbm, give_out, left_out, right_out, up_out, down_out, push, gradient, asked_ref, scratch, give_ref, sems):
     squares, copies = gather_gradient(
         slots, levels, asked_hbm, asked_ref, returned_ref, push_hbm, push, gradient, gradient_hbm, sems
     )
     sources = give_out.shape[0]
     sums = paired(squares, seen_cost(returned_ref, slots) + spread_cost_ref[0:1, :])
-    give_out[...] = jnp.zeros_like(give_out)
-    give_out[:, 3 * slots, :] = jnp.broadcast_to(sums, (sources, LANES))
+    give_ref[...] = jnp.zeros_like(give_ref)
+    for i, part in enumerate(in_parts(sums, SPLIT)):
+        give_ref[:, 3 * slots + i, :] = jnp.broadcast_to(part, (sources, LANES))
     me = own_place()
     runs = gradient.shape[2] // LANES
 
@@ -556,32 +597,48 @@
         for p in range(slots):
             row, run = block_at(asked_ref[s, me * slots + p], runs)
             for k in range(3):
-                give_out[s, 3 * p + k : 3 * p + k + 1, :] = read_block(gradient, k, row, run)
+                give_ref[s, 3 * p + k : 3 * p + k + 1, :] = read_block(gradient, k, row, run)
 
     for_slots(sources, one)
     for (along_tile, along_radar), line in zip(CORNERS, corner_lines(gradient, levels)):
         exists, place = neighbour(along_tile, along_radar)
+        high, middle, low = in_parts(line, 3)
 
         @pl.when(exists)
         def _():
-            give_out[place, 3 * slots + 1 : 3 * slots + 2, :] = line
+            row = 3 * slots + SPLIT
+            give_ref[place, row : row + 1, :] = high + pltpu.roll(middle, LANES // 2, 1)
+            give_ref[place, row + 1 : row + 2, :] = low
 
     edges_kernel(levels, gradient, left_out, right_out, up_out, down_out, scratch)
+    lines = gradient.shape[1] // LANES
+    for along_radar, ref in ((-1, left_out), (1, right_out)):
+        exists, place = neighbour(0, along_radar)
+
+        @pl.when(exists)
+        def _():
+            columns = [ref[f : f + 1, :] for f in (COL_WY, COL_PART)]
+            put_columns(give_ref, place, 3 * slots + SPLIT + 2, columns, lines)
+
+    give_out[...] = give_ref[...].astype(BF16)
     for copy in copies:
         copy.wait()
 
 
-def second_owner_kernel(slots, levels, asked_hbm, returned_ref, rest_hbm, rest_cost_ref, gradient_out, give_out, up_out, down_out, rest, asked_ref, scratch, give_ref, sems):
+def second_owner_kernel(slots, levels, asked_hbm, returned_ref, rest_hbm, rest_cost_ref, left_hbm, right_hbm, gradient_out, give_out, up_out, down_out, rest, asked_ref, scratch, give_ref, bent_ref, sems, bent_sems):
     rows, width = gradient_out.shape[1], gradient_out.shape[2]
+    bents = [
+        pltpu.make_async_copy(source, bent_ref.at[i], bent_sems.at[i]) for i, source in enumerate((left_hbm, right_hbm))
+    ]
+    for copy in bents:
+        copy.start()
     squares, _ = gather_gradient(
         slots, levels, asked_hbm, asked_ref, returned_ref, rest_hbm, rest, gradient_out, None, sems
     )
     sums = paired(squares, seen_cost(returned_ref, slots) + rest_cost_ref[0:1, :])
     give_ref[...] = jnp.zeros_like(give_ref)
-    for i in range(SPLIT):
-        part = sums.astype(BF16).astype(F32)
+    for i, part in enumerate(in_parts(sums, SPLIT)):
         give_ref[:, i, :] = jnp.broadcast_to(part, (give_ref.shape[0], LANES))
-        sums = sums - part
     for k in range(3):
         up_out[k] = gradient_out[k, 0:levels, :].astype(BF16)
         down_out[k] = gradient_out[k, rows - levels : rows, :].astype(BF16)
@@ -595,26 +652,31 @@
         scratch[here, :] = packed
     turned = scratch[...].T
     lines = rows // LANES
-    for along_radar, first in ((-1, 0), (1, LANES - 8)):
+    for copy in bents:
+        copy.wait()
+    for i, (along_radar, first) in enumerate(((-1, 0), (1, LANES - 8))):
         exists, place = neighbour(0, along_radar)
 
         @pl.when(exists)
         def _():
-            for k in range(3):
-                for q in range(lines):
-                    row = SPLIT + k * lines + q
-                    piece = turned[first + k : first + k + 1, q * LANES : (q + 1) * LANES]
-                    give_ref[place, row : row + 1, :] = piece
+            columns = [turned[first + k : first + k + 1] for k in range(3)]
+            columns += [bent_ref[i, f : f + 1, :] for f in (COL_WX, COL_WZ)]
+            put_columns(give_ref, place, SPLIT, columns, lines)
 
     give_out[...] = give_ref[...].astype(BF16)
 
 
-def final_kernel(levels, total_cells, total_gates, sums_ref, first_cost_hbm, step_ref, wind_hbm, gradient_ref, left_0, right_0, above_0, below_0, left_1, right_1, above_1, below_1, above_ref, below_ref, wind_out, strain_out, cost_out, left_rows, right_rows, wind, strain, first_cost_ref, sems, cost_sem):
+def final_kernel(levels, slots, total_cells, total_gates, sums_ref, first_cost_hbm, step_ref, wind_hbm, gradient_ref, left_0, right_0, above_0, below_0, got_hbm, above_1, below_1, above_ref, below_ref, wind_out, strain_out, cost_out, left_rows, right_rows, wind, strain, first_cost_ref, got_ref, sems, cost_sem, got_sems):
     rows = gradient_ref.shape[1]
     cells = rows // levels
     winds = Pieces(wind_hbm, wind, sems.at[0], FINAL_PARTS).start()
     cost_copy = pltpu.make_async_copy(first_cost_hbm, first_cost_ref, cost_sem)
     cost_copy.start()
+    got_copies = []
+    for i, along_radar in enumerate((-1, 1)):
+        _, place = neighbour(0, along_radar)
+        got_copies.append(pltpu.make_async_copy(got_hbm.at[place], got_ref.at[i], got_sems.at[i]))
+        got_copies[-1].start()
     wind_outs = OutPieces(wind, wind_out, sems.at[1], FINAL_PARTS)
     strain_outs = OutPieces(strain, strain_out, sems.at[2], FINAL_PARTS)
     squares, cost = halves(jnp.sum(jnp.sum(sums_ref[:, 0:SPLIT, :].astype(F32), axis=0), axis=0, keepdims=True))
@@ -622,15 +684,16 @@
     cost_out[1] = (cost / total_gates)[0, 0]
     first_step = step_ref[0:1, 0:1]
     lines = rows // LANES
-    for along_radar, out, background, bent in ((-1, left_rows, left_0, left_1), (1, right_rows, right_0, right_1)):
+    for copy in got_copies:
+        copy.wait()
+    for i, (along_radar, out, background) in enumerate(((-1, left_rows, left_0), (1, right_rows, right_0))):
         exists, place = neighbour(0, along_radar)
+        *sent, bent_x, bent_z = take_columns(block_of(sums_ref, place), SPLIT, 5, lines)
+        (bent_y,) = take_columns(got_ref[i].astype(F32), 3 * slots + SPLIT + 2, 1, lines)
         columns = []
-        block = sums_ref[pl.ds(place, 1)].reshape(sums_ref.shape[1:]).astype(F32)
-        for k in range(3):
-            at = slice(COL_WIND[k], COL_WIND[k] + 1)
-            sent = [block[SPLIT + k * lines + q : SPLIT + 1 + k * lines + q] for q in range(lines)]
-            sent = jnp.where(exists, jnp.concatenate(sent, axis=1), 0.0)
-            columns.append(background[at, :] - first_step * bent[at, :] - step * sent)
+        for k, bent in enumerate((bent_x, bent_y, bent_z)):
+            change = jnp.where(exists, first_step * bent + step * sent[k], 0.0)
+            columns.append(background[COL_WIND[k] : COL_WIND[k] + 1, :] - change)
         out[...] = to_rows(jnp.concatenate(columns + [jnp.zeros((5, rows), F32)], axis=0))
 
     def settle(x):
@@ -732,12 +795,15 @@
     semaphores = pltpu.SemaphoreType.DMA
     places = pltpu.SMEM((devices, lanes), jnp.int32)
 
+    def row_halo(up, down):
+        above = shifted(down, "tile", 1)
+        below = shifted(up, "tile", -1)
+        return above, below
+
     def halo(left, right, up, down):
         from_left = shifted(right, "radar", 1)
         from_right = shifted(left, "radar", -1)
-        above = shifted(down, "tile", 1)
-        below = shifted(up, "tile", -1)
-        return from_left, from_right, above, below
+        return (from_left, from_right) + row_halo(up, down)
 
     def edges_of(values):
         out = call(
@@ -798,18 +864,18 @@
         out_raw=(0, 1),
         out_chip=(2,),
     )
+    given = -(-(3 * slots + SPLIT + 2 + 2 * rows // LANES) // 8) * 8
     gradient, give, *sides = call(
         functools.partial(first_owner_kernel, slots, levels),
-        (grid, shape(devices, height, LANES)) + edges + row_edges,
+        (grid, shape(devices, given, LANES, dtype=BF16)) + edges + row_edges,
         (asked, returned, push, spread_cost),
-        (whole, whole, places, side, semaphores((width_x + 2,))),
+        (whole, whole, places, side, pltpu.VMEM((devices, given, LANES), F32), semaphores((width_x + 2,))),
         chip=(0, 1, 3),
         raw=(0, 2),
         out_raw=(0,),
     )
     got = exchange(give)
-    around = halo(*sides)
-    around_1 = around
+    around_1 = row_halo(*sides[2:])
     returned, step, first_cost = call(
         functools.partial(second_source_kernel, slots, total_cells, total_gates),
         (shape(devices, height, LANES, dtype=BF16), line_out, line_out),
@@ -822,42 +888,51 @@
     rest, wind, rest_cost = call(
         functools.partial(second_cycle_kernel, levels, slots),
         (grid, grid, line_out),
-        (gradient,) + around + (got, field, push, spread, step),
+        (gradient,) + around_1 + (got, field, push, spread, step),
         (whole, whole, whole, plane, ring, side, side, strip, semaphores((6, PARTS))),
-        chip=(1, 2, 3, 4, 5, 9),
-        raw=(0, 6, 7, 8),
+        chip=(1, 2, 3, 7),
+        raw=(0, 4, 5, 6),
         out_raw=(0, 1),
         out_chip=(2,),
     )
     last_rows = (shape(3, levels, width_y, dtype=BF16), shape(3, levels, width_y, dtype=BF16))
-    sent = -(-(SPLIT + 3 * rows // LANES) // 8) * 8
+    sent = -(-(SPLIT + 5 * rows // LANES) // 8) * 8
     gradient, give, up, down = call(
         functools.partial(second_owner_kernel, slots, levels),
         (grid, shape(devices, sent, LANES, dtype=BF16)) + last_rows,
-        (asked, returned, rest, rest_cost),
-        (whole, places, side, pltpu.VMEM((devices, sent, LANES), F32), semaphores((width_x + 2,))),
+        (asked, returned, rest, rest_cost) + tuple(sides[:2]),
+        (
+            whole,
+            places,
+            side,
+            pltpu.VMEM((devices, sent, LANES), F32),
+            pltpu.VMEM((2, 8, rows), F32),
+            semaphores((width_x + 2,)),
+            semaphores((2,)),
+        ),
         chip=(0, 1, 3),
-        raw=(0, 2),
+        raw=(0, 2, 4, 5),
         out_chip=(0,),
     )
     sums = exchange(give)
-    above = shifted(down, "tile", 1)
-    below = shifted(up, "tile", -1)
+    around_2 = row_halo(up, down)
     wind, strain, costs = call(
-        functools.partial(final_kernel, levels, total_cells, total_gates),
+        functools.partial(final_kernel, levels, slots, total_cells, total_gates),
         (grid, shape(6, rows, width_y), shape(2)),
-        (sums, first_cost, step, wind, gradient) + around_0 + around_1 + (above, below),
+        (sums, first_cost, step, wind, gradient) + around_0 + (got,) + around_1 + around_2,
         (
             side,
             side,
             pltpu.VMEM((3, rows, width_y), F32),
             pltpu.VMEM((6, rows, width_y), F32),
             pltpu.SMEM((8, LANES), F32),
+            pltpu.VMEM((2, given, LANES), BF16),
             semaphores((3, FINAL_PARTS)),
             semaphores,
+            semaphores((2,)),
         ),
-        chip=(0, 4, 13, 14),
-        raw=(1, 3),
+        chip=(0, 4, 5, 6, 7, 8, 10, 11, 12, 13),
+        raw=(1, 3, 9),
         out_raw=(0, 1),
         out_smem=(2,),
     )

time: 112 us -> 105 us (0.938)
  starting transfers between devices: 48.4 us -> 41.1 us
    all_to_all x5, starting transfers between devices: 26.7 us -> 22.9 us  [exchange(): return lax.all_to_all(x, AXES, split_axis=0, concat_axis=0, tiled=True)]
    ppermute x10 -> x8, starting transfers between devices: 21.7 us -> 18.2 us  [shifted(): return lax.ppermute(x, axis, pairs)]
    all_to_all x5, waiting for transfers between devices: 2.83 us -> 5.88 us  [exchange(): return lax.all_to_all(x, AXES, split_axis=0, concat_axis=0, tiled=True)]
    ppermute x10 -> x8, waiting for transfers between devices: 10.7 us -> 7.81 us  [shifted(): return lax.ppermute(x, axis, pairs)]
  transfers between devices with their start and end apart: 15 -> 13, of which waited for: 5 -> 5; matrix products, arithmetic and copies ran while one was open for 0% -> 0% of each run, Pallas kernels for 15% -> 16%
where the time goes in v6:
time: 105 us
  starting transfers between devices  41.1 us (39%)
  Pallas kernels  32.3 us (31%)
  blocking collectives  14.4 us (14%)
  waiting for transfers between devices  13.7 us (13%)
  local copies, waits for them, and re-layouts  2.07 us (2%)
    pallas_call x11, Pallas kernels, call(): pl.pallas_call(kernel, out_shape=placed[0] if single else placed, in_spec...  32.3 us
    all_to_all x5, starting transfers between devices, exchange(): return lax.all_to_all(x, AXES, split_axis=0, concat_axis=0, tiled=True)  22.9 us
    ppermute x8, starting transfers between devices, shifted(): return lax.ppermute(x, axis, pairs)  18.2 us
    all_to_all x1, blocking collectives, exchange(): return lax.all_to_all(x, AXES, split_axis=0, concat_axis=0, tiled=True)  14.4 us
    ppermute x8, waiting for transfers between devices, shifted(): return lax.ppermute(x, axis, pairs)  7.81 us
    all_to_all x5, waiting for transfers between devices, exchange(): return lax.all_to_all(x, AXES, split_axis=0, concat_axis=0, tiled=True)  5.88 us
  transfers between devices with their start and end apart: 13, of which 5 were waited for; matrix products, arithmetic and copies ran while one was open for 0% of the time, Pallas kernels for 16%

profile of v6, /device:TPU:0, one launch (start us, length us, event | category | flops | bytes accessed | tf_op | source)
XLA Modules:
  0.0 104.5 jit_solution(17161191972617998643)
XLA Ops:
  0.6 0.0 copy-start.3
  0.6 0.6 copy-done.3
  1.3 0.6 shard_map.85
  1.9 14.4 %all_to_all.30.asked_hbm = s32[32,1,128]{2,1,0:T(1,128)S(1)} all-to-all(s32[32,1,128]{2,1,0:T(1,128)} %shard_map.85), channel_id=1, replica_groups=mesh['radar'=4,'tile'=8] {'radar','tile'}, dimensions={0} | all-to-all | bytes 32768 | tf_op jit(solution)/shard_map/all_to_all | solution.py:32
  16.3 0.0 copy-start
  16.3 1.4 %copy-done = f32[3,16,32,256]{3,2,1,0:T(8,128)S(1)} copy-done((f32[3,16,32,256]{3,2,1,0:T(8,128)S(1)}, f32[3,16,32,256]{3,2,1,0:T(8,128)}, u32[]{:S(2)}) %copy-start) | copy-done | bytes 1572888
  17.7 2.0 %shard_map.86 = bf16[32,8,128]{2,1,0:T(8,128)(2,1)} custom-call(s32[32,1,128]{2,1,0:T(1,128)S(1)} %all_to_all.30.asked_hbm, f32[3,512,256]{2,1,0:T(8,128)S(1)} %bitcast.8), custom_call_target="tpu_custom_call" | custom-call | flops 2000000 | bytes 1048576 | tf_op jit(solution)/shard_map/pallas_call | solution.py:759
  19.7 2.6 %all-to-all-start.1 = ((bf16[32,8,128]{2,1,0:T(8,128)(2,1)}), bf16[32,8,128]{2,1,0:T(8,128)(2,1)S(1)}, u32[]{:S(2)}, u32[]{:S(2)}) async-start(bf16[32,8,128]{2,1,0:T(8,128)(2,1)} %shard_map.86), calls=%async_computation.1 | async-start | bytes 131072 | tf_op jit(solution)/shard_map/all_to_all | solution.py:32
  22.3 2.5 %shard_map.89 = (f32[8,512]{1,0:T(8,128)}, f32[8,512]{1,0:T(8,128)}, f32[4,32,256]{2,1,0:T(8,128)}, f32[4,32,256]{2,1,0:T(8,128)}) custom-call(f32[3,512,256]{2,1,0:T(8,128)} %bitcast.5), custom_call_target="tpu_custom_call" | custom-call | flops 2000000 | bytes 1048576 | tf_op jit(solution)/shard_map/pallas_call | solution.py:759
  24.8 3.6 %collective-permute-start.2 = (f32[4,32,256]{2,1,0:T(8,128)}, f32[4,32,256]{2,1,0:T(8,128)S(1)}, u32[]{:S(2)}, u32[]{:S(2)}) collective-permute-start(f32[4,32,256]{2,1,0:T(8,128)} %get-tuple-element.38), channel_id=1, source_target_pairs={{0,1},{1,2},{2,3},{3,4},{4,5},{5,6},{6,7},{8,9},{9,10},{10,11},{11... | collective-permute-start | bytes 393224 | tf_op jit(solution)/shard_map/ppermute | solution.py:38
  28.4 1.3 %collective-permute-start.3 = (f32[4,32,256]{2,1,0:T(8,128)}, f32[4,32,256]{2,1,0:T(8,128)S(1)}, u32[]{:S(2)}, u32[]{:S(2)}) collective-permute-start(f32[4,32,256]{2,1,0:T(8,128)} %get-tuple-element.39), channel_id=1, source_target_pairs={{1,0},{2,1},{3,2},{4,3},{5,4},{6,5},{7,6},{9,8},{10,9},{11,10},{12... | collective-permute-start | bytes 393224 | tf_op jit(solution)/shard_map/ppermute | solution.py:38
  29.7 1.7 %shard_map.87 = (bf16[64,128,128]{2,1,0:T(8,128)(2,1)S(1)}, f32[8,32,128]{2,1,0:T(8,128)S(1)}) custom-call(bf16[64,128,128]{2,1,0:T(8,128)(2,1)} %weights_hbm.1, bf16[3,64,128]{2,1,0:T(8,128)(2,1)} %bitcast.10, bf16[64,128]{1,0:T(8,128)(2,1)} %observed_hbm.1, s32[1,32]{1,0:T(1,128)} %count_hbm.1), custom_call_target="tpu_custom_call" | custom-call | flops 2000000 | bytes 1048576 | tf_op jit(solution)/shard_map/pallas_call | solution.py:759
  31.4 0.0 copy-start.5
  31.4 0.0 copy-start.4
  31.4 0.0 all-to-all-done.1.cells_ref
  31.4 2.0 %shard_map.88 = (bf16[32,8,128]{2,1,0:T(8,128)(2,1)}, f32[2,32,128]{2,1,0:T(8,128)S(1)}) custom-call(bf16[32,8,128]{2,1,0:T(8,128)(2,1)S(1)} %all-to-all-done.1.cells_ref, bf16[64,128,128]{2,1,0:T(8,128)(2,1)S(1)} %get-tuple-element.33.weights_ref, f32[8,32,128]{2,1,0:T(8,128)S(1)} %get-tuple-element.34.sight_ref), custom_call_target="tpu_custom_call" | custom-call | flops 2000000 | bytes 1048576 | tf_op jit(solution)/shard_map/pallas_call | solution.py:759
  33.4 6.8 %all-to-all-start.2 = ((bf16[32,8,128]{2,1,0:T(8,128)(2,1)}), bf16[32,8,128]{2,1,0:T(8,128)(2,1)S(1)}, u32[]{:S(2)}, u32[]{:S(2)}) async-start(bf16[32,8,128]{2,1,0:T(8,128)(2,1)} %get-tuple-element.35), calls=%async_computation.2 | async-start | bytes 131072 | tf_op jit(solution)/shard_map/all_to_all | solution.py:32
  40.2 0.0 copy-done.5
  40.2 2.2 %collective-permute-start = (f32[8,512]{1,0:T(8,128)S(1)}, f32[8,512]{1,0:T(8,128)S(1)}, u32[]{:S(2)}, u32[]{:S(2)}) collective-permute-start(f32[8,512]{1,0:T(8,128)S(1)} %copy-done.5), channel_id=1, source_target_pairs={{0,8},{8,16},{16,24},{1,9},{9,17},{17,25},{2,10},{10,18},{18,26},{... | collective-permute-start | bytes 49160 | tf_op jit(solution)/shard_map/ppermute | solution.py:38
  42.4 0.0 copy-done.4
  42.4 1.3 %collective-permute-start.1 = (f32[8,512]{1,0:T(8,128)S(1)}, f32[8,512]{1,0:T(8,128)S(1)}, u32[]{:S(2)}, u32[]{:S(2)}) collective-permute-start(f32[8,512]{1,0:T(8,128)S(1)} %copy-done.4), channel_id=1, source_target_pairs={{8,0},{16,8},{24,16},{9,1},{17,9},{25,17},{10,2},{18,10},{26,18},{... | collective-permute-start | bytes 49160 | tf_op jit(solution)/shard_map/ppermute | solution.py:38
  43.7 0.0 collective-permute-done.left_ref.left_0
  43.7 2.9 %collective-permute-done.1.right_ref.right_0 = f32[8,512]{1,0:T(8,128)S(1)} collective-permute-done((f32[8,512]{1,0:T(8,128)S(1)}, f32[8,512]{1,0:T(8,128)S(1)}, u32[]{:S(2)}, u32[]{:S(2)}) %collective-permute-start.1) | collective-permute-done | bytes 16416 | tf_op jit(solution)/shard_map/ppermute | solution.py:38
  46.6 0.0 collective-permute-done.2.above_ref.above_0
  46.6 0.0 collective-permute-done.3.below_ref.below_0
  46.6 4.1 %shard_map.90 = (f32[3,512,256]{2,1,0:T(8,128)}, f32[512,256]{1,0:T(8,128)}, f32[8,128]{1,0:T(8,128)S(1)}) custom-call(f32[3,512,256]{2,1,0:T(8,128)} %bitcast.6, f32[8,512]{1,0:T(8,128)S(1)} %collective-permute-done.left_ref.left_0, f32[8,512]{1,0:T(8,128)S(1)} %collective-permute-done.1.right_ref.right_0, ...), custom_call_target="tpu_custom_call" | custom-call | flops 2000000 | bytes 1048576 | tf_op jit(solution)/shard_map/pallas_call | solution.py:759
  50.7 0.0 all-to-all-done.2.returned_ref
  50.7 3.9 %shard_map.91 = (f32[3,512,256]{2,1,0:T(8,128)}, bf16[32,24,128]{2,1,0:T(8,128)(2,1)}, f32[8,512]{1,0:T(8,128)}, f32[8,512]{1,0:T(8,128)}, f32[4,32,256]{2,1,0:T(8,128)}, /*index=5*/f32[4,32,256]{2,1,0:T(8,128)}) custom-call(s32[32,1,128]{2,1,0:T(1,128)S(1)} %all_to_all.30.asked_hbm, bf16[32,8,128]{2,1,0:T(8,128)(2,1)S(1)} %all-to-all-done.2.returned_ref, ...), custom_call_target="tpu_custom_call" | custom-call | flops 2000000 | bytes 1048576 | tf_op jit(solution)/shard_map/pallas_call | solution.py:759
  54.6 6.8 %all-to-all-start.3 = ((bf16[32,24,128]{2,1,0:T(8,128)(2,1)}), bf16[32,24,128]{2,1,0:T(8,128)(2,1)S(1)}, u32[]{:S(2)}, u32[]{:S(2)}) async-start(bf16[32,24,128]{2,1,0:T(8,128)(2,1)} %get-tuple-element.42), calls=%async_computation.3 | async-start | bytes 393216 | tf_op jit(solution)/shard_map/all_to_all | solution.py:32
  61.4 3.7 %collective-permute-start.4 = (f32[4,32,256]{2,1,0:T(8,128)}, f32[4,32,256]{2,1,0:T(8,128)S(1)}, u32[]{:S(2)}, u32[]{:S(2)}) collective-permute-start(f32[4,32,256]{2,1,0:T(8,128)} %get-tuple-element.46), channel_id=1, source_target_pairs={{0,1},{1,2},{2,3},{3,4},{4,5},{5,6},{6,7},{8,9},{9,10},{10,11},{11... | collective-permute-start | bytes 393224 | tf_op jit(solution)/shard_map/ppermute | solution.py:38
  65.1 1.3 %collective-permute-start.5 = (f32[4,32,256]{2,1,0:T(8,128)}, f32[4,32,256]{2,1,0:T(8,128)S(1)}, u32[]{:S(2)}, u32[]{:S(2)}) collective-permute-start(f32[4,32,256]{2,1,0:T(8,128)} %get-tuple-element.47), channel_id=1, source_target_pairs={{1,0},{2,1},{3,2},{4,3},{5,4},{6,5},{7,6},{9,8},{10,9},{11,10},{12... | collective-permute-start | bytes 393224 | tf_op jit(solution)/shard_map/ppermute | solution.py:38
  66.4 3.3 %all-to-all-done.3.got_ref.got_hbm = bf16[32,24,128]{2,1,0:T(8,128)(2,1)S(1)} async-done(((bf16[32,24,128]{2,1,0:T(8,128)(2,1)}), bf16[32,24,128]{2,1,0:T(8,128)(2,1)S(1)}, u32[]{:S(2)}, u32[]{:S(2)}) %all-to-all-start.3) | async-done | bytes 196640 | tf_op jit(solution)/shard_map/all_to_all | solution.py:32
  69.7 2.1 %shard_map.92 = (bf16[32,8,128]{2,1,0:T(8,128)(2,1)}, f32[8,128]{1,0:T(8,128)S(1)}, f32[8,128]{1,0:T(8,128)}) custom-call(bf16[32,24,128]{2,1,0:T(8,128)(2,1)S(1)} %all-to-all-done.3.got_ref.got_hbm, bf16[64,128,128]{2,1,0:T(8,128)(2,1)S(1)} %get-tuple-element.33.weights_ref, f32[8,32,128]{2,1,0:T(8,128)S(1)} %get-tuple-element.34.sight_ref, ...), custom_call_target="tpu_custom_call" | custom-call | flops 2000000 | bytes 1048576 | tf_op jit(solution)/shard_map/pallas_call | solution.py:759
  71.7 3.5 %all-to-all-start.4 = ((bf16[32,8,128]{2,1,0:T(8,128)(2,1)}), bf16[32,8,128]{2,1,0:T(8,128)(2,1)S(1)}, u32[]{:S(2)}, u32[]{:S(2)}) async-start(bf16[32,8,128]{2,1,0:T(8,128)(2,1)} %get-tuple-element.44), calls=%async_computation.4 | async-start | bytes 131072 | tf_op jit(solution)/shard_map/all_to_all | solution.py:32
  75.2 0.0 collective-permute-done.4.above_ref.above_1
  75.2 0.0 collective-permute-done.5.below_ref.below_1
  75.2 4.6 %shard_map.93 = (f32[3,512,256]{2,1,0:T(8,128)}, f32[3,512,256]{2,1,0:T(8,128)}, f32[8,128]{1,0:T(8,128)S(1)}) custom-call(f32[3,512,256]{2,1,0:T(8,128)} %get-tuple-element.45.w_hbm, f32[4,32,256]{2,1,0:T(8,128)S(1)} %collective-permute-done.4.above_ref.above_1, f32[4,32,256]{2,1,0:T(8,128)S(1)} %collective-permute-done.5.below_ref.below_1, ...), custom_call_target="tpu_custom_call" | custom-call | flops 2000000 | bytes 1048576 | tf_op jit(solution)/shard_map/pallas_call | solution.py:759
  79.9 0.0 copy-done.1
  79.9 0.0 copy-done.2
  79.9 2.6 %all-to-all-done.4.returned_ref = bf16[32,8,128]{2,1,0:T(8,128)(2,1)S(1)} async-done(((bf16[32,8,128]{2,1,0:T(8,128)(2,1)}), bf16[32,8,128]{2,1,0:T(8,128)(2,1)S(1)}, u32[]{:S(2)}, u32[]{:S(2)}) %all-to-all-start.4) | async-done | bytes 65568 | tf_op jit(solution)/shard_map/all_to_all | solution.py:32
  82.5 3.0 %shard_map.94 = (f32[3,512,256]{2,1,0:T(8,128)S(1)}, bf16[32,24,128]{2,1,0:T(8,128)(2,1)}, bf16[3,32,256]{2,1,0:T(8,128)(2,1)}, bf16[3,32,256]{2,1,0:T(8,128)(2,1)}) custom-call(s32[32,1,128]{2,1,0:T(1,128)S(1)} %all_to_all.30.asked_hbm, bf16[32,8,128]{2,1,0:T(8,128)(2,1)S(1)} %all-to-all-done.4.returned_ref, f32[3,512,256]{2,1,0:T(8,128)} %get-tuple-element.50.rest_hbm, ...), custom_call_target="tpu_custom_call" | custom-call | flops 2000000 | bytes 1048576 | tf_op jit(solution)/shard_map/pallas_call | solution.py:759
  85.5 3.2 %all-to-all-start.5 = ((bf16[32,24,128]{2,1,0:T(8,128)(2,1)}), bf16[32,24,128]{2,1,0:T(8,128)(2,1)S(1)}, u32[]{:S(2)}, u32[]{:S(2)}) async-start(bf16[32,24,128]{2,1,0:T(8,128)(2,1)} %get-tuple-element.54), calls=%async_computation.5 | async-start | bytes 393216 | tf_op jit(solution)/shard_map/all_to_all | solution.py:32
  88.8 3.7 %collective-permute-start.6 = (bf16[3,32,256]{2,1,0:T(8,128)(2,1)}, bf16[3,32,256]{2,1,0:T(8,128)(2,1)S(1)}, u32[]{:S(2)}, u32[]{:S(2)}) collective-permute-start(bf16[3,32,256]{2,1,0:T(8,128)(2,1)} %get-tuple-element.58), channel_id=1, source_target_pairs={{0,1},{1,2},{2,3},{3,4},{4,5},{5,6},{6,7},{8,9},{9,10},{10,11},{11... | collective-permute-start | bytes 147464 | tf_op jit(solution)/shard_map/ppermute | solution.py:38
  92.5 1.3 %collective-permute-start.7 = (bf16[3,32,256]{2,1,0:T(8,128)(2,1)}, bf16[3,32,256]{2,1,0:T(8,128)(2,1)S(1)}, u32[]{:S(2)}, u32[]{:S(2)}) collective-permute-start(bf16[3,32,256]{2,1,0:T(8,128)(2,1)} %get-tuple-element.59), channel_id=1, source_target_pairs={{1,0},{2,1},{3,2},{4,3},{5,4},{6,5},{7,6},{9,8},{10,9},{11,10},{12... | collective-permute-start | bytes 147464 | tf_op jit(solution)/shard_map/ppermute | solution.py:38
  93.8 0.8 collective-permute-done.6.above_ref
  94.6 4.1 %collective-permute-done.7.below_ref = bf16[3,32,256]{2,1,0:T(8,128)(2,1)S(1)} collective-permute-done((bf16[3,32,256]{2,1,0:T(8,128)(2,1)}, bf16[3,32,256]{2,1,0:T(8,128)(2,1)S(1)}, u32[]{:S(2)}, u32[]{:S(2)}) %collective-permute-start.7) | collective-permute-done | bytes 49184 | tf_op jit(solution)/shard_map/ppermute | solution.py:38
  98.7 0.0 all-to-all-done.5.sums_ref
  98.7 5.9 %shard_map.95 = (f32[3,512,256]{2,1,0:T(8,128)}, f32[6,512,256]{2,1,0:T(8,128)}, f32[2]{0:T(128)}) custom-call(bf16[32,24,128]{2,1,0:T(8,128)(2,1)S(1)} %all-to-all-done.5.sums_ref, f32[8,128]{1,0:T(8,128)} %get-tuple-element.55.first_cost_hbm, f32[8,128]{1,0:T(8,128)} %copy-done.2, f32[3,512,256]{2,1,0:T(8,128)} %get-tuple-element.56.wind_hbm, ...), custom_call_target="tpu_custom_call" | custom-call | flops 2000000 | bytes 1048576 | tf_op jit(solution)/shard_map/pallas_call | solution.py:759
  (2 shorter events, 0.0 us)
Async XLA Ops:
  0.6 0.7 copy-start.3
  16.3 1.4 %copy-start = (f32[3,16,32,256]{3,2,1,0:T(8,128)S(1)}, f32[3,16,32,256]{3,2,1,0:T(8,128)}, u32[]{:S(2)}) copy-start(f32[3,16,32,256]{3,2,1,0:T(8,128)} %param.6) | copy-start | bytes 4718596
  19.7 11.7 %all-to-all-start.1 = ((bf16[32,8,128]{2,1,0:T(8,128)(2,1)}), bf16[32,8,128]{2,1,0:T(8,128)(2,1)S(1)}, u32[]{:S(2)}, u32[]{:S(2)}) async-start(bf16[32,8,128]{2,1,0:T(8,128)(2,1)} %shard_map.86), calls=%async_computation.1 | async-start | bytes 131072 | tf_op jit(solution)/shard_map/all_to_all | solution.py:32
  24.8 21.8 %collective-permute-start.2 = (f32[4,32,256]{2,1,0:T(8,128)}, f32[4,32,256]{2,1,0:T(8,128)S(1)}, u32[]{:S(2)}, u32[]{:S(2)}) collective-permute-start(f32[4,32,256]{2,1,0:T(8,128)} %get-tuple-element.38), channel_id=1, source_target_pairs={{0,1},{1,2},{2,3},{3,4},{4,5},{5,6},{6,7},{8,9},{9,10},{10,11},{11... | collective-permute-start | bytes 393224 | tf_op jit(solution)/shard_map/ppermute | solution.py:38
  28.4 18.2 %collective-permute-start.3 = (f32[4,32,256]{2,1,0:T(8,128)}, f32[4,32,256]{2,1,0:T(8,128)S(1)}, u32[]{:S(2)}, u32[]{:S(2)}) collective-permute-start(f32[4,32,256]{2,1,0:T(8,128)} %get-tuple-element.39), channel_id=1, source_target_pairs={{1,0},{2,1},{3,2},{4,3},{5,4},{6,5},{7,6},{9,8},{10,9},{11,10},{12... | collective-permute-start | bytes 393224 | tf_op jit(solution)/shard_map/ppermute | solution.py:38
  31.4 8.8 %copy-start.5 = (f32[8,512]{1,0:T(8,128)S(1)}, f32[8,512]{1,0:T(8,128)}, u32[]{:S(2)}) copy-start(f32[8,512]{1,0:T(8,128)} %get-tuple-element.36) | copy-start | bytes 49156
  31.4 11.0 %copy-start.4 = (f32[8,512]{1,0:T(8,128)S(1)}, f32[8,512]{1,0:T(8,128)}, u32[]{:S(2)}) copy-start(f32[8,512]{1,0:T(8,128)} %get-tuple-element.37) | copy-start | bytes 49156
  33.4 17.4 %all-to-all-start.2 = ((bf16[32,8,128]{2,1,0:T(8,128)(2,1)}), bf16[32,8,128]{2,1,0:T(8,128)(2,1)S(1)}, u32[]{:S(2)}, u32[]{:S(2)}) async-start(bf16[32,8,128]{2,1,0:T(8,128)(2,1)} %get-tuple-element.35), calls=%async_computation.2 | async-start | bytes 131072 | tf_op jit(solution)/shard_map/all_to_all | solution.py:32
  40.2 3.5 %collective-permute-start = (f32[8,512]{1,0:T(8,128)S(1)}, f32[8,512]{1,0:T(8,128)S(1)}, u32[]{:S(2)}, u32[]{:S(2)}) collective-permute-start(f32[8,512]{1,0:T(8,128)S(1)} %copy-done.5), channel_id=1, source_target_pairs={{0,8},{8,16},{16,24},{1,9},{9,17},{17,25},{2,10},{10,18},{18,26},{... | collective-permute-start | bytes 49160 | tf_op jit(solution)/shard_map/ppermute | solution.py:38
  42.4 4.2 %collective-permute-start.1 = (f32[8,512]{1,0:T(8,128)S(1)}, f32[8,512]{1,0:T(8,128)S(1)}, u32[]{:S(2)}, u32[]{:S(2)}) collective-permute-start(f32[8,512]{1,0:T(8,128)S(1)} %copy-done.4), channel_id=1, source_target_pairs={{8,0},{16,8},{24,16},{9,1},{17,9},{25,17},{10,2},{18,10},{26,18},{... | collective-permute-start | bytes 49160 | tf_op jit(solution)/shard_map/ppermute | solution.py:38
  54.6 15.0 %all-to-all-start.3 = ((bf16[32,24,128]{2,1,0:T(8,128)(2,1)}), bf16[32,24,128]{2,1,0:T(8,128)(2,1)S(1)}, u32[]{:S(2)}, u32[]{:S(2)}) async-start(bf16[32,24,128]{2,1,0:T(8,128)(2,1)} %get-tuple-element.42), calls=%async_computation.3 | async-start | bytes 393216 | tf_op jit(solution)/shard_map/all_to_all | solution.py:32
  61.4 13.8 %collective-permute-start.4 = (f32[4,32,256]{2,1,0:T(8,128)}, f32[4,32,256]{2,1,0:T(8,128)S(1)}, u32[]{:S(2)}, u32[]{:S(2)}) collective-permute-start(f32[4,32,256]{2,1,0:T(8,128)} %get-tuple-element.46), channel_id=1, source_target_pairs={{0,1},{1,2},{2,3},{3,4},{4,5},{5,6},{6,7},{8,9},{9,10},{10,11},{11... | collective-permute-start | bytes 393224 | tf_op jit(solution)/shard_map/ppermute | solution.py:38
  65.1 10.1 %collective-permute-start.5 = (f32[4,32,256]{2,1,0:T(8,128)}, f32[4,32,256]{2,1,0:T(8,128)S(1)}, u32[]{:S(2)}, u32[]{:S(2)}) collective-permute-start(f32[4,32,256]{2,1,0:T(8,128)} %get-tuple-element.47), channel_id=1, source_target_pairs={{1,0},{2,1},{3,2},{4,3},{5,4},{6,5},{7,6},{9,8},{10,9},{11,10},{12... | collective-permute-start | bytes 393224 | tf_op jit(solution)/shard_map/ppermute | solution.py:38
  69.7 10.2 %copy-start.1 = (bf16[32,24,128]{2,1,0:T(8,128)(2,1)}, bf16[32,24,128]{2,1,0:T(8,128)(2,1)S(1)}, u32[]{:S(2)}) copy-start(bf16[32,24,128]{2,1,0:T(8,128)(2,1)S(1)} %all-to-all-done.3.got_ref.got_hbm) | copy-start | bytes 589828
  71.7 8.1 %copy-start.2 = (f32[8,128]{1,0:T(8,128)}, f32[8,128]{1,0:T(8,128)S(1)}, u32[]{:S(2)}) copy-start(f32[8,128]{1,0:T(8,128)S(1)} %get-tuple-element.49.step_ref) | copy-start | bytes 12292
  71.7 10.8 %all-to-all-start.4 = ((bf16[32,8,128]{2,1,0:T(8,128)(2,1)}), bf16[32,8,128]{2,1,0:T(8,128)(2,1)S(1)}, u32[]{:S(2)}, u32[]{:S(2)}) async-start(bf16[32,8,128]{2,1,0:T(8,128)(2,1)} %get-tuple-element.44), calls=%async_computation.4 | async-start | bytes 131072 | tf_op jit(solution)/shard_map/all_to_all | solution.py:32
  85.5 13.1 %all-to-all-start.5 = ((bf16[32,24,128]{2,1,0:T(8,128)(2,1)}), bf16[32,24,128]{2,1,0:T(8,128)(2,1)S(1)}, u32[]{:S(2)}, u32[]{:S(2)}) async-start(bf16[32,24,128]{2,1,0:T(8,128)(2,1)} %get-tuple-element.54), calls=%async_computation.5 | async-start | bytes 393216 | tf_op jit(solution)/shard_map/all_to_all | solution.py:32
  88.8 5.8 %collective-permute-start.6 = (bf16[3,32,256]{2,1,0:T(8,128)(2,1)}, bf16[3,32,256]{2,1,0:T(8,128)(2,1)S(1)}, u32[]{:S(2)}, u32[]{:S(2)}) collective-permute-start(bf16[3,32,256]{2,1,0:T(8,128)(2,1)} %get-tuple-element.58), channel_id=1, source_target_pairs={{0,1},{1,2},{2,3},{3,4},{4,5},{5,6},{6,7},{8,9},{9,10},{10,11},{11... | collective-permute-start | bytes 147464 | tf_op jit(solution)/shard_map/ppermute | solution.py:38
  92.5 6.2 %collective-permute-start.7 = (bf16[3,32,256]{2,1,0:T(8,128)(2,1)}, bf16[3,32,256]{2,1,0:T(8,128)(2,1)S(1)}, u32[]{:S(2)}, u32[]{:S(2)}) collective-permute-start(bf16[3,32,256]{2,1,0:T(8,128)(2,1)} %get-tuple-element.59), channel_id=1, source_target_pairs={{1,0},{2,1},{3,2},{4,3},{5,4},{6,5},{7,6},{9,8},{10,9},{11,10},{12... | collective-permute-start | bytes 147464 | tf_op jit(solution)/shard_map/ppermute | solution.py:38

commit v7 on v6

--- a/solution.py
+++ b/solution.py
@@ -390,7 +390,7 @@
     winds.finish()
 
 
-def for_slots(count, body, step=8):
+def for_slots(count, body, step=16):
     step = min(step, count)
 
     def run(i, carry):
@@ -471,7 +471,7 @@
         for p in range(slots):
             proj_ref[p, here, :] = seen[:, p * LANES : (p + 1) * LANES]
 
-    for_slots(sources, one, 16)
+    for_slots(sources, one, 32)
 
 
 def radial(proj_ref, sight_ref, p, sources, height):
@@ -500,7 +500,7 @@
         product = lax.dot_general(adjoint, weights, (((1,), (0,)), ((), ())), preferred_element_type=F32)
         out_ref[s] = (product + line_ref[here, :]).astype(out_ref.dtype)
 
-    for_slots(sources, one, 16)
+    for_slots(sources, one, 32)
 
 
 def first_source_kernel(slots, cells_ref, weights_ref, sight_ref, returned_out, misfit_out, proj_ref, adj_ref, line_ref):
@@ -666,12 +666,14 @@
     give_out[...] = give_ref[...].astype(BF16)
 
 
-def final_kernel(levels, slots, total_cells, total_gates, sums_ref, first_cost_hbm, step_ref, wind_hbm, gradient_ref, left_0, right_0, above_0, below_0, got_hbm, above_1, below_1, above_ref, below_ref, wind_out, strain_out, cost_out, left_rows, right_rows, wind, strain, first_cost_ref, got_ref, sems, cost_sem, got_sems):
+def final_kernel(levels, slots, total_cells, total_gates, sums_ref, first_cost_hbm, step_hbm, wind_hbm, gradient_ref, left_0, right_0, above_0, below_0, got_hbm, above_1, below_1, above_ref, below_ref, wind_out, strain_out, cost_out, left_rows, right_rows, wind, strain, first_cost_ref, step_ref, got_ref, sems, cost_sem, step_sem, got_sems):
     rows = gradient_ref.shape[1]
     cells = rows // levels
     winds = Pieces(wind_hbm, wind, sems.at[0], FINAL_PARTS).start()
     cost_copy = pltpu.make_async_copy(first_cost_hbm, first_cost_ref, cost_sem)
     cost_copy.start()
+    step_copy = pltpu.make_async_copy(step_hbm, step_ref, step_sem)
+    step_copy.start()
     got_copies = []
     for i, along_radar in enumerate((-1, 1)):
         _, place = neighbour(0, along_radar)
@@ -682,6 +684,7 @@
     squares, cost = halves(jnp.sum(jnp.sum(sums_ref[:, 0:SPLIT, :].astype(F32), axis=0), axis=0, keepdims=True))
     step = STEP_LENGTH / jnp.sqrt(squares / total_cells + EPSILON)
     cost_out[1] = (cost / total_gates)[0, 0]
+    step_copy.wait()
     first_step = step_ref[0:1, 0:1]
     lines = rows // LANES
     for copy in got_copies:
@@ -926,13 +929,15 @@
             pltpu.VMEM((3, rows, width_y), F32),
             pltpu.VMEM((6, rows, width_y), F32),
             pltpu.SMEM((8, LANES), F32),
+            pltpu.VMEM((8, LANES), F32),
             pltpu.VMEM((2, given, LANES), BF16),
             semaphores((3, FINAL_PARTS)),
+            semaphores,
             semaphores,
             semaphores((2,)),
         ),
         chip=(0, 4, 5, 6, 7, 8, 10, 11, 12, 13),
-        raw=(1, 3, 9),
+        raw=(1, 2, 3, 9),
         out_raw=(0, 1),
         out_smem=(2,),
     )

time: 105 us -> 104 us (level)
  Pallas kernels: 32.3 us -> 30.8 us
    pallas_call x11, Pallas kernels: 32.3 us -> 30.8 us  [call(): pl.pallas_call(kernel, out_shape=placed[0] if single else placed, in_spec...]
where the time goes in v7:
time: 104 us; the launch traced here: 103 us
  starting transfers between devices  41.1 us (40%)
  Pallas kernels  30.8 us (30%)
  blocking collectives  14.4 us (14%)
  waiting for transfers between devices  13.7 us (13%)
  local copies, waits for them, and re-layouts  2.07 us (2%)
    pallas_call x11, Pallas kernels, call(): pl.pallas_call(kernel, out_shape=placed[0] if single else placed, in_spec...  30.8 us
    all_to_all x5, starting transfers between devices, exchange(): return lax.all_to_all(x, AXES, split_axis=0, concat_axis=0, tiled=True)  22.9 us
    ppermute x8, starting transfers between devices, shifted(): return lax.ppermute(x, axis, pairs)  18.2 us
    all_to_all x1, blocking collectives, exchange(): return lax.all_to_all(x, AXES, split_axis=0, concat_axis=0, tiled=True)  14.4 us
    ppermute x8, waiting for transfers between devices, shifted(): return lax.ppermute(x, axis, pairs)  7.81 us
    all_to_all x5, waiting for transfers between devices, exchange(): return lax.all_to_all(x, AXES, split_axis=0, concat_axis=0, tiled=True)  5.88 us
  transfers between devices with their start and end apart: 13, of which 5 were waited for; matrix products, arithmetic and copies ran while one was open for 0% of the time, Pallas kernels for 16%

profile of v7, /device:TPU:0, one launch (start us, length us, event | category | flops | bytes accessed | tf_op | source)
XLA Modules:
  0.0 103.0 jit_solution(11680213580076938660)
XLA Ops:
  0.6 0.0 copy-start.3
  0.6 0.6 copy-done.3
  1.3 0.6 shard_map.85
  1.9 14.4 %all_to_all.30.asked_hbm = s32[32,1,128]{2,1,0:T(1,128)S(1)} all-to-all(s32[32,1,128]{2,1,0:T(1,128)} %shard_map.85), channel_id=1, replica_groups=mesh['radar'=4,'tile'=8] {'radar','tile'}, dimensions={0} | all-to-all | bytes 32768 | tf_op jit(solution)/shard_map/all_to_all | solution.py:32
  16.3 0.0 copy-start
  16.3 1.4 %copy-done = f32[3,16,32,256]{3,2,1,0:T(8,128)S(1)} copy-done((f32[3,16,32,256]{3,2,1,0:T(8,128)S(1)}, f32[3,16,32,256]{3,2,1,0:T(8,128)}, u32[]{:S(2)}) %copy-start) | copy-done | bytes 1572888
  17.7 2.0 %shard_map.86 = bf16[32,8,128]{2,1,0:T(8,128)(2,1)} custom-call(s32[32,1,128]{2,1,0:T(1,128)S(1)} %all_to_all.30.asked_hbm, f32[3,512,256]{2,1,0:T(8,128)S(1)} %bitcast.8), custom_call_target="tpu_custom_call" | custom-call | flops 2000000 | bytes 1048576 | tf_op jit(solution)/shard_map/pallas_call | solution.py:762
  19.7 2.6 %all-to-all-start.1 = ((bf16[32,8,128]{2,1,0:T(8,128)(2,1)}), bf16[32,8,128]{2,1,0:T(8,128)(2,1)S(1)}, u32[]{:S(2)}, u32[]{:S(2)}) async-start(bf16[32,8,128]{2,1,0:T(8,128)(2,1)} %shard_map.86), calls=%async_computation.1 | async-start | bytes 131072 | tf_op jit(solution)/shard_map/all_to_all | solution.py:32
  22.3 2.5 %shard_map.89 = (f32[8,512]{1,0:T(8,128)}, f32[8,512]{1,0:T(8,128)}, f32[4,32,256]{2,1,0:T(8,128)}, f32[4,32,256]{2,1,0:T(8,128)}) custom-call(f32[3,512,256]{2,1,0:T(8,128)} %bitcast.5), custom_call_target="tpu_custom_call" | custom-call | flops 2000000 | bytes 1048576 | tf_op jit(solution)/shard_map/pallas_call | solution.py:762
  24.8 3.6 %collective-permute-start.2 = (f32[4,32,256]{2,1,0:T(8,128)}, f32[4,32,256]{2,1,0:T(8,128)S(1)}, u32[]{:S(2)}, u32[]{:S(2)}) collective-permute-start(f32[4,32,256]{2,1,0:T(8,128)} %get-tuple-element.38), channel_id=1, source_target_pairs={{0,1},{1,2},{2,3},{3,4},{4,5},{5,6},{6,7},{8,9},{9,10},{10,11},{11... | collective-permute-start | bytes 393224 | tf_op jit(solution)/shard_map/ppermute | solution.py:38
  28.4 1.3 %collective-permute-start.3 = (f32[4,32,256]{2,1,0:T(8,128)}, f32[4,32,256]{2,1,0:T(8,128)S(1)}, u32[]{:S(2)}, u32[]{:S(2)}) collective-permute-start(f32[4,32,256]{2,1,0:T(8,128)} %get-tuple-element.39), channel_id=1, source_target_pairs={{1,0},{2,1},{3,2},{4,3},{5,4},{6,5},{7,6},{9,8},{10,9},{11,10},{12... | collective-permute-start | bytes 393224 | tf_op jit(solution)/shard_map/ppermute | solution.py:38
  29.7 1.7 %shard_map.87 = (bf16[64,128,128]{2,1,0:T(8,128)(2,1)S(1)}, f32[8,32,128]{2,1,0:T(8,128)S(1)}) custom-call(bf16[64,128,128]{2,1,0:T(8,128)(2,1)} %weights_hbm.1, bf16[3,64,128]{2,1,0:T(8,128)(2,1)} %bitcast.10, bf16[64,128]{1,0:T(8,128)(2,1)} %observed_hbm.1, s32[1,32]{1,0:T(1,128)} %count_hbm.1), custom_call_target="tpu_custom_call" | custom-call | flops 2000000 | bytes 1048576 | tf_op jit(solution)/shard_map/pallas_call | solution.py:762
  31.4 0.0 copy-start.5
  31.4 0.0 copy-start.4
  31.4 0.0 all-to-all-done.1.cells_ref
  31.4 1.6 %shard_map.88 = (bf16[32,8,128]{2,1,0:T(8,128)(2,1)}, f32[2,32,128]{2,1,0:T(8,128)S(1)}) custom-call(bf16[32,8,128]{2,1,0:T(8,128)(2,1)S(1)} %all-to-all-done.1.cells_ref, bf16[64,128,128]{2,1,0:T(8,128)(2,1)S(1)} %get-tuple-element.33.weights_ref, f32[8,32,128]{2,1,0:T(8,128)S(1)} %get-tuple-element.34.sight_ref), custom_call_target="tpu_custom_call" | custom-call | flops 2000000 | bytes 1048576 | tf_op jit(solution)/shard_map/pallas_call | solution.py:762
  33.0 6.8 %all-to-all-start.2 = ((bf16[32,8,128]{2,1,0:T(8,128)(2,1)}), bf16[32,8,128]{2,1,0:T(8,128)(2,1)S(1)}, u32[]{:S(2)}, u32[]{:S(2)}) async-start(bf16[32,8,128]{2,1,0:T(8,128)(2,1)} %get-tuple-element.35), calls=%async_computation.2 | async-start | bytes 131072 | tf_op jit(solution)/shard_map/all_to_all | solution.py:32
  39.8 0.0 copy-done.5
  39.8 2.2 %collective-permute-start = (f32[8,512]{1,0:T(8,128)S(1)}, f32[8,512]{1,0:T(8,128)S(1)}, u32[]{:S(2)}, u32[]{:S(2)}) collective-permute-start(f32[8,512]{1,0:T(8,128)S(1)} %copy-done.5), channel_id=1, source_target_pairs={{0,8},{8,16},{16,24},{1,9},{9,17},{17,25},{2,10},{10,18},{18,26},{... | collective-permute-start | bytes 49160 | tf_op jit(solution)/shard_map/ppermute | solution.py:38
  42.0 0.0 copy-done.4
  42.0 1.3 %collective-permute-start.1 = (f32[8,512]{1,0:T(8,128)S(1)}, f32[8,512]{1,0:T(8,128)S(1)}, u32[]{:S(2)}, u32[]{:S(2)}) collective-permute-start(f32[8,512]{1,0:T(8,128)S(1)} %copy-done.4), channel_id=1, source_target_pairs={{8,0},{16,8},{24,16},{9,1},{17,9},{25,17},{10,2},{18,10},{26,18},{... | collective-permute-start | bytes 49160 | tf_op jit(solution)/shard_map/ppermute | solution.py:38
  43.3 0.0 collective-permute-done.left_ref.left_0
  43.3 2.9 %collective-permute-done.1.right_ref.right_0 = f32[8,512]{1,0:T(8,128)S(1)} collective-permute-done((f32[8,512]{1,0:T(8,128)S(1)}, f32[8,512]{1,0:T(8,128)S(1)}, u32[]{:S(2)}, u32[]{:S(2)}) %collective-permute-start.1) | collective-permute-done | bytes 16416 | tf_op jit(solution)/shard_map/ppermute | solution.py:38
  46.2 0.0 collective-permute-done.2.above_ref.above_0
  46.2 0.0 collective-permute-done.3.below_ref.below_0
  46.2 4.1 %shard_map.90 = (f32[3,512,256]{2,1,0:T(8,128)}, f32[512,256]{1,0:T(8,128)}, f32[8,128]{1,0:T(8,128)S(1)}) custom-call(f32[3,512,256]{2,1,0:T(8,128)} %bitcast.6, f32[8,512]{1,0:T(8,128)S(1)} %collective-permute-done.left_ref.left_0, f32[8,512]{1,0:T(8,128)S(1)} %collective-permute-done.1.right_ref.right_0, ...), custom_call_target="tpu_custom_call" | custom-call | flops 2000000 | bytes 1048576 | tf_op jit(solution)/shard_map/pallas_call | solution.py:762
  50.3 0.0 all-to-all-done.2.returned_ref
  50.3 3.9 %shard_map.91 = (f32[3,512,256]{2,1,0:T(8,128)}, bf16[32,24,128]{2,1,0:T(8,128)(2,1)}, f32[8,512]{1,0:T(8,128)}, f32[8,512]{1,0:T(8,128)}, f32[4,32,256]{2,1,0:T(8,128)}, /*index=5*/f32[4,32,256]{2,1,0:T(8,128)}) custom-call(s32[32,1,128]{2,1,0:T(1,128)S(1)} %all_to_all.30.asked_hbm, bf16[32,8,128]{2,1,0:T(8,128)(2,1)S(1)} %all-to-all-done.2.returned_ref, ...), custom_call_target="tpu_custom_call" | custom-call | flops 2000000 | bytes 1048576 | tf_op jit(solution)/shard_map/pallas_call | solution.py:762
  54.2 6.8 %all-to-all-start.3 = ((bf16[32,24,128]{2,1,0:T(8,128)(2,1)}), bf16[32,24,128]{2,1,0:T(8,128)(2,1)S(1)}, u32[]{:S(2)}, u32[]{:S(2)}) async-start(bf16[32,24,128]{2,1,0:T(8,128)(2,1)} %get-tuple-element.42), calls=%async_computation.3 | async-start | bytes 393216 | tf_op jit(solution)/shard_map/all_to_all | solution.py:32
  61.0 3.7 %collective-permute-start.4 = (f32[4,32,256]{2,1,0:T(8,128)}, f32[4,32,256]{2,1,0:T(8,128)S(1)}, u32[]{:S(2)}, u32[]{:S(2)}) collective-permute-start(f32[4,32,256]{2,1,0:T(8,128)} %get-tuple-element.46), channel_id=1, source_target_pairs={{0,1},{1,2},{2,3},{3,4},{4,5},{5,6},{6,7},{8,9},{9,10},{10,11},{11... | collective-permute-start | bytes 393224 | tf_op jit(solution)/shard_map/ppermute | solution.py:38
  64.7 1.3 %collective-permute-start.5 = (f32[4,32,256]{2,1,0:T(8,128)}, f32[4,32,256]{2,1,0:T(8,128)S(1)}, u32[]{:S(2)}, u32[]{:S(2)}) collective-permute-start(f32[4,32,256]{2,1,0:T(8,128)} %get-tuple-element.47), channel_id=1, source_target_pairs={{1,0},{2,1},{3,2},{4,3},{5,4},{6,5},{7,6},{9,8},{10,9},{11,10},{12... | collective-permute-start | bytes 393224 | tf_op jit(solution)/shard_map/ppermute | solution.py:38
  66.0 3.3 %all-to-all-done.3.got_ref.got_hbm = bf16[32,24,128]{2,1,0:T(8,128)(2,1)S(1)} async-done(((bf16[32,24,128]{2,1,0:T(8,128)(2,1)}), bf16[32,24,128]{2,1,0:T(8,128)(2,1)S(1)}, u32[]{:S(2)}, u32[]{:S(2)}) %all-to-all-start.3) | async-done | bytes 196640 | tf_op jit(solution)/shard_map/all_to_all | solution.py:32
  69.3 1.6 %shard_map.92 = (bf16[32,8,128]{2,1,0:T(8,128)(2,1)}, f32[8,128]{1,0:T(8,128)S(1)}, f32[8,128]{1,0:T(8,128)}) custom-call(bf16[32,24,128]{2,1,0:T(8,128)(2,1)S(1)} %all-to-all-done.3.got_ref.got_hbm, bf16[64,128,128]{2,1,0:T(8,128)(2,1)S(1)} %get-tuple-element.33.weights_ref, f32[8,32,128]{2,1,0:T(8,128)S(1)} %get-tuple-element.34.sight_ref, ...), custom_call_target="tpu_custom_call" | custom-call | flops 2000000 | bytes 1048576 | tf_op jit(solution)/shard_map/pallas_call | solution.py:762
  70.8 3.5 %all-to-all-start.4 = ((bf16[32,8,128]{2,1,0:T(8,128)(2,1)}), bf16[32,8,128]{2,1,0:T(8,128)(2,1)S(1)}, u32[]{:S(2)}, u32[]{:S(2)}) async-start(bf16[32,8,128]{2,1,0:T(8,128)(2,1)} %get-tuple-element.44), calls=%async_computation.4 | async-start | bytes 131072 | tf_op jit(solution)/shard_map/all_to_all | solution.py:32
  74.3 0.0 collective-permute-done.4.above_ref.above_1
  74.3 0.0 collective-permute-done.5.below_ref.below_1
  74.3 4.6 %shard_map.93 = (f32[3,512,256]{2,1,0:T(8,128)}, f32[3,512,256]{2,1,0:T(8,128)}, f32[8,128]{1,0:T(8,128)S(1)}) custom-call(f32[3,512,256]{2,1,0:T(8,128)} %get-tuple-element.45.w_hbm, f32[4,32,256]{2,1,0:T(8,128)S(1)} %collective-permute-done.4.above_ref.above_1, f32[4,32,256]{2,1,0:T(8,128)S(1)} %collective-permute-done.5.below_ref.below_1, ...), custom_call_target="tpu_custom_call" | custom-call | flops 2000000 | bytes 1048576 | tf_op jit(solution)/shard_map/pallas_call | solution.py:762
  79.0 0.0 copy-done.1
  79.0 0.0 copy-done.2
  79.0 2.6 %all-to-all-done.4.returned_ref = bf16[32,8,128]{2,1,0:T(8,128)(2,1)S(1)} async-done(((bf16[32,8,128]{2,1,0:T(8,128)(2,1)}), bf16[32,8,128]{2,1,0:T(8,128)(2,1)S(1)}, u32[]{:S(2)}, u32[]{:S(2)}) %all-to-all-start.4) | async-done | bytes 65568 | tf_op jit(solution)/shard_map/all_to_all | solution.py:32
  81.6 3.0 %shard_map.94 = (f32[3,512,256]{2,1,0:T(8,128)S(1)}, bf16[32,24,128]{2,1,0:T(8,128)(2,1)}, bf16[3,32,256]{2,1,0:T(8,128)(2,1)}, bf16[3,32,256]{2,1,0:T(8,128)(2,1)}) custom-call(s32[32,1,128]{2,1,0:T(1,128)S(1)} %all_to_all.30.asked_hbm, bf16[32,8,128]{2,1,0:T(8,128)(2,1)S(1)} %all-to-all-done.4.returned_ref, f32[3,512,256]{2,1,0:T(8,128)} %get-tuple-element.50.rest_hbm, ...), custom_call_target="tpu_custom_call" | custom-call | flops 2000000 | bytes 1048576 | tf_op jit(solution)/shard_map/pallas_call | solution.py:762
  84.6 3.2 %all-to-all-start.5 = ((bf16[32,24,128]{2,1,0:T(8,128)(2,1)}), bf16[32,24,128]{2,1,0:T(8,128)(2,1)S(1)}, u32[]{:S(2)}, u32[]{:S(2)}) async-start(bf16[32,24,128]{2,1,0:T(8,128)(2,1)} %get-tuple-element.54), calls=%async_computation.5 | async-start | bytes 393216 | tf_op jit(solution)/shard_map/all_to_all | solution.py:32
  87.9 3.7 %collective-permute-start.6 = (bf16[3,32,256]{2,1,0:T(8,128)(2,1)}, bf16[3,32,256]{2,1,0:T(8,128)(2,1)S(1)}, u32[]{:S(2)}, u32[]{:S(2)}) collective-permute-start(bf16[3,32,256]{2,1,0:T(8,128)(2,1)} %get-tuple-element.58), channel_id=1, source_target_pairs={{0,1},{1,2},{2,3},{3,4},{4,5},{5,6},{6,7},{8,9},{9,10},{10,11},{11... | collective-permute-start | bytes 147464 | tf_op jit(solution)/shard_map/ppermute | solution.py:38
  91.6 1.3 %collective-permute-start.7 = (bf16[3,32,256]{2,1,0:T(8,128)(2,1)}, bf16[3,32,256]{2,1,0:T(8,128)(2,1)S(1)}, u32[]{:S(2)}, u32[]{:S(2)}) collective-permute-start(bf16[3,32,256]{2,1,0:T(8,128)(2,1)} %get-tuple-element.59), channel_id=1, source_target_pairs={{1,0},{2,1},{3,2},{4,3},{5,4},{6,5},{7,6},{9,8},{10,9},{11,10},{12... | collective-permute-start | bytes 147464 | tf_op jit(solution)/shard_map/ppermute | solution.py:38
  92.9 0.8 collective-permute-done.6.above_ref
  93.7 4.1 %collective-permute-done.7.below_ref = bf16[3,32,256]{2,1,0:T(8,128)(2,1)S(1)} collective-permute-done((bf16[3,32,256]{2,1,0:T(8,128)(2,1)}, bf16[3,32,256]{2,1,0:T(8,128)(2,1)S(1)}, u32[]{:S(2)}, u32[]{:S(2)}) %collective-permute-start.7) | collective-permute-done | bytes 49184 | tf_op jit(solution)/shard_map/ppermute | solution.py:38
  97.7 0.0 all-to-all-done.5.sums_ref
  97.8 5.2 %shard_map.95 = (f32[3,512,256]{2,1,0:T(8,128)}, f32[6,512,256]{2,1,0:T(8,128)}, f32[2]{0:T(128)}) custom-call(bf16[32,24,128]{2,1,0:T(8,128)(2,1)S(1)} %all-to-all-done.5.sums_ref, f32[8,128]{1,0:T(8,128)} %get-tuple-element.55.first_cost_hbm, f32[8,128]{1,0:T(8,128)} %copy-done.2, f32[3,512,256]{2,1,0:T(8,128)} %get-tuple-element.56.wind_hbm, ...), custom_call_target="tpu_custom_call" | custom-call | flops 2000000 | bytes 1048576 | tf_op jit(solution)/shard_map/pallas_call | solution.py:762
  (2 shorter events, 0.0 us)
Async XLA Ops:
  0.6 0.7 copy-start.3
  16.3 1.4 %copy-start = (f32[3,16,32,256]{3,2,1,0:T(8,128)S(1)}, f32[3,16,32,256]{3,2,1,0:T(8,128)}, u32[]{:S(2)}) copy-start(f32[3,16,32,256]{3,2,1,0:T(8,128)} %param.6) | copy-start | bytes 4718596
  19.7 11.7 %all-to-all-start.1 = ((bf16[32,8,128]{2,1,0:T(8,128)(2,1)}), bf16[32,8,128]{2,1,0:T(8,128)(2,1)S(1)}, u32[]{:S(2)}, u32[]{:S(2)}) async-start(bf16[32,8,128]{2,1,0:T(8,128)(2,1)} %shard_map.86), calls=%async_computation.1 | async-start | bytes 131072 | tf_op jit(solution)/shard_map/all_to_all | solution.py:32
  24.8 21.4 %collective-permute-start.2 = (f32[4,32,256]{2,1,0:T(8,128)}, f32[4,32,256]{2,1,0:T(8,128)S(1)}, u32[]{:S(2)}, u32[]{:S(2)}) collective-permute-start(f32[4,32,256]{2,1,0:T(8,128)} %get-tuple-element.38), channel_id=1, source_target_pairs={{0,1},{1,2},{2,3},{3,4},{4,5},{5,6},{6,7},{8,9},{9,10},{10,11},{11... | collective-permute-start | bytes 393224 | tf_op jit(solution)/shard_map/ppermute | solution.py:38
  28.4 17.8 %collective-permute-start.3 = (f32[4,32,256]{2,1,0:T(8,128)}, f32[4,32,256]{2,1,0:T(8,128)S(1)}, u32[]{:S(2)}, u32[]{:S(2)}) collective-permute-start(f32[4,32,256]{2,1,0:T(8,128)} %get-tuple-element.39), channel_id=1, source_target_pairs={{1,0},{2,1},{3,2},{4,3},{5,4},{6,5},{7,6},{9,8},{10,9},{11,10},{12... | collective-permute-start | bytes 393224 | tf_op jit(solution)/shard_map/ppermute | solution.py:38
  31.4 8.4 %copy-start.5 = (f32[8,512]{1,0:T(8,128)S(1)}, f32[8,512]{1,0:T(8,128)}, u32[]{:S(2)}) copy-start(f32[8,512]{1,0:T(8,128)} %get-tuple-element.36) | copy-start | bytes 49156
  31.4 10.6 %copy-start.4 = (f32[8,512]{1,0:T(8,128)S(1)}, f32[8,512]{1,0:T(8,128)}, u32[]{:S(2)}) copy-start(f32[8,512]{1,0:T(8,128)} %get-tuple-element.37) | copy-start | bytes 49156
  33.0 17.4 %all-to-all-start.2 = ((bf16[32,8,128]{2,1,0:T(8,128)(2,1)}), bf16[32,8,128]{2,1,0:T(8,128)(2,1)S(1)}, u32[]{:S(2)}, u32[]{:S(2)}) async-start(bf16[32,8,128]{2,1,0:T(8,128)(2,1)} %get-tuple-element.35), calls=%async_computation.2 | async-start | bytes 131072 | tf_op jit(solution)/shard_map/all_to_all | solution.py:32
  39.8 3.5 %collective-permute-start = (f32[8,512]{1,0:T(8,128)S(1)}, f32[8,512]{1,0:T(8,128)S(1)}, u32[]{:S(2)}, u32[]{:S(2)}) collective-permute-start(f32[8,512]{1,0:T(8,128)S(1)} %copy-done.5), channel_id=1, source_target_pairs={{0,8},{8,16},{16,24},{1,9},{9,17},{17,25},{2,10},{10,18},{18,26},{... | collective-permute-start | bytes 49160 | tf_op jit(solution)/shard_map/ppermute | solution.py:38
  42.0 4.2 %collective-permute-start.1 = (f32[8,512]{1,0:T(8,128)S(1)}, f32[8,512]{1,0:T(8,128)S(1)}, u32[]{:S(2)}, u32[]{:S(2)}) collective-permute-start(f32[8,512]{1,0:T(8,128)S(1)} %copy-done.4), channel_id=1, source_target_pairs={{8,0},{16,8},{24,16},{9,1},{17,9},{25,17},{10,2},{18,10},{26,18},{... | collective-permute-start | bytes 49160 | tf_op jit(solution)/shard_map/ppermute | solution.py:38
  54.2 15.0 %all-to-all-start.3 = ((bf16[32,24,128]{2,1,0:T(8,128)(2,1)}), bf16[32,24,128]{2,1,0:T(8,128)(2,1)S(1)}, u32[]{:S(2)}, u32[]{:S(2)}) async-start(bf16[32,24,128]{2,1,0:T(8,128)(2,1)} %get-tuple-element.42), calls=%async_computation.3 | async-start | bytes 393216 | tf_op jit(solution)/shard_map/all_to_all | solution.py:32
  61.0 13.3 %collective-permute-start.4 = (f32[4,32,256]{2,1,0:T(8,128)}, f32[4,32,256]{2,1,0:T(8,128)S(1)}, u32[]{:S(2)}, u32[]{:S(2)}) collective-permute-start(f32[4,32,256]{2,1,0:T(8,128)} %get-tuple-element.46), channel_id=1, source_target_pairs={{0,1},{1,2},{2,3},{3,4},{4,5},{5,6},{6,7},{8,9},{9,10},{10,11},{11... | collective-permute-start | bytes 393224 | tf_op jit(solution)/shard_map/ppermute | solution.py:38
  64.7 9.6 %collective-permute-start.5 = (f32[4,32,256]{2,1,0:T(8,128)}, f32[4,32,256]{2,1,0:T(8,128)S(1)}, u32[]{:S(2)}, u32[]{:S(2)}) collective-permute-start(f32[4,32,256]{2,1,0:T(8,128)} %get-tuple-element.47), channel_id=1, source_target_pairs={{1,0},{2,1},{3,2},{4,3},{5,4},{6,5},{7,6},{9,8},{10,9},{11,10},{12... | collective-permute-start | bytes 393224 | tf_op jit(solution)/shard_map/ppermute | solution.py:38
  69.3 9.7 %copy-start.1 = (bf16[32,24,128]{2,1,0:T(8,128)(2,1)}, bf16[32,24,128]{2,1,0:T(8,128)(2,1)S(1)}, u32[]{:S(2)}) copy-start(bf16[32,24,128]{2,1,0:T(8,128)(2,1)S(1)} %all-to-all-done.3.got_ref.got_hbm) | copy-start | bytes 589828
  70.8 8.1 %copy-start.2 = (f32[8,128]{1,0:T(8,128)}, f32[8,128]{1,0:T(8,128)S(1)}, u32[]{:S(2)}) copy-start(f32[8,128]{1,0:T(8,128)S(1)} %get-tuple-element.49.step_ref.step_hbm) | copy-start | bytes 12292
  70.8 10.8 %all-to-all-start.4 = ((bf16[32,8,128]{2,1,0:T(8,128)(2,1)}), bf16[32,8,128]{2,1,0:T(8,128)(2,1)S(1)}, u32[]{:S(2)}, u32[]{:S(2)}) async-start(bf16[32,8,128]{2,1,0:T(8,128)(2,1)} %get-tuple-element.44), calls=%async_computation.4 | async-start | bytes 131072 | tf_op jit(solution)/shard_map/all_to_all | solution.py:32
  84.6 13.1 %all-to-all-start.5 = ((bf16[32,24,128]{2,1,0:T(8,128)(2,1)}), bf16[32,24,128]{2,1,0:T(8,128)(2,1)S(1)}, u32[]{:S(2)}, u32[]{:S(2)}) async-start(bf16[32,24,128]{2,1,0:T(8,128)(2,1)} %get-tuple-element.54), calls=%async_computation.5 | async-start | bytes 393216 | tf_op jit(solution)/shard_map/all_to_all | solution.py:32
  87.9 5.8 %collective-permute-start.6 = (bf16[3,32,256]{2,1,0:T(8,128)(2,1)}, bf16[3,32,256]{2,1,0:T(8,128)(2,1)S(1)}, u32[]{:S(2)}, u32[]{:S(2)}) collective-permute-start(bf16[3,32,256]{2,1,0:T(8,128)(2,1)} %get-tuple-element.58), channel_id=1, source_target_pairs={{0,1},{1,2},{2,3},{3,4},{4,5},{5,6},{6,7},{8,9},{9,10},{10,11},{11... | collective-permute-start | bytes 147464 | tf_op jit(solution)/shard_map/ppermute | solution.py:38
  91.6 6.2 %collective-permute-start.7 = (bf16[3,32,256]{2,1,0:T(8,128)(2,1)}, bf16[3,32,256]{2,1,0:T(8,128)(2,1)S(1)}, u32[]{:S(2)}, u32[]{:S(2)}) collective-permute-start(bf16[3,32,256]{2,1,0:T(8,128)(2,1)} %get-tuple-element.59), channel_id=1, source_target_pairs={{1,0},{2,1},{3,2},{4,3},{5,4},{6,5},{7,6},{9,8},{10,9},{11,10},{12... | collective-permute-start | bytes 147464 | tf_op jit(solution)/shard_map/ppermute | solution.py:38
